TPU v7x, 256 devices: a whole 4x4x8 slice. The times are simulated.
256 devices in a mesh: seq: 128 (over y, x_hi, z, core), head: 2 (over x_lo).
Axes of the slice: x: 4 (x_hi: 2, x_lo: 2; x = x_hi * 2 + x_lo), y: 4, z: 8, core: 2. Of those that a mesh axis runs over, the one named last changes fastest.
Arguments:
- query: bfloat16 [32768, 2048], P('seq', 'head'), may hold values from -4.5 to 4.5
- key_value: bfloat16 [32768, 512], P('seq'), may hold values from -4.5 to 4.5
- out_grad: bfloat16 [32768, 2048], P('seq', 'head'), may hold values from -48 to 48
- inputs_normed: bfloat16 [32768, 4096], P('seq'), may hold values from -24 to 24
- kv_weight: bfloat16 [2, 4096, 256], P(None, 'head'), may hold values from -0.09375 to 0.09375
- segment_ids: int32 [32768], replicated, may hold values from 0 to 7, never falling along the last dimension, each value on 1 to 8192 neighbouring positions
Outputs:
- query_grad: bfloat16 [32768, 2048], P('seq', 'head')
- input_grad: bfloat16 [32768, 4096], P('seq', 'head')
- weight_grad: float32 [2, 4096, 256], P('head', 'seq')
All inputs are finite; a program needn't handle non-finite values.
Results may differ from a plain program's by a relative error of at most 0.015.
Values may be sent and summed in bfloat16 or wider, within the bound.
No kernel may reach another device: no remote copies, remote signals or barrier semaphores. Data moves between devices by JAX's collectives and lax.ppermute only.
A program may use at most 64 MiB of HBM per device.

v0:
```python
import math

import jax
import jax.numpy as jnp
from jax import lax
from jax.experimental import pallas as pl
from jax.experimental.pallas import tpu as pltpu
from jax.sharding import Mesh
from jax.sharding import PartitionSpec as P

WIN = 2048
SEQ = ("y", "xh", "z", "c")
ALL = ("y", "xh", "z", "c", "l")
PAIRS = 64
LINE = 8
BF = jnp.bfloat16
F32 = jnp.float32


def moved(value, steps, flip):
    routes = []
    for source in range(PAIRS):
        target = source + steps
        if not 0 <= target < PAIRS:
            continue
        turn = int(flip and source // LINE != target // LINE)
        for core in range(2):
            for side in range(2):
                routes.append(((source * 2 + core) * 2 + side, (target * 2 + core) * 2 + (side ^ turn)))
    return lax.ppermute(value, ALL, routes)


def swapped(value, axis):
    return lax.ppermute(value, axis, [(0, 1), (1, 0)])


def turned(value, axis, steps):
    count = lax.axis_size(axis)
    return lax.ppermute(value, axis, [(i, (i + steps) % count) for i in range(count)])


def columns(value, which, width):
    return lax.dynamic_slice_in_dim(value, which * width, width, 1)


def attention_kernel(
    side_ref,
    low_ref,
    query_ref,
    out_ref,
    own_ref,
    m1,
    m2,
    m3,
    m4,
    o1,
    o2,
    o3,
    o4,
    near_ref,
    far_ref,
    query_grad_ref,
    given_ref,
    kept_ref,
    keys,
    values,
    queries,
    outs,
    probs,
    dprobs,
    tops,
    turned_grad,
):
    blocks, tok, hd = keys.shape
    heads = query_ref.shape[1] // hd
    inv_root = 1.0 / math.sqrt(hd)
    to_two = inv_root * math.log2(math.e)
    last = blocks - 1
    mine = {1: m1, 2: m2, 3: m3, 4: m4}
    other = {1: o1, 2: o2, 3: o3, 4: o4}
    for h in range(heads):
        queries[h * tok : (h + 1) * tok, :] = query_ref[:, h * hd : (h + 1) * hd]
        outs[h * tok : (h + 1) * tok, :] = out_ref[:, h * hd : (h + 1) * hd]

    @pl.when(side_ref[0] == 0)
    def _():
        for d in mine:
            keys[last - 2 * d] = mine[d][...]
            values[last - 2 * d] = other[d][...]

    @pl.when(side_ref[0] != 0)
    def _():
        for d in mine:
            keys[last - 2 * d] = other[d][...]
            values[last - 2 * d] = mine[d][...]

    keys[last] = own_ref[:, :hd]
    values[last] = own_ref[:, hd:]
    for place, ref, at in ((1, far_ref, 0), (3, far_ref, 1), (5, near_ref, 0), (7, near_ref, 1)):
        keys[place] = ref[at * tok : (at + 1) * tok, :hd]
        values[place] = ref[at * tok : (at + 1) * tok, hd:]

    along = (((1,), (1,)), ((), ()))
    down = (((0,), (0,)), ((), ()))
    low = low_ref[...]
    wide = heads * tok

    def first(block, carry, diagonal):
        top, mass, delta = carry
        row = lax.broadcasted_iota(jnp.int32, (tok, wide), 0)
        ok = row + block * tok >= low
        if diagonal:
            column = lax.broadcasted_iota(jnp.int32, (tok, wide), 1)
            ok = ok & (row <= (column & (tok - 1)))
        scores = lax.dot_general(keys[block], queries[...], along, preferred_element_type=F32)
        dprob = lax.dot_general(values[block], outs[...], along, preferred_element_type=F32)
        scores = jnp.where(ok, scores, -jnp.inf)
        here = jnp.max(scores, axis=0, keepdims=True)
        if not diagonal:
            here = jnp.maximum(here, top)
        prob = jnp.exp2((scores - here) * to_two)
        new_mass = jnp.sum(prob, axis=0, keepdims=True)
        new_delta = jnp.sum(prob * dprob, axis=0, keepdims=True)
        if not diagonal:
            fade = jnp.exp2((top - here) * to_two)
            new_mass = new_mass + mass * fade
            new_delta = new_delta + delta * fade
        probs[block] = prob
        dprobs[block] = dprob
        tops[block] = here
        return here, new_mass, new_delta

    carry = first(last, (None, None, None), True)
    carry = lax.fori_loop(0, last, lambda i, carry: first(i, carry, False), carry)
    top, mass, delta = carry
    inverse = 1.0 / mass
    delta = delta * inverse
    turned_grad[...] = jnp.zeros_like(turned_grad)

    def second(block, ref, at):
        factor = jnp.exp2((tops[block] - top) * to_two) * inverse
        prob = probs[block] * factor
        dscore = (prob * (dprobs[block] - delta)).astype(BF)
        key_grad = jnp.dot(dscore, queries[...], preferred_element_type=F32) * inv_root
        value_grad = jnp.dot(prob.astype(BF), outs[...], preferred_element_type=F32)
        ref[at, :, :hd] = key_grad.astype(BF)
        ref[at, :, hd:] = value_grad.astype(BF)
        turned_grad[...] += lax.dot_general(keys[block], dscore, down, preferred_element_type=F32)

    def odd(i, _):
        second(2 * i + 1, given_ref, i)
        return 0

    def even(i, _):
        second(2 * i, kept_ref, i)
        return 0

    lax.fori_loop(0, blocks // 2, odd, 0)
    lax.fori_loop(0, blocks // 2 + 1, even, 0)
    for h in range(heads):
        part = turned_grad[:, h * tok : (h + 1) * tok] * inv_root
        query_grad_ref[:, h * hd : (h + 1) * hd] = part.T.astype(BF)


def attention(side, low, query, out_grad, own, mine, other, near, far):
    tok, width = query.shape
    hd = own.shape[1] // 2
    heads = width // hd
    wide = heads * tok
    vmem = pl.BlockSpec(memory_space=pltpu.VMEM)
    work = 2 * 5 * wide * 9 * tok * hd
    return pl.pallas_call(
        attention_kernel,
        out_shape=(
            jax.ShapeDtypeStruct((tok, width), BF),
            jax.ShapeDtypeStruct((4, tok, 2 * hd), BF),
            jax.ShapeDtypeStruct((5, tok, 2 * hd), BF),
        ),
        in_specs=[pl.BlockSpec(memory_space=pltpu.SMEM)] + [vmem] * 14,
        out_specs=(vmem, vmem, vmem),
        scratch_shapes=[
            pltpu.VMEM((9, tok, hd), BF),
            pltpu.VMEM((9, tok, hd), BF),
            pltpu.VMEM((wide, hd), BF),
            pltpu.VMEM((wide, hd), BF),
            pltpu.VMEM((9, tok, wide), F32),
            pltpu.VMEM((9, tok, wide), F32),
            pltpu.VMEM((9, 1, wide), F32),
            pltpu.VMEM((hd, wide), F32),
        ],
        compiler_params=pltpu.CompilerParams(vmem_limit_bytes=48 * 1024 * 1024),
        cost_estimate=pl.CostEstimate(
            flops=work, transcendentals=wide * 9 * tok, bytes_accessed=8 * 1024 * 1024
        ),
        name="attention",
    )(side, low, query, out_grad, own, *mine, *other, near, far)


def merge_kernel(one_ref, two_ref, sum_ref):
    sum_ref[...] = (one_ref[...] + two_ref[...].astype(F32)).astype(sum_ref.dtype)


def merged(one, two):
    vmem = pl.BlockSpec(memory_space=pltpu.VMEM)
    return pl.pallas_call(
        merge_kernel,
        out_shape=jax.ShapeDtypeStruct(one.shape, BF),
        in_specs=[vmem, vmem],
        out_specs=vmem,
        compiler_params=pltpu.CompilerParams(vmem_limit_bytes=4 * 1024 * 1024),
        cost_estimate=pl.CostEstimate(flops=one.size, transcendentals=0, bytes_accessed=one.size * 8),
        name="merge",
    )(one, two)


def local(query, key_value, out_grad, inputs_normed, kv_weight, segment_ids):
    tok = query.shape[0]
    hd = key_value.shape[1] // 2
    heads = query.shape[1] // hd
    y, _, z, c, l = (lax.axis_index(axis) for axis in ALL)
    seq_index = lax.axis_index(SEQ)

    def taken(distance):
        turn = (z + distance >= LINE).astype(jnp.int32)
        return columns(key_value, l ^ turn, hd)

    mine, other = {}, {}
    for d in (4, 1, 2, 3):
        mine[d] = moved(taken(d), d, True)
    for d in (1, 2, 3, 4):
        other[d] = swapped(mine[d], "l")
    blocks = {0: key_value}
    for d in (1, 2, 3, 4):
        blocks[d] = jnp.where(
            l == 0,
            jnp.concatenate([mine[d], other[d]], axis=1),
            jnp.concatenate([other[d], mine[d]], axis=1),
        )

    def crossing(low, high):
        return jnp.where(
            c == 0,
            jnp.concatenate([blocks[low + 1], blocks[low]], axis=0),
            jnp.concatenate([blocks[high + 1], blocks[high]], axis=0),
        )

    near = swapped(crossing(0, 1), "c")
    far = swapped(crossing(2, 3), "c")
    width = inputs_normed.shape[1] // 4
    x_parts = [columns(inputs_normed, y, width)]
    for k in (1, 2, 3):
        x_parts.append(turned(columns(inputs_normed, (y + k) % 4, width), "y", k))

    begin = seq_index * tok
    padded = jnp.concatenate([jnp.full((WIN,), -1, jnp.int32), segment_ids], axis=0)
    key_seg = lax.dynamic_slice_in_dim(padded, begin, WIN + tok, 0)
    query_seg = lax.dynamic_slice_in_dim(segment_ids, begin, tok, 0)
    before = jnp.sum((key_seg[:, None] < query_seg[None, :]).astype(jnp.int32), axis=0)
    low = jnp.maximum(before, 1 + jnp.arange(tok, dtype=jnp.int32))
    low = jnp.tile(low, heads)[None, :]
    query_grad, given, kept = attention(
        l.reshape(1).astype(jnp.int32),
        low,
        query,
        out_grad,
        key_value,
        [mine[d] for d in (1, 2, 3, 4)],
        [other[d] for d in (1, 2, 3, 4)],
        near,
        far,
    )
    arrived = swapped(given.reshape(4 * tok, 2 * hd), "c")
    arrived, x_parts = lax.optimization_barrier((arrived, x_parts))
    x_rows = jnp.concatenate(x_parts, axis=0)

    def core_sum(d, which):
        def piece(j):
            if not 0 <= j < 4:
                return jnp.zeros((tok, hd), F32)
            rows = arrived[(3 - j) * tok : (4 - j) * tok]
            return columns(rows, which, hd).astype(F32)

        return columns(kept[4 - d], which, hd).astype(F32) + jnp.where(c == 0, piece(d), piece(d - 1))

    back = {}
    sums = {}
    for d in (4, 3, 2, 1, 0):
        side = l ^ (z < d).astype(jnp.int32)
        got = swapped(core_sum(d, 1 - side).astype(BF), "l")
        sums[d] = (core_sum(d, side), got)
    for d in (3, 4, 2, 1):
        total = merged(*sums[d])
        back[d] = moved(total, -d, True).astype(F32)
    own = (sums[0][0] + sums[0][1].astype(F32) + back[1] + back[2] + back[3] + back[4]).astype(BF)

    partner = swapped(own, "l")
    spread_rows = []
    for k in (1, 2, 3):
        spread_rows.append(turned(own, "y", k))
    partner, spread_rows = lax.optimization_barrier((partner, spread_rows))
    both = jnp.concatenate([own, partner], axis=1)
    first = lax.dynamic_index_in_dim(kv_weight, l, 0, keepdims=False)
    second = lax.dynamic_index_in_dim(kv_weight, 1 - l, 0, keepdims=False)
    input_grad = lax.dot_general(
        both,
        jnp.concatenate([first, second], axis=1),
        (((1,), (1,)), ((), ())),
        preferred_element_type=F32,
    ).astype(BF)

    rows = jnp.concatenate([own] + spread_rows, axis=0)
    norm = 1.0 / math.sqrt(tok * lax.axis_size(SEQ))
    weight_part = lax.dot_general(
        x_rows, rows, (((0,), (0,)), ((), ())), preferred_element_type=F32
    )
    weight_part = (weight_part * norm).reshape(16, 2, width // 32, hd)
    kept = lax.dynamic_index_in_dim(weight_part, c, 1, keepdims=False)
    given = lax.dynamic_index_in_dim(weight_part, 1 - c, 1, keepdims=False)
    total = (kept + swapped(given.astype(BF), "c").astype(F32)).astype(BF)
    spread = lax.all_to_all(total, ("xh", "z"), split_axis=0, concat_axis=0, tiled=True)
    weight_grad = spread.astype(F32).sum(axis=0)
    return (query_grad, input_grad, weight_grad[None])


def solution(mesh):
    finer = Mesh(mesh.devices.reshape(4, 2, 8, 2, 2), ALL)
    placed = (
        P(SEQ, "l"),
        P(SEQ, None),
        P(SEQ, "l"),
        P(SEQ, None),
        P(None, "l", None),
        P(),
    )
    return jax.shard_map(
        local,
        mesh=finer,
        in_specs=placed,
        out_specs=(P(SEQ, "l"), P(SEQ, "l"), P("l", SEQ, None)),
        check_vma=False,
    )
```

profile of v0, /device:TPU:32, one launch (start us, length us, event | category | flops | bytes accessed | tf_op | source)
XLA Modules:
  0.0 159.6 jit_solution(7863532024928081708)
XLA Ops:
  2.0 3.8 %collective-permute-start = (bf16[256,256]{1,0:T(8,128)(2,1)S(1)}, bf16[256,256]{1,0:T(8,128)(2,1)S(1)}, u32[]{:S(2)}, u32[]{:S(2)}) collective-permute-start(bf16[256,256]{1,0:T(8,128)(2,1)S(1)} %get-tuple-element.62), channel_id=1, source_target_pairs={{0,4},{1,5},{2,6},{3,7},{4,8},{5,9},{6,10},{7,11},{8,12},{9,13},{1... | collective-permute-start | bytes 393224 | tf_op jit(solution)/shard_map/ppermute | solution.py:30
  5.8 6.3 %collective-permute-start.1 = (bf16[256,256]{1,0:T(8,128)(2,1)S(1)}, bf16[256,256]{1,0:T(8,128)(2,1)S(1)}, u32[]{:S(2)}, u32[]{:S(2)}) collective-permute-start(bf16[256,256]{1,0:T(8,128)(2,1)S(1)} %get-tuple-element.61), channel_id=1, source_target_pairs={{0,8},{1,9},{2,10},{3,11},{4,12},{5,13},{6,14},{7,15},{8,16},{9,17... | collective-permute-start | bytes 393224 | tf_op jit(solution)/shard_map/ppermute | solution.py:30
  12.1 3.9 %collective-permute-start.2 = (bf16[256,256]{1,0:T(8,128)(2,1)S(1)}, bf16[256,256]{1,0:T(8,128)(2,1)S(1)}, u32[]{:S(2)}, u32[]{:S(2)}) collective-permute-start(bf16[256,256]{1,0:T(8,128)(2,1)S(1)} %get-tuple-element.60), channel_id=1, source_target_pairs={{0,12},{1,13},{2,14},{3,15},{4,16},{5,17},{6,18},{7,19},{8,20},{9,... | collective-permute-start | bytes 393224 | tf_op jit(solution)/shard_map/ppermute | solution.py:30
  16.0 5.5 %collective-permute-start.3 = (bf16[256,256]{1,0:T(8,128)(2,1)S(1)}, bf16[256,256]{1,0:T(8,128)(2,1)S(1)}, u32[]{:S(2)}, u32[]{:S(2)}) collective-permute-start(bf16[256,256]{1,0:T(8,128)(2,1)S(1)} %get-tuple-element.59), channel_id=1, source_target_pairs={{0,16},{1,17},{2,18},{3,19},{4,20},{5,21},{6,22},{7,23},{8,24},{9,... | collective-permute-start | bytes 393224 | tf_op jit(solution)/shard_map/ppermute | solution.py:30
  21.9 1.7 %collective-permute-start.5 = (bf16[256,256]{1,0:T(8,128)(2,1)S(1)}, bf16[256,256]{1,0:T(8,128)(2,1)S(1)}, u32[]{:S(2)}, u32[]{:S(2)}) collective-permute-start(bf16[256,256]{1,0:T(8,128)(2,1)S(1)} %collective-permute-done.1.m2), channel_id=1, source_target_pairs={{0,1},{1,0},{2,3},{3,2},{4,5},{5,4},{6,7},{7,6},{8,9},{9,8},{10,11... | collective-permute-start | bytes 393224 | tf_op jit(solution)/shard_map/ppermute | solution.py:34
  25.5 1.7 %collective-permute-start.7 = (bf16[256,256]{1,0:T(8,128)(2,1)S(1)}, bf16[256,256]{1,0:T(8,128)(2,1)S(1)}, u32[]{:S(2)}, u32[]{:S(2)}) collective-permute-start(bf16[256,256]{1,0:T(8,128)(2,1)S(1)} %collective-permute-done.3.m4), channel_id=1, source_target_pairs={{0,1},{1,0},{2,3},{3,2},{4,5},{5,4},{6,7},{7,6},{8,9},{9,8},{10,11... | collective-permute-start | bytes 393224 | tf_op jit(solution)/shard_map/ppermute | solution.py:34
  28.1 2.7 %collective-permute-done.5.o2 = bf16[256,256]{1,0:T(8,128)(2,1)S(1)} collective-permute-done((bf16[256,256]{1,0:T(8,128)(2,1)S(1)}, bf16[256,256]{1,0:T(8,128)(2,1)S(1)}, u32[]{:S(2)}, u32[]{:S(2)}) %collective-permute-start.5) | collective-permute-done | bytes 131104 | tf_op jit(solution)/shard_map/ppermute | solution.py:34
  30.9 1.8 %collective-permute-done.6.o3 = bf16[256,256]{1,0:T(8,128)(2,1)S(1)} collective-permute-done((bf16[256,256]{1,0:T(8,128)(2,1)S(1)}, bf16[256,256]{1,0:T(8,128)(2,1)S(1)}, u32[]{:S(2)}, u32[]{:S(2)}) %collective-permute-start.6) | collective-permute-done | bytes 131104 | tf_op jit(solution)/shard_map/ppermute | solution.py:34
  37.5 11.6 %attention.1 = (bf16[256,1024]{1,0:T(8,128)(2,1)}, bf16[4,256,512]{2,1,0:T(8,128)(2,1)S(1)}, bf16[5,256,512]{2,1,0:T(8,128)(2,1)S(1)}) custom-call(s32[1]{0:T(128)} %bitcast.side_ref, s32[1,1024]{1,0:T(1,128)S(1)} %bitcast.48, bf16[256,1024]{1,0:T(8,128)(2,1)S(1)} %copy-done.1, bf16[256,1024]{1,0:T(8,128)(2,1)S(1)} %copy-done.2, ...), custom_call_target="tpu_custom_call" | custom-call | flops 6039797760 | bytes 8388608 | tf_op jit(solution)/shard_map/attention/pallas_call | solution.py:172
  49.2 2.7 %constant_dynamic-slice_fusion = (bf16[256,1024]{1,0:T(8,128)(2,1)S(1)}, bf16[256,1024]{1,0:T(8,128)(2,1)}, bf16[256,1024]{1,0:T(8,128)(2,1)}, bf16[256,1024]{1,0:T(8,128)(2,1)}) fusion(bf16[256,4096]{1,0:T(8,128)(2,1)} %param.9, s32[]{:T(128)S(6)} %select_n.203, s32[]{:T(128)S(6)} %select_n.199, s32[]{:T(128)S(6)} %select_n.197, s32[]{:T(128)S(6)} %select_n.201), kind=kLoop, calls=%fused_computation.59 | loop fusion | bytes 4194320 | tf_op jit(solution)/shard_map/dynamic_slice | solution.py:43
  51.9 6.6 %collective-permute-start.11 = (bf16[256,1024]{1,0:T(8,128)(2,1)}, bf16[256,1024]{1,0:T(8,128)(2,1)}, u32[]{:S(2)}, u32[]{:S(2)}) collective-permute-start(bf16[256,1024]{1,0:T(8,128)(2,1)} %get-tuple-element.28), channel_id=1, source_target_pairs={{0,64},{64,128},{128,192},{192,0},{1,65},{65,129},{129,193},{193,1... | collective-permute-start | bytes 1572872 | tf_op jit(solution)/shard_map/ppermute | solution.py:39
  58.5 3.3 %collective-permute-start.12 = (bf16[256,1024]{1,0:T(8,128)(2,1)}, bf16[256,1024]{1,0:T(8,128)(2,1)}, u32[]{:S(2)}, u32[]{:S(2)}) collective-permute-start(bf16[256,1024]{1,0:T(8,128)(2,1)} %get-tuple-element.30), channel_id=1, source_target_pairs={{0,128},{64,192},{128,0},{192,64},{1,129},{65,193},{129,1},{193,65... | collective-permute-start | bytes 1572872 | tf_op jit(solution)/shard_map/ppermute | solution.py:39
  62.8 10.3 %collective-permute-done.11 = bf16[256,1024]{1,0:T(8,128)(2,1)} collective-permute-done((bf16[256,1024]{1,0:T(8,128)(2,1)}, bf16[256,1024]{1,0:T(8,128)(2,1)}, u32[]{:S(2)}, u32[]{:S(2)}) %collective-permute-start.11) | collective-permute-done | bytes 524320 | tf_op jit(solution)/shard_map/ppermute | solution.py:39
  73.1 12.4 %collective-permute-done.12 = bf16[256,1024]{1,0:T(8,128)(2,1)} collective-permute-done((bf16[256,1024]{1,0:T(8,128)(2,1)}, bf16[256,1024]{1,0:T(8,128)(2,1)}, u32[]{:S(2)}, u32[]{:S(2)}) %collective-permute-start.12) | collective-permute-done | bytes 524320 | tf_op jit(solution)/shard_map/ppermute | solution.py:39
  88.0 1.4 collective-permute-start.17
  90.0 1.4 collective-permute-start.21
  92.1 1.7 %collective-permute-done.15.two_ref = bf16[256,256]{1,0:T(8,128)(2,1)S(1)} collective-permute-done((bf16[256,256]{1,0:T(8,128)(2,1)S(1)}, bf16[256,256]{1,0:T(8,128)(2,1)S(1)}, u32[]{:S(2)}, u32[]{:S(2)}) %collective-permute-start.15) | collective-permute-done | bytes 131104 | tf_op jit(solution)/shard_map/ppermute | solution.py:34
  93.8 3.1 %collective-permute-start.16 = (bf16[256,256]{1,0:T(8,128)(2,1)S(1)}, bf16[256,256]{1,0:T(8,128)(2,1)S(1)}, u32[]{:S(2)}, u32[]{:S(2)}) collective-permute-start(bf16[256,256]{1,0:T(8,128)(2,1)S(1)} %merge.4), channel_id=1, source_target_pairs={{4,0},{5,1},{6,2},{7,3},{8,4},{9,5},{10,6},{11,7},{12,8},{13,9},{1... | collective-permute-start | bytes 393224 | tf_op jit(solution)/shard_map/ppermute | solution.py:30
  99.4 1.3 collective-permute-start.20
  100.7 1.4 collective-permute-done.21.two_ref
  104.2 6.5 %collective-permute-done.18 = bf16[256,256]{1,0:T(8,128)(2,1)S(1)} collective-permute-done((bf16[256,256]{1,0:T(8,128)(2,1)S(1)}, bf16[256,256]{1,0:T(8,128)(2,1)S(1)}, u32[]{:S(2)}, u32[]{:S(2)}) %collective-permute-start.18) | collective-permute-done | bytes 131104 | tf_op jit(solution)/shard_map/ppermute | solution.py:30
  110.6 2.4 %collective-permute-done.20 = bf16[256,256]{1,0:T(8,128)(2,1)S(1)} collective-permute-done((bf16[256,256]{1,0:T(8,128)(2,1)S(1)}, bf16[256,256]{1,0:T(8,128)(2,1)S(1)}, u32[]{:S(2)}, u32[]{:S(2)}) %collective-permute-start.20) | collective-permute-done | bytes 131104 | tf_op jit(solution)/shard_map/ppermute | solution.py:30
  113.0 9.9 %collective-permute-done.22 = bf16[256,256]{1,0:T(8,128)(2,1)S(1)} collective-permute-done((bf16[256,256]{1,0:T(8,128)(2,1)S(1)}, bf16[256,256]{1,0:T(8,128)(2,1)S(1)}, u32[]{:S(2)}, u32[]{:S(2)}) %collective-permute-start.22) | collective-permute-done | bytes 131104 | tf_op jit(solution)/shard_map/ppermute | solution.py:30
  124.9 3.1 %collective-permute-start.25 = (bf16[256,256]{1,0:T(8,128)(2,1)S(1)}, bf16[256,256]{1,0:T(8,128)(2,1)S(1)}, u32[]{:S(2)}, u32[]{:S(2)}) collective-permute-start(bf16[256,256]{1,0:T(8,128)(2,1)S(1)} %fusion.36), channel_id=1, source_target_pairs={{0,128},{64,192},{128,0},{192,64},{1,129},{65,193},{129,1},{193,65... | collective-permute-start | bytes 393224 | tf_op jit(solution)/shard_map/ppermute | solution.py:39
  128.4 2.8 %collective-permute-done.24 = bf16[256,256]{1,0:T(8,128)(2,1)S(1)} collective-permute-done((bf16[256,256]{1,0:T(8,128)(2,1)S(1)}, bf16[256,256]{1,0:T(8,128)(2,1)S(1)}, u32[]{:S(2)}, u32[]{:S(2)}) %collective-permute-start.24) | collective-permute-done | bytes 131104 | tf_op jit(solution)/shard_map/ppermute | solution.py:39
  131.3 1.7 %collective-permute-done.25 = bf16[256,256]{1,0:T(8,128)(2,1)S(1)} collective-permute-done((bf16[256,256]{1,0:T(8,128)(2,1)S(1)}, bf16[256,256]{1,0:T(8,128)(2,1)S(1)}, u32[]{:S(2)}, u32[]{:S(2)}) %collective-permute-start.25) | collective-permute-done | bytes 131104 | tf_op jit(solution)/shard_map/ppermute | solution.py:39
  133.0 2.1 %fusion.11 = f32[1024,256]{1,0:T(8,128)S(1)} fusion(bf16[256,1024]{1,0:T(8,128)(2,1)} %collective-permute-done.13, bf16[256,1024]{1,0:T(8,128)(2,1)} %collective-permute-done.12, bf16[256,1024]{1,0:T(8,128)(2,1)} %collective-permute-done.11, bf16[256,1024]{1,0:T(8,128)(2,1)S(1)} %copy-done.4, bf16[256,256]{1,0:T(8,128)(2,1)S(1)} %collective-permute-done.26, ...), kind=kOutput, calls=%fused_computation.13 | convolution fusion | flops 547618816 | bytes 3670016 | tf_op jit(solution)/shard_map/dot_general | solution.py:313
  135.2 1.7 %collective-permute-done.27 = bf16[16,32,256]{2,1,0:T(8,128)(2,1)} collective-permute-done((bf16[16,32,256]{2,1,0:T(8,128)(2,1)S(1)}, bf16[16,32,256]{2,1,0:T(8,128)(2,1)}, u32[]{:S(2)}, u32[]{:S(2)}) %collective-permute-start.27) | collective-permute-done | bytes 262176 | tf_op jit(solution)/shard_map/ppermute | solution.py:34
  136.9 1.7 %fusion.21 = bf16[16,32,256]{2,1,0:T(8,128)(2,1)} fusion(bf16[16,32,256]{2,1,0:T(8,128)(2,1)} %collective-permute-done.27, f32[16,2,32,256]{3,2,1,0:T(8,128)S(1)} %bitcast.51, s32[]{:T(128)S(6)} %select_n.225), kind=kLoop, calls=%fused_computation.26 | loop fusion | flops 393216 | bytes 1048580 | tf_op jit(solution)/shard_map/convert_element_type | solution.py:319
  138.6 8.5 %all-to-all-start = ((bf16[16,32,256]{2,1,0:T(8,128)(2,1)}), bf16[16,32,256]{2,1,0:T(8,128)(2,1)S(1)}, u32[]{:S(2)}, u32[]{:S(2)}) async-start(bf16[16,32,256]{2,1,0:T(8,128)(2,1)} %fusion.21), calls=%async_computation | async-start | bytes 524288 | tf_op jit(solution)/shard_map/all_to_all | solution.py:320
  148.0 1.7 %convolution_convert_fusion = bf16[256,2048]{1,0:T(8,128)(2,1)} fusion(bf16[2048,256]{1,0:T(8,128)(2,1)S(1)} %get-tuple-element.32, bf16[2048,256]{1,0:T(8,128)(2,1)S(1)} %get-tuple-element.31, bf16[256,256]{1,0:T(8,128)(2,1)S(1)} %copy-done.6, bf16[256,256]{1,0:T(8,128)(2,1)S(1)} %fusion.36), kind=kOutput, calls=%fused_computation | convolution fusion | flops 542113792 | bytes 3407872 | tf_op jit(solution)/shard_map/dot_general | solution.py:304
  149.7 9.2 %all-to-all-done = bf16[16,32,256]{2,1,0:T(8,128)(2,1)S(1)} async-done(((bf16[16,32,256]{2,1,0:T(8,128)(2,1)}), bf16[16,32,256]{2,1,0:T(8,128)(2,1)S(1)}, u32[]{:S(2)}, u32[]{:S(2)}) %all-to-all-start) | async-done | bytes 262176 | tf_op jit(solution)/shard_map/all_to_all | solution.py:320
  (68 shorter events, 22.9 us)
Async XLA Ops:
  0.6 33.7 %copy-start = (bf16[256,512]{1,0:T(8,128)(2,1)S(1)}, bf16[256,512]{1,0:T(8,128)(2,1)}, u32[]{:S(2)}) copy-start(bf16[256,512]{1,0:T(8,128)(2,1)} %own_ref.1) | copy-start | bytes 786436
  2.0 19.6 %collective-permute-start = (bf16[256,256]{1,0:T(8,128)(2,1)S(1)}, bf16[256,256]{1,0:T(8,128)(2,1)S(1)}, u32[]{:S(2)}, u32[]{:S(2)}) collective-permute-start(bf16[256,256]{1,0:T(8,128)(2,1)S(1)} %get-tuple-element.62), channel_id=1, source_target_pairs={{0,4},{1,5},{2,6},{3,7},{4,8},{5,9},{6,10},{7,11},{8,12},{9,13},{1... | collective-permute-start | bytes 393224 | tf_op jit(solution)/shard_map/ppermute | solution.py:30
  5.8 16.1 %collective-permute-start.1 = (bf16[256,256]{1,0:T(8,128)(2,1)S(1)}, bf16[256,256]{1,0:T(8,128)(2,1)S(1)}, u32[]{:S(2)}, u32[]{:S(2)}) collective-permute-start(bf16[256,256]{1,0:T(8,128)(2,1)S(1)} %get-tuple-element.61), channel_id=1, source_target_pairs={{0,8},{1,9},{2,10},{3,11},{4,12},{5,13},{6,14},{7,15},{8,16},{9,17... | collective-permute-start | bytes 393224 | tf_op jit(solution)/shard_map/ppermute | solution.py:30
  12.1 13.1 %collective-permute-start.2 = (bf16[256,256]{1,0:T(8,128)(2,1)S(1)}, bf16[256,256]{1,0:T(8,128)(2,1)S(1)}, u32[]{:S(2)}, u32[]{:S(2)}) collective-permute-start(bf16[256,256]{1,0:T(8,128)(2,1)S(1)} %get-tuple-element.60), channel_id=1, source_target_pairs={{0,12},{1,13},{2,14},{3,15},{4,16},{5,17},{6,18},{7,19},{8,20},{9,... | collective-permute-start | bytes 393224 | tf_op jit(solution)/shard_map/ppermute | solution.py:30
  16.0 9.5 %collective-permute-start.3 = (bf16[256,256]{1,0:T(8,128)(2,1)S(1)}, bf16[256,256]{1,0:T(8,128)(2,1)S(1)}, u32[]{:S(2)}, u32[]{:S(2)}) collective-permute-start(bf16[256,256]{1,0:T(8,128)(2,1)S(1)} %get-tuple-element.59), channel_id=1, source_target_pairs={{0,16},{1,17},{2,18},{3,19},{4,20},{5,21},{6,22},{7,23},{8,24},{9,... | collective-permute-start | bytes 393224 | tf_op jit(solution)/shard_map/ppermute | solution.py:30
  21.5 6.5 %collective-permute-start.4 = (bf16[256,256]{1,0:T(8,128)(2,1)S(1)}, bf16[256,256]{1,0:T(8,128)(2,1)S(1)}, u32[]{:S(2)}, u32[]{:S(2)}) collective-permute-start(bf16[256,256]{1,0:T(8,128)(2,1)S(1)} %collective-permute-done.m1), channel_id=1, source_target_pairs={{0,1},{1,0},{2,3},{3,2},{4,5},{5,4},{6,7},{7,6},{8,9},{9,8},{10,11... | collective-permute-start | bytes 393224 | tf_op jit(solution)/shard_map/ppermute | solution.py:34
  21.9 8.9 %collective-permute-start.5 = (bf16[256,256]{1,0:T(8,128)(2,1)S(1)}, bf16[256,256]{1,0:T(8,128)(2,1)S(1)}, u32[]{:S(2)}, u32[]{:S(2)}) collective-permute-start(bf16[256,256]{1,0:T(8,128)(2,1)S(1)} %collective-permute-done.1.m2), channel_id=1, source_target_pairs={{0,1},{1,0},{2,3},{3,2},{4,5},{5,4},{6,7},{7,6},{8,9},{9,8},{10,11... | collective-permute-start | bytes 393224 | tf_op jit(solution)/shard_map/ppermute | solution.py:34
  25.2 7.6 %collective-permute-start.6 = (bf16[256,256]{1,0:T(8,128)(2,1)S(1)}, bf16[256,256]{1,0:T(8,128)(2,1)S(1)}, u32[]{:S(2)}, u32[]{:S(2)}) collective-permute-start(bf16[256,256]{1,0:T(8,128)(2,1)S(1)} %collective-permute-done.2.m3), channel_id=1, source_target_pairs={{0,1},{1,0},{2,3},{3,2},{4,5},{5,4},{6,7},{7,6},{8,9},{9,8},{10,11... | collective-permute-start | bytes 393224 | tf_op jit(solution)/shard_map/ppermute | solution.py:34
  25.5 8.7 %collective-permute-start.7 = (bf16[256,256]{1,0:T(8,128)(2,1)S(1)}, bf16[256,256]{1,0:T(8,128)(2,1)S(1)}, u32[]{:S(2)}, u32[]{:S(2)}) collective-permute-start(bf16[256,256]{1,0:T(8,128)(2,1)S(1)} %collective-permute-done.3.m4), channel_id=1, source_target_pairs={{0,1},{1,0},{2,3},{3,2},{4,5},{5,4},{6,7},{7,6},{8,9},{9,8},{10,11... | collective-permute-start | bytes 393224 | tf_op jit(solution)/shard_map/ppermute | solution.py:34
  34.7 2.0 %collective-permute-start.8 = (bf16[512,512]{1,0:T(8,128)(2,1)S(1)}, bf16[512,512]{1,0:T(8,128)(2,1)S(1)}, u32[]{:S(2)}, u32[]{:S(2)}) collective-permute-start(bf16[512,512]{1,0:T(8,128)(2,1)S(1)} %get-tuple-element.58), channel_id=1, source_target_pairs={{0,2},{2,0},{1,3},{3,1},{4,6},{6,4},{5,7},{7,5},{8,10},{10,8},{9,1... | collective-permute-start | bytes 1572872 | tf_op jit(solution)/shard_map/ppermute | solution.py:34
  34.8 2.6 %collective-permute-start.9 = (bf16[512,512]{1,0:T(8,128)(2,1)S(1)}, bf16[512,512]{1,0:T(8,128)(2,1)S(1)}, u32[]{:S(2)}, u32[]{:S(2)}) collective-permute-start(bf16[512,512]{1,0:T(8,128)(2,1)S(1)} %get-tuple-element.57), channel_id=1, source_target_pairs={{0,2},{2,0},{1,3},{3,1},{4,6},{6,4},{5,7},{7,5},{8,10},{10,8},{9,1... | collective-permute-start | bytes 1572872 | tf_op jit(solution)/shard_map/ppermute | solution.py:34
  49.1 36.5 %collective-permute-start.10 = (bf16[1024,512]{1,0:T(8,128)(2,1)S(1)}, bf16[1024,512]{1,0:T(8,128)(2,1)}, u32[]{:S(2)}, u32[]{:S(2)}) collective-permute-start(bf16[1024,512]{1,0:T(8,128)(2,1)S(1)} %bitcast.49), channel_id=1, source_target_pairs={{0,2},{2,0},{1,3},{3,1},{4,6},{6,4},{5,7},{7,5},{8,10},{10,8},{9,1... | collective-permute-start | bytes 3145736 | tf_op jit(solution)/shard_map/ppermute | solution.py:34
  51.9 21.2 %collective-permute-start.11 = (bf16[256,1024]{1,0:T(8,128)(2,1)}, bf16[256,1024]{1,0:T(8,128)(2,1)}, u32[]{:S(2)}, u32[]{:S(2)}) collective-permute-start(bf16[256,1024]{1,0:T(8,128)(2,1)} %get-tuple-element.28), channel_id=1, source_target_pairs={{0,64},{64,128},{128,192},{192,0},{1,65},{65,129},{129,193},{193,1... | collective-permute-start | bytes 1572872 | tf_op jit(solution)/shard_map/ppermute | solution.py:39
  58.5 27.1 %collective-permute-start.12 = (bf16[256,1024]{1,0:T(8,128)(2,1)}, bf16[256,1024]{1,0:T(8,128)(2,1)}, u32[]{:S(2)}, u32[]{:S(2)}) collective-permute-start(bf16[256,1024]{1,0:T(8,128)(2,1)} %get-tuple-element.30), channel_id=1, source_target_pairs={{0,128},{64,192},{128,0},{192,64},{1,129},{65,193},{129,1},{193,65... | collective-permute-start | bytes 1572872 | tf_op jit(solution)/shard_map/ppermute | solution.py:39
  61.8 23.7 %collective-permute-start.13 = (bf16[256,1024]{1,0:T(8,128)(2,1)S(1)}, bf16[256,1024]{1,0:T(8,128)(2,1)}, u32[]{:S(2)}, u32[]{:S(2)}) collective-permute-start(bf16[256,1024]{1,0:T(8,128)(2,1)S(1)} %get-tuple-element.27), channel_id=1, source_target_pairs={{0,192},{64,0},{128,64},{192,128},{1,193},{65,1},{129,65},{193,129... | collective-permute-start | bytes 1572872 | tf_op jit(solution)/shard_map/ppermute | solution.py:39
  87.3 45.7 %copy-start.4 = (bf16[256,1024]{1,0:T(8,128)(2,1)S(1)}, bf16[256,1024]{1,0:T(8,128)(2,1)}, u32[]{:S(2)}) copy-start(bf16[256,1024]{1,0:T(8,128)(2,1)} %get-tuple-element.20) | copy-start | bytes 1572868
  87.3 6.5 %collective-permute-start.15 = (bf16[256,256]{1,0:T(8,128)(2,1)S(1)}, bf16[256,256]{1,0:T(8,128)(2,1)S(1)}, u32[]{:S(2)}, u32[]{:S(2)}) collective-permute-start(bf16[256,256]{1,0:T(8,128)(2,1)S(1)} %get-tuple-element.42), channel_id=1, source_target_pairs={{0,1},{1,0},{2,3},{3,2},{4,5},{5,4},{6,7},{7,6},{8,9},{9,8},{10,11... | collective-permute-start | bytes 393224 | tf_op jit(solution)/shard_map/ppermute | solution.py:34
  88.0 8.9 %collective-permute-start.17 = (bf16[256,256]{1,0:T(8,128)(2,1)S(1)}, bf16[256,256]{1,0:T(8,128)(2,1)S(1)}, u32[]{:S(2)}, u32[]{:S(2)}) collective-permute-start(bf16[256,256]{1,0:T(8,128)(2,1)S(1)} %get-tuple-element.52), channel_id=1, source_target_pairs={{0,1},{1,0},{2,3},{3,2},{4,5},{5,4},{6,7},{7,6},{8,9},{9,8},{10,11... | collective-permute-start | bytes 393224 | tf_op jit(solution)/shard_map/ppermute | solution.py:34
  89.4 10.0 %collective-permute-start.19 = (bf16[256,256]{1,0:T(8,128)(2,1)S(1)}, bf16[256,256]{1,0:T(8,128)(2,1)S(1)}, u32[]{:S(2)}, u32[]{:S(2)}) collective-permute-start(bf16[256,256]{1,0:T(8,128)(2,1)S(1)} %get-tuple-element.54), channel_id=1, source_target_pairs={{0,1},{1,0},{2,3},{3,2},{4,5},{5,4},{6,7},{7,6},{8,9},{9,8},{10,11... | collective-permute-start | bytes 393224 | tf_op jit(solution)/shard_map/ppermute | solution.py:34
  90.0 12.1 %collective-permute-start.21 = (bf16[256,256]{1,0:T(8,128)(2,1)S(1)}, bf16[256,256]{1,0:T(8,128)(2,1)S(1)}, u32[]{:S(2)}, u32[]{:S(2)}) collective-permute-start(bf16[256,256]{1,0:T(8,128)(2,1)S(1)} %get-tuple-element.56), channel_id=1, source_target_pairs={{0,1},{1,0},{2,3},{3,2},{4,5},{5,4},{6,7},{7,6},{8,9},{9,8},{10,11... | collective-permute-start | bytes 393224 | tf_op jit(solution)/shard_map/ppermute | solution.py:34
  91.4 12.1 %collective-permute-start.14 = (bf16[256,256]{1,0:T(8,128)(2,1)S(1)}, bf16[256,256]{1,0:T(8,128)(2,1)S(1)}, u32[]{:S(2)}, u32[]{:S(2)}) collective-permute-start(bf16[256,256]{1,0:T(8,128)(2,1)S(1)} %get-tuple-element.50), channel_id=1, source_target_pairs={{0,1},{1,0},{2,3},{3,2},{4,5},{5,4},{6,7},{7,6},{8,9},{9,8},{10,11... | collective-permute-start | bytes 393224 | tf_op jit(solution)/shard_map/ppermute | solution.py:34
  93.8 10.4 %collective-permute-start.16 = (bf16[256,256]{1,0:T(8,128)(2,1)S(1)}, bf16[256,256]{1,0:T(8,128)(2,1)S(1)}, u32[]{:S(2)}, u32[]{:S(2)}) collective-permute-start(bf16[256,256]{1,0:T(8,128)(2,1)S(1)} %merge.4), channel_id=1, source_target_pairs={{4,0},{5,1},{6,2},{7,3},{8,4},{9,5},{10,6},{11,7},{12,8},{13,9},{1... | collective-permute-start | bytes 393224 | tf_op jit(solution)/shard_map/ppermute | solution.py:30
  96.9 13.7 %collective-permute-start.18 = (bf16[256,256]{1,0:T(8,128)(2,1)S(1)}, bf16[256,256]{1,0:T(8,128)(2,1)S(1)}, u32[]{:S(2)}, u32[]{:S(2)}) collective-permute-start(bf16[256,256]{1,0:T(8,128)(2,1)S(1)} %merge.5), channel_id=1, source_target_pairs={{8,0},{9,1},{10,2},{11,3},{12,4},{13,5},{14,6},{15,7},{16,8},{17,9... | collective-permute-start | bytes 393224 | tf_op jit(solution)/shard_map/ppermute | solution.py:30
  99.4 13.6 %collective-permute-start.20 = (bf16[256,256]{1,0:T(8,128)(2,1)S(1)}, bf16[256,256]{1,0:T(8,128)(2,1)S(1)}, u32[]{:S(2)}, u32[]{:S(2)}) collective-permute-start(bf16[256,256]{1,0:T(8,128)(2,1)S(1)} %merge.6), channel_id=1, source_target_pairs={{12,0},{13,1},{14,2},{15,3},{16,4},{17,5},{18,6},{19,7},{20,8},{21... | collective-permute-start | bytes 393224 | tf_op jit(solution)/shard_map/ppermute | solution.py:30
  102.1 20.8 %collective-permute-start.22 = (bf16[256,256]{1,0:T(8,128)(2,1)S(1)}, bf16[256,256]{1,0:T(8,128)(2,1)S(1)}, u32[]{:S(2)}, u32[]{:S(2)}) collective-permute-start(bf16[256,256]{1,0:T(8,128)(2,1)S(1)} %merge.7), channel_id=1, source_target_pairs={{16,0},{17,1},{18,2},{19,3},{20,4},{21,5},{22,6},{23,7},{24,8},{25... | collective-permute-start | bytes 393224 | tf_op jit(solution)/shard_map/ppermute | solution.py:30
  123.0 5.4 %collective-permute-start.23 = (bf16[256,256]{1,0:T(8,128)(2,1)S(1)}, bf16[256,256]{1,0:T(8,128)(2,1)S(1)}, u32[]{:S(2)}, u32[]{:S(2)}) collective-permute-start(bf16[256,256]{1,0:T(8,128)(2,1)S(1)} %fusion.36), channel_id=1, source_target_pairs={{0,1},{1,0},{2,3},{3,2},{4,5},{5,4},{6,7},{7,6},{8,9},{9,8},{10,11... | collective-permute-start | bytes 393224 | tf_op jit(solution)/shard_map/ppermute | solution.py:34
  123.7 7.6 %collective-permute-start.24 = (bf16[256,256]{1,0:T(8,128)(2,1)S(1)}, bf16[256,256]{1,0:T(8,128)(2,1)S(1)}, u32[]{:S(2)}, u32[]{:S(2)}) collective-permute-start(bf16[256,256]{1,0:T(8,128)(2,1)S(1)} %fusion.36), channel_id=1, source_target_pairs={{0,64},{64,128},{128,192},{192,0},{1,65},{65,129},{129,193},{193,1... | collective-permute-start | bytes 393224 | tf_op jit(solution)/shard_map/ppermute | solution.py:39
  124.9 8.0 %collective-permute-start.25 = (bf16[256,256]{1,0:T(8,128)(2,1)S(1)}, bf16[256,256]{1,0:T(8,128)(2,1)S(1)}, u32[]{:S(2)}, u32[]{:S(2)}) collective-permute-start(bf16[256,256]{1,0:T(8,128)(2,1)S(1)} %fusion.36), channel_id=1, source_target_pairs={{0,128},{64,192},{128,0},{192,64},{1,129},{65,193},{129,1},{193,65... | collective-permute-start | bytes 393224 | tf_op jit(solution)/shard_map/ppermute | solution.py:39
  128.0 5.0 %collective-permute-start.26 = (bf16[256,256]{1,0:T(8,128)(2,1)S(1)}, bf16[256,256]{1,0:T(8,128)(2,1)S(1)}, u32[]{:S(2)}, u32[]{:S(2)}) collective-permute-start(bf16[256,256]{1,0:T(8,128)(2,1)S(1)} %fusion.36), channel_id=1, source_target_pairs={{0,192},{64,0},{128,64},{192,128},{1,193},{65,1},{129,65},{193,129... | collective-permute-start | bytes 393224 | tf_op jit(solution)/shard_map/ppermute | solution.py:39
  135.1 12.0 %copy-start.3 = (bf16[2,2048,256]{2,1,0:T(8,128)(2,1)S(1)}, bf16[2,2048,256]{2,1,0:T(8,128)(2,1)}, u32[]{:S(2)}) copy-start(bf16[2,2048,256]{2,1,0:T(8,128)(2,1)} %param.10) | copy-start | bytes 6291460
  135.1 1.8 %collective-permute-start.27 = (bf16[16,32,256]{2,1,0:T(8,128)(2,1)S(1)}, bf16[16,32,256]{2,1,0:T(8,128)(2,1)}, u32[]{:S(2)}, u32[]{:S(2)}) collective-permute-start(bf16[16,32,256]{2,1,0:T(8,128)(2,1)S(1)} %fusion.22), channel_id=1, source_target_pairs={{0,2},{2,0},{1,3},{3,1},{4,6},{6,4},{5,7},{7,5},{8,10},{10,8},{9,1... | collective-permute-start | bytes 786440 | tf_op jit(solution)/shard_map/ppermute | solution.py:34
  138.6 20.4 %all-to-all-start = ((bf16[16,32,256]{2,1,0:T(8,128)(2,1)}), bf16[16,32,256]{2,1,0:T(8,128)(2,1)S(1)}, u32[]{:S(2)}, u32[]{:S(2)}) async-start(bf16[16,32,256]{2,1,0:T(8,128)(2,1)} %fusion.21), calls=%async_computation | async-start | bytes 524288 | tf_op jit(solution)/shard_map/all_to_all | solution.py:320
  (4 other events, 24.1 us)
where the time goes:
time: 161 us; the launch traced here: 160 us
  waiting for transfers between devices  69.4 us (43%)
  starting transfers between devices  61 us (38%)
  Pallas kernels  11.7 us (7%)
  local copies, waits for them, and re-layouts  7.85 us (5%)
  other arithmetic  4.9 us (3%)
  matrix products  3.81 us (2%)
    ppermute x6, waiting for transfers between devices, turned(): lax.ppermute(value, axis, [(i, (i + steps) % count) for i in range(count)])  27.2 us
    ppermute x8, starting transfers between devices, moved(): return lax.ppermute(value, ALL, routes)  26.5 us
    ppermute x8, waiting for transfers between devices, moved(): return lax.ppermute(value, ALL, routes)  19.4 us
    ppermute x6, starting transfers between devices, turned(): lax.ppermute(value, axis, [(i, (i + steps) % count) for i in range(count)])  15.5 us
    ppermute x14, waiting for transfers between devices, swapped(): return lax.ppermute(value, axis, [(0, 1), (1, 0)])  13.5 us
    pallas_call x1, Pallas kernels, attention(): pl.pallas_call(attention_kernel, out_shape=(jax.ShapeDtypeStruct((tok, wi...  11.6 us
    ppermute x14, starting transfers between devices, swapped(): return lax.ppermute(value, axis, [(0, 1), (1, 0)])  10.4 us
    all_to_all x1, waiting for transfers between devices, local(): lax.all_to_all(total, ('xh', 'z'), split_axis=0, concat_axis=0, tiled=True)  9.24 us
  transfers between devices with their start and end apart: 29, of which 21 were waited for; matrix products, arithmetic and copies ran while one was open for 5% of the time, Pallas kernels for 0%

commit v1 on v0

--- a/solution.py
+++ b/solution.py
@@ -49,14 +49,12 @@
     query_ref,
     out_ref,
     own_ref,
-    m1,
-    m2,
-    m3,
-    m4,
-    o1,
-    o2,
-    o3,
-    o4,
+    mine1,
+    mine4,
+    mine23,
+    other1,
+    other4,
+    other23,
     near_ref,
     far_ref,
     query_grad_ref,
@@ -76,8 +74,8 @@
     inv_root = 1.0 / math.sqrt(hd)
     to_two = inv_root * math.log2(math.e)
     last = blocks - 1
-    mine = {1: m1, 2: m2, 3: m3, 4: m4}
-    other = {1: o1, 2: o2, 3: o3, 4: o4}
+    mine = {1: mine1, 4: mine4, 2: mine23.at[:tok], 3: mine23.at[tok:]}
+    other = {1: other1, 4: other4, 2: other23.at[:tok], 3: other23.at[tok:]}
     for h in range(heads):
         queries[h * tok : (h + 1) * tok, :] = query_ref[:, h * hd : (h + 1) * hd]
         outs[h * tok : (h + 1) * tok, :] = out_ref[:, h * hd : (h + 1) * hd]
@@ -176,7 +174,7 @@
             jax.ShapeDtypeStruct((4, tok, 2 * hd), BF),
             jax.ShapeDtypeStruct((5, tok, 2 * hd), BF),
         ),
-        in_specs=[pl.BlockSpec(memory_space=pltpu.SMEM)] + [vmem] * 14,
+        in_specs=[pl.BlockSpec(memory_space=pltpu.SMEM)] + [vmem] * 12,
         out_specs=(vmem, vmem, vmem),
         scratch_shapes=[
             pltpu.VMEM((9, tok, hd), BF),
@@ -196,21 +194,26 @@
     )(side, low, query, out_grad, own, *mine, *other, near, far)
 
 
-def merge_kernel(one_ref, two_ref, sum_ref):
-    sum_ref[...] = (one_ref[...] + two_ref[...].astype(F32)).astype(sum_ref.dtype)
-
-
-def merged(one, two):
+def merge_kernel(*refs):
+    parts, sum_ref = refs[:-1], refs[-1]
+    total = parts[0][...].astype(F32)
+    for part in parts[1:]:
+        total = total + part[...].astype(F32)
+    sum_ref[...] = total.astype(sum_ref.dtype)
+
+
+def merged(*parts):
     vmem = pl.BlockSpec(memory_space=pltpu.VMEM)
+    size = parts[0].size
     return pl.pallas_call(
         merge_kernel,
-        out_shape=jax.ShapeDtypeStruct(one.shape, BF),
-        in_specs=[vmem, vmem],
+        out_shape=jax.ShapeDtypeStruct(parts[0].shape, BF),
+        in_specs=[vmem] * len(parts),
         out_specs=vmem,
         compiler_params=pltpu.CompilerParams(vmem_limit_bytes=4 * 1024 * 1024),
-        cost_estimate=pl.CostEstimate(flops=one.size, transcendentals=0, bytes_accessed=one.size * 8),
+        cost_estimate=pl.CostEstimate(flops=size, transcendentals=0, bytes_accessed=size * 8),
         name="merge",
-    )(one, two)
+    )(*parts)
 
 
 def local(query, key_value, out_grad, inputs_normed, kv_weight, segment_ids):
@@ -224,11 +227,14 @@
         turn = (z + distance >= LINE).astype(jnp.int32)
         return columns(key_value, l ^ turn, hd)
 
-    mine, other = {}, {}
-    for d in (4, 1, 2, 3):
-        mine[d] = moved(taken(d), d, True)
-    for d in (1, 2, 3, 4):
-        other[d] = swapped(mine[d], "l")
+    mine1 = moved(taken(1), 1, True)
+    mine4 = moved(taken(4), 4, True)
+    mine23 = moved(jnp.concatenate([columns(key_value, l, hd), mine1], axis=0), 2, False)
+    other1 = swapped(mine1, "l")
+    other4 = swapped(mine4, "l")
+    other23 = swapped(mine23, "l")
+    mine = {1: mine1, 4: mine4, 2: mine23[:tok], 3: mine23[tok:]}
+    other = {1: other1, 4: other4, 2: other23[:tok], 3: other23[tok:]}
     blocks = {0: key_value}
     for d in (1, 2, 3, 4):
         blocks[d] = jnp.where(
@@ -264,8 +270,8 @@
         query,
         out_grad,
         key_value,
-        [mine[d] for d in (1, 2, 3, 4)],
-        [other[d] for d in (1, 2, 3, 4)],
+        (mine1, mine4, mine23),
+        (other1, other4, other23),
         near,
         far,
     )
@@ -282,16 +288,28 @@
 
         return columns(kept[4 - d], which, hd).astype(F32) + jnp.where(c == 0, piece(d), piece(d - 1))
 
-    back = {}
-    sums = {}
-    for d in (4, 3, 2, 1, 0):
-        side = l ^ (z < d).astype(jnp.int32)
-        got = swapped(core_sum(d, 1 - side).astype(BF), "l")
-        sums[d] = (core_sum(d, side), got)
-    for d in (3, 4, 2, 1):
-        total = merged(*sums[d])
-        back[d] = moved(total, -d, True).astype(F32)
-    own = (sums[0][0] + sums[0][1].astype(F32) + back[1] + back[2] + back[3] + back[4]).astype(BF)
+    sides = {
+        4: l ^ (z < 4).astype(jnp.int32),
+        3: l ^ ((z + LINE - 2) % LINE < 1).astype(jnp.int32),
+        2: l,
+        1: l ^ (z < 1).astype(jnp.int32),
+        0: l,
+    }
+
+    def paired(*distances):
+        keep = jnp.concatenate([core_sum(d, sides[d]) for d in distances], axis=0)
+        give = jnp.concatenate([core_sum(d, 1 - sides[d]).astype(BF) for d in distances], axis=0)
+        return keep, swapped(give, "l")
+
+    two_three = merged(*paired(2, 3))
+    four = merged(*paired(4))
+    one = paired(1)
+    none = paired(0)
+    back23 = moved(two_three, -2, False)
+    back4 = moved(four, -4, True)
+    one = merged(*one, back23[tok:])
+    back1 = moved(one, -1, True)
+    own = sum(part.astype(F32) for part in (*none, back23[:tok], back1, back4)).astype(BF)
 
     partner = swapped(own, "l")
     spread_rows = []

time: 161 us -> 161 us (level)
  starting transfers between devices: 61 us -> 62.8 us
    ppermute x14 -> x12, waiting for transfers between devices: 13.5 us -> 19.8 us  [swapped(): return lax.ppermute(value, axis, [(0, 1), (1, 0)])]
    ppermute x8 -> x6, waiting for transfers between devices: 19.4 us -> 13.8 us  [moved(): return lax.ppermute(value, ALL, routes)]
    ppermute x6, waiting for transfers between devices: 27.2 us -> 25.6 us  [turned(): lax.ppermute(value, axis, [(i, (i + steps) % count) for i in range(count)])]
    ppermute x8 -> x6, starting transfers between devices: 26.5 us -> 25 us  [moved(): return lax.ppermute(value, ALL, routes)]
    ppermute x14 -> x12, starting transfers between devices: 10.4 us -> 11.4 us  [swapped(): return lax.ppermute(value, axis, [(0, 1), (1, 0)])]
  transfers between devices with their start and end apart: 29 -> 25, of which waited for: 21 -> 17; matrix products, arithmetic and copies ran while one was open for 5% -> 5% of each run, Pallas kernels for 0% -> 0%
where the time goes in v1:
time: 161 us; the launch traced here: 160 us
  waiting for transfers between devices  68.5 us (43%)
  starting transfers between devices  62.8 us (39%)
  Pallas kernels  11.7 us (7%)
  local copies, waits for them, and re-layouts  6.88 us (4%)
  other arithmetic  4.86 us (3%)
  matrix products  3.81 us (2%)
    ppermute x6, waiting for transfers between devices, turned(): lax.ppermute(value, axis, [(i, (i + steps) % count) for i in range(count)])  25.6 us
    ppermute x6, starting transfers between devices, moved(): return lax.ppermute(value, ALL, routes)  25 us
    ppermute x12, waiting for transfers between devices, swapped(): return lax.ppermute(value, axis, [(0, 1), (1, 0)])  19.8 us
    ppermute x6, starting transfers between devices, turned(): lax.ppermute(value, axis, [(i, (i + steps) % count) for i in range(count)])  16.4 us
    ppermute x6, waiting for transfers between devices, moved(): return lax.ppermute(value, ALL, routes)  13.8 us
    pallas_call x1, Pallas kernels, attention(): pl.pallas_call(attention_kernel, out_shape=(jax.ShapeDtypeStruct((tok, wi...  11.6 us
    ppermute x12, starting transfers between devices, swapped(): return lax.ppermute(value, axis, [(0, 1), (1, 0)])  11.4 us
    all_to_all x1, starting transfers between devices, local(): lax.all_to_all(total, ('xh', 'z'), split_axis=0, concat_axis=0, tiled=True)  10.1 us
  transfers between devices with their start and end apart: 25, of which 17 were waited for; matrix products, arithmetic and copies ran while one was open for 5% of the time, Pallas kernels for 0%

profile of v1, /device:TPU:32, one launch (start us, length us, event | category | flops | bytes accessed | tf_op | source)
XLA Modules:
  0.0 159.5 jit_solution(8086003758316980656)
XLA Ops:
  1.9 4.0 %collective-permute-start = (bf16[256,256]{1,0:T(8,128)(2,1)S(1)}, bf16[256,256]{1,0:T(8,128)(2,1)S(1)}, u32[]{:S(2)}, u32[]{:S(2)}) collective-permute-start(bf16[256,256]{1,0:T(8,128)(2,1)S(1)} %get-tuple-element.65), channel_id=1, source_target_pairs={{0,4},{1,5},{2,6},{3,7},{4,8},{5,9},{6,10},{7,11},{8,12},{9,13},{1... | collective-permute-start | bytes 393224 | tf_op jit(solution)/shard_map/ppermute | solution.py:30
  5.9 7.1 %collective-permute-start.1 = (bf16[256,256]{1,0:T(8,128)(2,1)S(1)}, bf16[256,256]{1,0:T(8,128)(2,1)S(1)}, u32[]{:S(2)}, u32[]{:S(2)}) collective-permute-start(bf16[256,256]{1,0:T(8,128)(2,1)S(1)} %get-tuple-element.64), channel_id=1, source_target_pairs={{0,16},{1,17},{2,18},{3,19},{4,20},{5,21},{6,22},{7,23},{8,24},{9,... | collective-permute-start | bytes 393224 | tf_op jit(solution)/shard_map/ppermute | solution.py:30
  13.1 2.4 %collective-permute-start.2 = (bf16[512,256]{1,0:T(8,128)(2,1)S(1)}, bf16[512,256]{1,0:T(8,128)(2,1)S(1)}, u32[]{:S(2)}, u32[]{:S(2)}) collective-permute-start(bf16[512,256]{1,0:T(8,128)(2,1)S(1)} %pad_maximum_fusion.1), channel_id=1, source_target_pairs={{0,8},{1,9},{2,10},{3,11},{4,12},{5,13},{6,14},{7,15},{8,16},{9,17... | collective-permute-start | bytes 786440 | tf_op jit(solution)/shard_map/ppermute | solution.py:30
  15.4 1.6 collective-permute-start.3
  19.5 1.5 collective-permute-done.3.other1
  21.1 8.9 %collective-permute-done.2.mine23 = bf16[512,256]{1,0:T(8,128)(2,1)S(1)} collective-permute-done((bf16[512,256]{1,0:T(8,128)(2,1)S(1)}, bf16[512,256]{1,0:T(8,128)(2,1)S(1)}, u32[]{:S(2)}, u32[]{:S(2)}) %collective-permute-start.2) | collective-permute-done | bytes 262176 | tf_op jit(solution)/shard_map/ppermute | solution.py:30
  30.0 1.5 collective-permute-start.5
  31.7 6.6 %collective-permute-done.5.other23 = bf16[512,256]{1,0:T(8,128)(2,1)S(1)} collective-permute-done((bf16[512,256]{1,0:T(8,128)(2,1)S(1)}, bf16[512,256]{1,0:T(8,128)(2,1)S(1)}, u32[]{:S(2)}, u32[]{:S(2)}) %collective-permute-start.5) | collective-permute-done | bytes 262176 | tf_op jit(solution)/shard_map/ppermute | solution.py:34
  41.6 11.6 %attention.1 = (bf16[256,1024]{1,0:T(8,128)(2,1)}, bf16[4,256,512]{2,1,0:T(8,128)(2,1)S(1)}, bf16[5,256,512]{2,1,0:T(8,128)(2,1)S(1)}) custom-call(s32[1]{0:T(128)} %bitcast.side_ref, s32[1,1024]{1,0:T(1,128)S(1)} %bitcast.48, bf16[256,1024]{1,0:T(8,128)(2,1)S(1)} %copy-done.1, bf16[256,1024]{1,0:T(8,128)(2,1)S(1)} %copy-done.2, ...), custom_call_target="tpu_custom_call" | custom-call | flops 6039797760 | bytes 8388608 | tf_op jit(solution)/shard_map/attention/pallas_call | solution.py:170
  53.3 2.9 %constant_dynamic-slice_fusion = (bf16[256,1024]{1,0:T(8,128)(2,1)}, bf16[256,1024]{1,0:T(8,128)(2,1)}, bf16[256,1024]{1,0:T(8,128)(2,1)}, bf16[256,1024]{1,0:T(8,128)(2,1)}) fusion(bf16[256,4096]{1,0:T(8,128)(2,1)} %param.9, s32[]{:T(128)S(6)} %select_n.196, s32[]{:T(128)S(6)} %select_n.192, s32[]{:T(128)S(6)} %select_n.190, s32[]{:T(128)S(6)} %select_n.194), kind=kLoop, calls=%fused_computation.61 | loop fusion | bytes 4194320 | tf_op jit(solution)/shard_map/dynamic_slice | solution.py:43
  56.2 5.9 %collective-permute-start.10 = (bf16[256,1024]{1,0:T(8,128)(2,1)}, bf16[256,1024]{1,0:T(8,128)(2,1)}, u32[]{:S(2)}, u32[]{:S(2)}) collective-permute-start(bf16[256,1024]{1,0:T(8,128)(2,1)} %get-tuple-element.30), channel_id=1, source_target_pairs={{0,128},{64,192},{128,0},{192,64},{1,129},{65,193},{129,1},{193,65... | collective-permute-start | bytes 1572872 | tf_op jit(solution)/shard_map/ppermute | solution.py:39
  64.3 11.0 %collective-permute-done.10 = bf16[256,1024]{1,0:T(8,128)(2,1)} collective-permute-done((bf16[256,1024]{1,0:T(8,128)(2,1)}, bf16[256,1024]{1,0:T(8,128)(2,1)}, u32[]{:S(2)}, u32[]{:S(2)}) %collective-permute-start.10) | collective-permute-done | bytes 524320 | tf_op jit(solution)/shard_map/ppermute | solution.py:39
  75.3 10.9 %collective-permute-done.11 = bf16[256,1024]{1,0:T(8,128)(2,1)} collective-permute-done((bf16[256,1024]{1,0:T(8,128)(2,1)}, bf16[256,1024]{1,0:T(8,128)(2,1)}, u32[]{:S(2)}, u32[]{:S(2)}) %collective-permute-start.11) | collective-permute-done | bytes 524320 | tf_op jit(solution)/shard_map/ppermute | solution.py:39
  86.7 1.8 %collective-permute-start.13 = (bf16[512,256]{1,0:T(8,128)(2,1)S(1)}, bf16[512,256]{1,0:T(8,128)(2,1)S(1)}, u32[]{:S(2)}, u32[]{:S(2)}) collective-permute-start(bf16[512,256]{1,0:T(8,128)(2,1)S(1)} %pad_maximum_fusion.2), channel_id=1, source_target_pairs={{0,1},{1,0},{2,3},{3,2},{4,5},{5,4},{6,7},{7,6},{8,9},{9,8},{10,11... | collective-permute-start | bytes 786440 | tf_op jit(solution)/shard_map/ppermute | solution.py:34
  88.6 6.5 %collective-permute-done.13.refs_1_ = bf16[512,256]{1,0:T(8,128)(2,1)S(1)} collective-permute-done((bf16[512,256]{1,0:T(8,128)(2,1)S(1)}, bf16[512,256]{1,0:T(8,128)(2,1)S(1)}, u32[]{:S(2)}, u32[]{:S(2)}) %collective-permute-start.13) | collective-permute-done | bytes 262176 | tf_op jit(solution)/shard_map/ppermute | solution.py:34
  95.1 1.3 collective-permute-start.14
  96.4 2.0 %collective-permute-start.17 = (bf16[256,256]{1,0:T(8,128)(2,1)S(1)}, bf16[256,256]{1,0:T(8,128)(2,1)S(1)}, u32[]{:S(2)}, u32[]{:S(2)}) collective-permute-start(bf16[256,256]{1,0:T(8,128)(2,1)S(1)} %get-tuple-element.56), channel_id=1, source_target_pairs={{0,1},{1,0},{2,3},{3,2},{4,5},{5,4},{6,7},{7,6},{8,9},{9,8},{10,11... | collective-permute-start | bytes 393224 | tf_op jit(solution)/shard_map/ppermute | solution.py:34
  98.7 1.7 %collective-permute-start.12 = (bf16[256,256]{1,0:T(8,128)(2,1)S(1)}, bf16[256,256]{1,0:T(8,128)(2,1)S(1)}, u32[]{:S(2)}, u32[]{:S(2)}) collective-permute-start(bf16[256,256]{1,0:T(8,128)(2,1)S(1)} %get-tuple-element.50), channel_id=1, source_target_pairs={{0,1},{1,0},{2,3},{3,2},{4,5},{5,4},{6,7},{7,6},{8,9},{9,8},{10,11... | collective-permute-start | bytes 393224 | tf_op jit(solution)/shard_map/ppermute | solution.py:34
  100.4 2.6 %collective-permute-done.17.refs_1_ = bf16[256,256]{1,0:T(8,128)(2,1)S(1)} collective-permute-done((bf16[256,256]{1,0:T(8,128)(2,1)S(1)}, bf16[256,256]{1,0:T(8,128)(2,1)S(1)}, u32[]{:S(2)}, u32[]{:S(2)}) %collective-permute-start.17) | collective-permute-done | bytes 131104 | tf_op jit(solution)/shard_map/ppermute | solution.py:34
  104.3 1.8 %collective-permute-done.14 = bf16[512,256]{1,0:T(8,128)(2,1)S(1)} collective-permute-done((bf16[512,256]{1,0:T(8,128)(2,1)S(1)}, bf16[512,256]{1,0:T(8,128)(2,1)S(1)}, u32[]{:S(2)}, u32[]{:S(2)}) %collective-permute-start.14) | collective-permute-done | bytes 262176 | tf_op jit(solution)/shard_map/ppermute | solution.py:30
  106.2 8.9 %collective-permute-start.16 = (bf16[256,256]{1,0:T(8,128)(2,1)S(1)}, bf16[256,256]{1,0:T(8,128)(2,1)S(1)}, u32[]{:S(2)}, u32[]{:S(2)}) collective-permute-start(bf16[256,256]{1,0:T(8,128)(2,1)S(1)} %merge.4), channel_id=1, source_target_pairs={{4,0},{5,1},{6,2},{7,3},{8,4},{9,5},{10,6},{11,7},{12,8},{13,9},{1... | collective-permute-start | bytes 393224 | tf_op jit(solution)/shard_map/ppermute | solution.py:30
  115.1 2.5 %collective-permute-done.16 = bf16[256,256]{1,0:T(8,128)(2,1)S(1)} collective-permute-done((bf16[256,256]{1,0:T(8,128)(2,1)S(1)}, bf16[256,256]{1,0:T(8,128)(2,1)S(1)}, u32[]{:S(2)}, u32[]{:S(2)}) %collective-permute-start.16) | collective-permute-done | bytes 131104 | tf_op jit(solution)/shard_map/ppermute | solution.py:30
  117.7 1.3 collective-permute-start.19
  119.1 4.4 %collective-permute-start.20 = (bf16[256,256]{1,0:T(8,128)(2,1)S(1)}, bf16[256,256]{1,0:T(8,128)(2,1)S(1)}, u32[]{:S(2)}, u32[]{:S(2)}) collective-permute-start(bf16[256,256]{1,0:T(8,128)(2,1)S(1)} %fusion.35), channel_id=1, source_target_pairs={{0,64},{64,128},{128,192},{192,0},{1,65},{65,129},{129,193},{193,1... | collective-permute-start | bytes 393224 | tf_op jit(solution)/shard_map/ppermute | solution.py:39
  123.5 2.8 %collective-permute-start.21 = (bf16[256,256]{1,0:T(8,128)(2,1)S(1)}, bf16[256,256]{1,0:T(8,128)(2,1)S(1)}, u32[]{:S(2)}, u32[]{:S(2)}) collective-permute-start(bf16[256,256]{1,0:T(8,128)(2,1)S(1)} %fusion.35), channel_id=1, source_target_pairs={{0,128},{64,192},{128,0},{192,64},{1,129},{65,193},{129,1},{193,65... | collective-permute-start | bytes 393224 | tf_op jit(solution)/shard_map/ppermute | solution.py:39
  127.8 2.9 %collective-permute-done.21 = bf16[256,256]{1,0:T(8,128)(2,1)S(1)} collective-permute-done((bf16[256,256]{1,0:T(8,128)(2,1)S(1)}, bf16[256,256]{1,0:T(8,128)(2,1)S(1)}, u32[]{:S(2)}, u32[]{:S(2)}) %collective-permute-start.21) | collective-permute-done | bytes 131104 | tf_op jit(solution)/shard_map/ppermute | solution.py:39
  131.3 2.1 %fusion.11 = f32[1024,256]{1,0:T(8,128)S(1)} fusion(bf16[256,1024]{1,0:T(8,128)(2,1)} %collective-permute-done.11, bf16[256,1024]{1,0:T(8,128)(2,1)} %collective-permute-done.10, bf16[256,1024]{1,0:T(8,128)(2,1)} %collective-permute-done.9, bf16[256,1024]{1,0:T(8,128)(2,1)S(1)} %copy-done.4, bf16[256,256]{1,0:T(8,128)(2,1)S(1)} %collective-permute-done.22, ...), kind=kOutput, calls=%fused_computation.13 | convolution fusion | flops 547618816 | bytes 3670016 | tf_op jit(solution)/shard_map/dot_general | solution.py:331
  133.5 1.7 %collective-permute-done.23 = bf16[16,32,256]{2,1,0:T(8,128)(2,1)} collective-permute-done((bf16[16,32,256]{2,1,0:T(8,128)(2,1)S(1)}, bf16[16,32,256]{2,1,0:T(8,128)(2,1)}, u32[]{:S(2)}, u32[]{:S(2)}) %collective-permute-start.23) | collective-permute-done | bytes 262176 | tf_op jit(solution)/shard_map/ppermute | solution.py:34
  135.2 1.7 %fusion.21 = bf16[16,32,256]{2,1,0:T(8,128)(2,1)} fusion(bf16[16,32,256]{2,1,0:T(8,128)(2,1)} %collective-permute-done.23, f32[16,2,32,256]{3,2,1,0:T(8,128)S(1)} %bitcast.51, s32[]{:T(128)S(6)} %select_n.217), kind=kLoop, calls=%fused_computation.27 | loop fusion | flops 393216 | bytes 1048580 | tf_op jit(solution)/shard_map/convert_element_type | solution.py:337
  136.9 10.1 %all-to-all-start = ((bf16[16,32,256]{2,1,0:T(8,128)(2,1)}), bf16[16,32,256]{2,1,0:T(8,128)(2,1)S(1)}, u32[]{:S(2)}, u32[]{:S(2)}) async-start(bf16[16,32,256]{2,1,0:T(8,128)(2,1)} %fusion.21), calls=%async_computation | async-start | bytes 524288 | tf_op jit(solution)/shard_map/all_to_all | solution.py:338
  147.9 1.7 %convolution_convert_fusion = bf16[256,2048]{1,0:T(8,128)(2,1)} fusion(bf16[2048,256]{1,0:T(8,128)(2,1)S(1)} %get-tuple-element.32, bf16[2048,256]{1,0:T(8,128)(2,1)S(1)} %get-tuple-element.31, bf16[256,256]{1,0:T(8,128)(2,1)S(1)} %copy-done.6, bf16[256,256]{1,0:T(8,128)(2,1)S(1)} %fusion.35), kind=kOutput, calls=%fused_computation | convolution fusion | flops 542113792 | bytes 3407872 | tf_op jit(solution)/shard_map/dot_general | solution.py:322
  149.6 9.2 %all-to-all-done = bf16[16,32,256]{2,1,0:T(8,128)(2,1)S(1)} async-done(((bf16[16,32,256]{2,1,0:T(8,128)(2,1)}), bf16[16,32,256]{2,1,0:T(8,128)(2,1)S(1)}, u32[]{:S(2)}, u32[]{:S(2)}) %all-to-all-start) | async-done | bytes 262176 | tf_op jit(solution)/shard_map/all_to_all | solution.py:338
  (64 shorter events, 15.8 us)
Async XLA Ops:
  1.9 36.5 %copy-start = (bf16[256,512]{1,0:T(8,128)(2,1)S(1)}, bf16[256,512]{1,0:T(8,128)(2,1)}, u32[]{:S(2)}) copy-start(bf16[256,512]{1,0:T(8,128)(2,1)} %own_ref.1) | copy-start | bytes 786436
  1.9 11.1 %collective-permute-start = (bf16[256,256]{1,0:T(8,128)(2,1)S(1)}, bf16[256,256]{1,0:T(8,128)(2,1)S(1)}, u32[]{:S(2)}, u32[]{:S(2)}) collective-permute-start(bf16[256,256]{1,0:T(8,128)(2,1)S(1)} %get-tuple-element.65), channel_id=1, source_target_pairs={{0,4},{1,5},{2,6},{3,7},{4,8},{5,9},{6,10},{7,11},{8,12},{9,13},{1... | collective-permute-start | bytes 393224 | tf_op jit(solution)/shard_map/ppermute | solution.py:30
  5.9 11.7 %collective-permute-start.1 = (bf16[256,256]{1,0:T(8,128)(2,1)S(1)}, bf16[256,256]{1,0:T(8,128)(2,1)S(1)}, u32[]{:S(2)}, u32[]{:S(2)}) collective-permute-start(bf16[256,256]{1,0:T(8,128)(2,1)S(1)} %get-tuple-element.64), channel_id=1, source_target_pairs={{0,16},{1,17},{2,18},{3,19},{4,20},{5,21},{6,22},{7,23},{8,24},{9,... | collective-permute-start | bytes 393224 | tf_op jit(solution)/shard_map/ppermute | solution.py:30
  13.1 16.9 %collective-permute-start.2 = (bf16[512,256]{1,0:T(8,128)(2,1)S(1)}, bf16[512,256]{1,0:T(8,128)(2,1)S(1)}, u32[]{:S(2)}, u32[]{:S(2)}) collective-permute-start(bf16[512,256]{1,0:T(8,128)(2,1)S(1)} %pad_maximum_fusion.1), channel_id=1, source_target_pairs={{0,8},{1,9},{2,10},{3,11},{4,12},{5,13},{6,14},{7,15},{8,16},{9,17... | collective-permute-start | bytes 786440 | tf_op jit(solution)/shard_map/ppermute | solution.py:30
  15.4 5.5 %collective-permute-start.3 = (bf16[256,256]{1,0:T(8,128)(2,1)S(1)}, bf16[256,256]{1,0:T(8,128)(2,1)S(1)}, u32[]{:S(2)}, u32[]{:S(2)}) collective-permute-start(bf16[256,256]{1,0:T(8,128)(2,1)S(1)} %collective-permute-done.mine1), channel_id=1, source_target_pairs={{0,1},{1,0},{2,3},{3,2},{4,5},{5,4},{6,7},{7,6},{8,9},{9,8},{10,11... | collective-permute-start | bytes 393224 | tf_op jit(solution)/shard_map/ppermute | solution.py:34
  17.6 13.9 %collective-permute-start.4 = (bf16[256,256]{1,0:T(8,128)(2,1)S(1)}, bf16[256,256]{1,0:T(8,128)(2,1)S(1)}, u32[]{:S(2)}, u32[]{:S(2)}) collective-permute-start(bf16[256,256]{1,0:T(8,128)(2,1)S(1)} %collective-permute-done.1.mine4), channel_id=1, source_target_pairs={{0,1},{1,0},{2,3},{3,2},{4,5},{5,4},{6,7},{7,6},{8,9},{9,8},{10,11... | collective-permute-start | bytes 393224 | tf_op jit(solution)/shard_map/ppermute | solution.py:34
  30.0 8.3 %collective-permute-start.5 = (bf16[512,256]{1,0:T(8,128)(2,1)S(1)}, bf16[512,256]{1,0:T(8,128)(2,1)S(1)}, u32[]{:S(2)}, u32[]{:S(2)}) collective-permute-start(bf16[512,256]{1,0:T(8,128)(2,1)S(1)} %collective-permute-done.2.mine23), channel_id=1, source_target_pairs={{0,1},{1,0},{2,3},{3,2},{4,5},{5,4},{6,7},{7,6},{8,9},{9,8},{10,11... | collective-permute-start | bytes 786440 | tf_op jit(solution)/shard_map/ppermute | solution.py:34
  31.6 9.9 %copy-start.1 = (bf16[256,1024]{1,0:T(8,128)(2,1)S(1)}, bf16[256,1024]{1,0:T(8,128)(2,1)}, u32[]{:S(2)}) copy-start(bf16[256,1024]{1,0:T(8,128)(2,1)} %query_ref.1) | copy-start | bytes 1572868
  31.7 9.9 %copy-start.2 = (bf16[256,1024]{1,0:T(8,128)(2,1)S(1)}, bf16[256,1024]{1,0:T(8,128)(2,1)}, u32[]{:S(2)}) copy-start(bf16[256,1024]{1,0:T(8,128)(2,1)} %out_ref.1) | copy-start | bytes 1572868
  38.8 2.0 %collective-permute-start.6 = (bf16[512,512]{1,0:T(8,128)(2,1)S(1)}, bf16[512,512]{1,0:T(8,128)(2,1)S(1)}, u32[]{:S(2)}, u32[]{:S(2)}) collective-permute-start(bf16[512,512]{1,0:T(8,128)(2,1)S(1)} %get-tuple-element.58), channel_id=1, source_target_pairs={{0,2},{2,0},{1,3},{3,1},{4,6},{6,4},{5,7},{7,5},{8,10},{10,8},{9,1... | collective-permute-start | bytes 1572872 | tf_op jit(solution)/shard_map/ppermute | solution.py:34
  38.9 2.6 %collective-permute-start.7 = (bf16[512,512]{1,0:T(8,128)(2,1)S(1)}, bf16[512,512]{1,0:T(8,128)(2,1)S(1)}, u32[]{:S(2)}, u32[]{:S(2)}) collective-permute-start(bf16[512,512]{1,0:T(8,128)(2,1)S(1)} %get-tuple-element.57), channel_id=1, source_target_pairs={{0,2},{2,0},{1,3},{3,1},{4,6},{6,4},{5,7},{7,5},{8,10},{10,8},{9,1... | collective-permute-start | bytes 1572872 | tf_op jit(solution)/shard_map/ppermute | solution.py:34
  53.2 33.0 %collective-permute-start.8 = (bf16[1024,512]{1,0:T(8,128)(2,1)S(1)}, bf16[1024,512]{1,0:T(8,128)(2,1)S(1)}, u32[]{:S(2)}, u32[]{:S(2)}) collective-permute-start(bf16[1024,512]{1,0:T(8,128)(2,1)S(1)} %bitcast.49), channel_id=1, source_target_pairs={{0,2},{2,0},{1,3},{3,1},{4,6},{6,4},{5,7},{7,5},{8,10},{10,8},{9,1... | collective-permute-start | bytes 3145736 | tf_op jit(solution)/shard_map/ppermute | solution.py:34
  56.2 19.1 %collective-permute-start.10 = (bf16[256,1024]{1,0:T(8,128)(2,1)}, bf16[256,1024]{1,0:T(8,128)(2,1)}, u32[]{:S(2)}, u32[]{:S(2)}) collective-permute-start(bf16[256,1024]{1,0:T(8,128)(2,1)} %get-tuple-element.30), channel_id=1, source_target_pairs={{0,128},{64,192},{128,0},{192,64},{1,129},{65,193},{129,1},{193,65... | collective-permute-start | bytes 1572872 | tf_op jit(solution)/shard_map/ppermute | solution.py:39
  62.1 24.0 %collective-permute-start.11 = (bf16[256,1024]{1,0:T(8,128)(2,1)}, bf16[256,1024]{1,0:T(8,128)(2,1)}, u32[]{:S(2)}, u32[]{:S(2)}) collective-permute-start(bf16[256,1024]{1,0:T(8,128)(2,1)} %get-tuple-element.27), channel_id=1, source_target_pairs={{0,192},{64,0},{128,64},{192,128},{1,193},{65,1},{129,65},{193,129... | collective-permute-start | bytes 1572872 | tf_op jit(solution)/shard_map/ppermute | solution.py:39
  63.2 23.0 %collective-permute-start.9 = (bf16[256,1024]{1,0:T(8,128)(2,1)}, bf16[256,1024]{1,0:T(8,128)(2,1)}, u32[]{:S(2)}, u32[]{:S(2)}) collective-permute-start(bf16[256,1024]{1,0:T(8,128)(2,1)} %get-tuple-element.28), channel_id=1, source_target_pairs={{0,64},{64,128},{128,192},{192,0},{1,65},{65,129},{129,193},{193,1... | collective-permute-start | bytes 1572872 | tf_op jit(solution)/shard_map/ppermute | solution.py:39
  86.7 8.3 %collective-permute-start.13 = (bf16[512,256]{1,0:T(8,128)(2,1)S(1)}, bf16[512,256]{1,0:T(8,128)(2,1)S(1)}, u32[]{:S(2)}, u32[]{:S(2)}) collective-permute-start(bf16[512,256]{1,0:T(8,128)(2,1)S(1)} %pad_maximum_fusion.2), channel_id=1, source_target_pairs={{0,1},{1,0},{2,3},{3,2},{4,5},{5,4},{6,7},{7,6},{8,9},{9,8},{10,11... | collective-permute-start | bytes 786440 | tf_op jit(solution)/shard_map/ppermute | solution.py:34
  88.5 42.7 %copy-start.4 = (bf16[256,1024]{1,0:T(8,128)(2,1)S(1)}, bf16[256,1024]{1,0:T(8,128)(2,1)}, u32[]{:S(2)}) copy-start(bf16[256,1024]{1,0:T(8,128)(2,1)} %get-tuple-element.20) | copy-start | bytes 1572868
  95.1 11.1 %collective-permute-start.14 = (bf16[512,256]{1,0:T(8,128)(2,1)S(1)}, bf16[512,256]{1,0:T(8,128)(2,1)S(1)}, u32[]{:S(2)}, u32[]{:S(2)}) collective-permute-start(bf16[512,256]{1,0:T(8,128)(2,1)S(1)} %merge.3), channel_id=1, source_target_pairs={{8,0},{9,1},{10,2},{11,3},{12,4},{13,5},{14,6},{15,7},{16,8},{17,9... | collective-permute-start | bytes 786440 | tf_op jit(solution)/shard_map/ppermute | solution.py:30
  96.4 6.6 %collective-permute-start.17 = (bf16[256,256]{1,0:T(8,128)(2,1)S(1)}, bf16[256,256]{1,0:T(8,128)(2,1)S(1)}, u32[]{:S(2)}, u32[]{:S(2)}) collective-permute-start(bf16[256,256]{1,0:T(8,128)(2,1)S(1)} %get-tuple-element.56), channel_id=1, source_target_pairs={{0,1},{1,0},{2,3},{3,2},{4,5},{5,4},{6,7},{7,6},{8,9},{9,8},{10,11... | collective-permute-start | bytes 393224 | tf_op jit(solution)/shard_map/ppermute | solution.py:34
  98.4 7.8 %collective-permute-start.15 = (bf16[256,256]{1,0:T(8,128)(2,1)S(1)}, bf16[256,256]{1,0:T(8,128)(2,1)S(1)}, u32[]{:S(2)}, u32[]{:S(2)}) collective-permute-start(bf16[256,256]{1,0:T(8,128)(2,1)S(1)} %get-tuple-element.46), channel_id=1, source_target_pairs={{0,1},{1,0},{2,3},{3,2},{4,5},{5,4},{6,7},{7,6},{8,9},{9,8},{10,11... | collective-permute-start | bytes 393224 | tf_op jit(solution)/shard_map/ppermute | solution.py:34
  98.7 16.5 %collective-permute-start.12 = (bf16[256,256]{1,0:T(8,128)(2,1)S(1)}, bf16[256,256]{1,0:T(8,128)(2,1)S(1)}, u32[]{:S(2)}, u32[]{:S(2)}) collective-permute-start(bf16[256,256]{1,0:T(8,128)(2,1)S(1)} %get-tuple-element.50), channel_id=1, source_target_pairs={{0,1},{1,0},{2,3},{3,2},{4,5},{5,4},{6,7},{7,6},{8,9},{9,8},{10,11... | collective-permute-start | bytes 393224 | tf_op jit(solution)/shard_map/ppermute | solution.py:34
  103.0 12.1 %collective-permute-start.18 = (bf16[256,256]{1,0:T(8,128)(2,1)S(1)}, bf16[256,256]{1,0:T(8,128)(2,1)S(1)}, u32[]{:S(2)}, u32[]{:S(2)}) collective-permute-start(bf16[256,256]{1,0:T(8,128)(2,1)S(1)} %merge.5), channel_id=1, source_target_pairs={{16,0},{17,1},{18,2},{19,3},{20,4},{21,5},{22,6},{23,7},{24,8},{25... | collective-permute-start | bytes 393224 | tf_op jit(solution)/shard_map/ppermute | solution.py:30
  106.2 11.4 %collective-permute-start.16 = (bf16[256,256]{1,0:T(8,128)(2,1)S(1)}, bf16[256,256]{1,0:T(8,128)(2,1)S(1)}, u32[]{:S(2)}, u32[]{:S(2)}) collective-permute-start(bf16[256,256]{1,0:T(8,128)(2,1)S(1)} %merge.4), channel_id=1, source_target_pairs={{4,0},{5,1},{6,2},{7,3},{8,4},{9,5},{10,6},{11,7},{12,8},{13,9},{1... | collective-permute-start | bytes 393224 | tf_op jit(solution)/shard_map/ppermute | solution.py:30
  117.7 9.7 %collective-permute-start.19 = (bf16[256,256]{1,0:T(8,128)(2,1)S(1)}, bf16[256,256]{1,0:T(8,128)(2,1)S(1)}, u32[]{:S(2)}, u32[]{:S(2)}) collective-permute-start(bf16[256,256]{1,0:T(8,128)(2,1)S(1)} %fusion.35), channel_id=1, source_target_pairs={{0,1},{1,0},{2,3},{3,2},{4,5},{5,4},{6,7},{7,6},{8,9},{9,8},{10,11... | collective-permute-start | bytes 393224 | tf_op jit(solution)/shard_map/ppermute | solution.py:34
  119.1 8.7 %collective-permute-start.20 = (bf16[256,256]{1,0:T(8,128)(2,1)S(1)}, bf16[256,256]{1,0:T(8,128)(2,1)S(1)}, u32[]{:S(2)}, u32[]{:S(2)}) collective-permute-start(bf16[256,256]{1,0:T(8,128)(2,1)S(1)} %fusion.35), channel_id=1, source_target_pairs={{0,64},{64,128},{128,192},{192,0},{1,65},{65,129},{129,193},{193,1... | collective-permute-start | bytes 393224 | tf_op jit(solution)/shard_map/ppermute | solution.py:39
  123.5 7.2 %collective-permute-start.21 = (bf16[256,256]{1,0:T(8,128)(2,1)S(1)}, bf16[256,256]{1,0:T(8,128)(2,1)S(1)}, u32[]{:S(2)}, u32[]{:S(2)}) collective-permute-start(bf16[256,256]{1,0:T(8,128)(2,1)S(1)} %fusion.35), channel_id=1, source_target_pairs={{0,128},{64,192},{128,0},{192,64},{1,129},{65,193},{129,1},{193,65... | collective-permute-start | bytes 393224 | tf_op jit(solution)/shard_map/ppermute | solution.py:39
  126.3 5.0 %collective-permute-start.22 = (bf16[256,256]{1,0:T(8,128)(2,1)S(1)}, bf16[256,256]{1,0:T(8,128)(2,1)S(1)}, u32[]{:S(2)}, u32[]{:S(2)}) collective-permute-start(bf16[256,256]{1,0:T(8,128)(2,1)S(1)} %fusion.35), channel_id=1, source_target_pairs={{0,192},{64,0},{128,64},{192,128},{1,193},{65,1},{129,65},{193,129... | collective-permute-start | bytes 393224 | tf_op jit(solution)/shard_map/ppermute | solution.py:39
  127.5 3.8 %copy-start.5 = (bf16[256,256]{1,0:T(8,128)(2,1)}, bf16[256,256]{1,0:T(8,128)(2,1)S(1)}, u32[]{:S(2)}) copy-start(bf16[256,256]{1,0:T(8,128)(2,1)S(1)} %collective-permute-done.19) | copy-start | bytes 393220
  133.4 13.6 %copy-start.3 = (bf16[2,2048,256]{2,1,0:T(8,128)(2,1)S(1)}, bf16[2,2048,256]{2,1,0:T(8,128)(2,1)}, u32[]{:S(2)}) copy-start(bf16[2,2048,256]{2,1,0:T(8,128)(2,1)} %param.10) | copy-start | bytes 6291460
  133.4 1.8 %collective-permute-start.23 = (bf16[16,32,256]{2,1,0:T(8,128)(2,1)S(1)}, bf16[16,32,256]{2,1,0:T(8,128)(2,1)}, u32[]{:S(2)}, u32[]{:S(2)}) collective-permute-start(bf16[16,32,256]{2,1,0:T(8,128)(2,1)S(1)} %fusion.22), channel_id=1, source_target_pairs={{0,2},{2,0},{1,3},{3,1},{4,6},{6,4},{5,7},{7,5},{8,10},{10,8},{9,1... | collective-permute-start | bytes 786440 | tf_op jit(solution)/shard_map/ppermute | solution.py:34
  136.9 22.0 %all-to-all-start = ((bf16[16,32,256]{2,1,0:T(8,128)(2,1)}), bf16[16,32,256]{2,1,0:T(8,128)(2,1)S(1)}, u32[]{:S(2)}, u32[]{:S(2)}) async-start(bf16[16,32,256]{2,1,0:T(8,128)(2,1)} %fusion.21), calls=%async_computation | async-start | bytes 524288 | tf_op jit(solution)/shard_map/all_to_all | solution.py:338
  147.0 0.9 copy-start.6

commit v2 on v1

--- a/solution.py
+++ b/solution.py
@@ -80,15 +80,16 @@
         queries[h * tok : (h + 1) * tok, :] = query_ref[:, h * hd : (h + 1) * hd]
         outs[h * tok : (h + 1) * tok, :] = out_ref[:, h * hd : (h + 1) * hd]
 
-    @pl.when(side_ref[0] == 0)
-    def _():
-        for d in mine:
+    for d in mine:
+        side = side_ref[1 if d == 1 else 0]
+
+        @pl.when(side == 0)
+        def _():
             keys[last - 2 * d] = mine[d][...]
             values[last - 2 * d] = other[d][...]
 
-    @pl.when(side_ref[0] != 0)
-    def _():
-        for d in mine:
+        @pl.when(side != 0)
+        def _():
             keys[last - 2 * d] = other[d][...]
             values[last - 2 * d] = mine[d][...]
 
@@ -227,9 +228,12 @@
         turn = (z + distance >= LINE).astype(jnp.int32)
         return columns(key_value, l ^ turn, hd)
 
-    mine1 = moved(taken(1), 1, True)
+    ahead = (z >= LINE - 2).astype(jnp.int32)
+    ahead_next = ((z + 1) % LINE >= LINE - 2).astype(jnp.int32)
+    turn = (z + 1 >= LINE).astype(jnp.int32)
+    mine1 = moved(columns(key_value, l ^ turn ^ ahead_next, hd), 1, True)
     mine4 = moved(taken(4), 4, True)
-    mine23 = moved(jnp.concatenate([columns(key_value, l, hd), mine1], axis=0), 2, False)
+    mine23 = moved(jnp.concatenate([taken(2), mine1], axis=0), 2, True)
     other1 = swapped(mine1, "l")
     other4 = swapped(mine4, "l")
     other23 = swapped(mine23, "l")
@@ -238,7 +242,7 @@
     blocks = {0: key_value}
     for d in (1, 2, 3, 4):
         blocks[d] = jnp.where(
-            l == 0,
+            (l ^ ahead if d == 1 else l) == 0,
             jnp.concatenate([mine[d], other[d]], axis=1),
             jnp.concatenate([other[d], mine[d]], axis=1),
         )
@@ -265,7 +269,7 @@
     low = jnp.maximum(before, 1 + jnp.arange(tok, dtype=jnp.int32))
     low = jnp.tile(low, heads)[None, :]
     query_grad, given, kept = attention(
-        l.reshape(1).astype(jnp.int32),
+        jnp.stack([l, l ^ ahead]).astype(jnp.int32),
         low,
         query,
         out_grad,
@@ -290,8 +294,8 @@
 
     sides = {
         4: l ^ (z < 4).astype(jnp.int32),
-        3: l ^ ((z + LINE - 2) % LINE < 1).astype(jnp.int32),
-        2: l,
+        3: l ^ (z < 3).astype(jnp.int32),
+        2: l ^ (z < 2).astype(jnp.int32),
         1: l ^ (z < 1).astype(jnp.int32),
         0: l,
     }
@@ -305,7 +309,7 @@
     four = merged(*paired(4))
     one = paired(1)
     none = paired(0)
-    back23 = moved(two_three, -2, False)
+    back23 = moved(two_three, -2, True)
     back4 = moved(four, -4, True)
     one = merged(*one, back23[tok:])
     back1 = moved(one, -1, True)

time: 161 us -> 161 us (level)
    ppermute x12, waiting for transfers between devices: 19.8 us -> 21.9 us  [swapped(): return lax.ppermute(value, axis, [(0, 1), (1, 0)])]
  transfers between devices with their start and end apart: 25 -> 25, of which waited for: 17 -> 16; matrix products, arithmetic and copies ran while one was open for 5% -> 5% of each run, Pallas kernels for 0% -> 0%
where the time goes in v2:
time: 161 us; the launch traced here: 160 us
  waiting for transfers between devices  68.7 us (43%)
  starting transfers between devices  61.2 us (38%)
  Pallas kernels  12.3 us (8%)
  local copies, waits for them, and re-layouts  7.77 us (5%)
  other arithmetic  4.92 us (3%)
  matrix products  3.81 us (2%)
    ppermute x6, waiting for transfers between devices, turned(): lax.ppermute(value, axis, [(i, (i + steps) % count) for i in range(count)])  25.3 us
    ppermute x6, starting transfers between devices, moved(): return lax.ppermute(value, ALL, routes)  24.3 us
    ppermute x12, waiting for transfers between devices, swapped(): return lax.ppermute(value, axis, [(0, 1), (1, 0)])  21.9 us
    ppermute x6, starting transfers between devices, turned(): lax.ppermute(value, axis, [(i, (i + steps) % count) for i in range(count)])  15.3 us
    ppermute x6, waiting for transfers between devices, moved(): return lax.ppermute(value, ALL, routes)  12.3 us
    pallas_call x1, Pallas kernels, attention(): pl.pallas_call(attention_kernel, out_shape=(jax.ShapeDtypeStruct((tok, wi...  12.2 us
    ppermute x12, starting transfers between devices, swapped(): return lax.ppermute(value, axis, [(0, 1), (1, 0)])  11.7 us
    all_to_all x1, starting transfers between devices, local(): lax.all_to_all(total, ('xh', 'z'), split_axis=0, concat_axis=0, tiled=True)  10 us
  transfers between devices with their start and end apart: 25, of which 16 were waited for; matrix products, arithmetic and copies ran while one was open for 5% of the time, Pallas kernels for 0%

profile of v2, /device:TPU:32, one launch (start us, length us, event | category | flops | bytes accessed | tf_op | source)
XLA Modules:
  0.0 159.7 jit_solution(12356809995393867813)
XLA Ops:
  1.8 4.0 %collective-permute-start = (bf16[256,256]{1,0:T(8,128)(2,1)S(1)}, bf16[256,256]{1,0:T(8,128)(2,1)S(1)}, u32[]{:S(2)}, u32[]{:S(2)}) collective-permute-start(bf16[256,256]{1,0:T(8,128)(2,1)S(1)} %get-tuple-element.65), channel_id=1, source_target_pairs={{0,4},{1,5},{2,6},{3,7},{4,8},{5,9},{6,10},{7,11},{8,12},{9,13},{1... | collective-permute-start | bytes 393224 | tf_op jit(solution)/shard_map/ppermute | solution.py:30
  5.8 7.3 %collective-permute-start.1 = (bf16[256,256]{1,0:T(8,128)(2,1)S(1)}, bf16[256,256]{1,0:T(8,128)(2,1)S(1)}, u32[]{:S(2)}, u32[]{:S(2)}) collective-permute-start(bf16[256,256]{1,0:T(8,128)(2,1)S(1)} %get-tuple-element.64), channel_id=1, source_target_pairs={{0,16},{1,17},{2,18},{3,19},{4,20},{5,21},{6,22},{7,23},{8,24},{9,... | collective-permute-start | bytes 393224 | tf_op jit(solution)/shard_map/ppermute | solution.py:30
  13.1 2.4 %collective-permute-start.2 = (bf16[512,256]{1,0:T(8,128)(2,1)S(1)}, bf16[512,256]{1,0:T(8,128)(2,1)S(1)}, u32[]{:S(2)}, u32[]{:S(2)}) collective-permute-start(bf16[512,256]{1,0:T(8,128)(2,1)S(1)} %pad_maximum_fusion.1), channel_id=1, source_target_pairs={{0,8},{1,9},{2,10},{3,11},{4,12},{5,13},{6,14},{7,15},{8,16},{9,17... | collective-permute-start | bytes 786440 | tf_op jit(solution)/shard_map/ppermute | solution.py:30
  17.0 1.5 collective-permute-start.3
  20.1 3.0 %collective-permute-done.3.other1 = bf16[256,256]{1,0:T(8,128)(2,1)S(1)} collective-permute-done((bf16[256,256]{1,0:T(8,128)(2,1)S(1)}, bf16[256,256]{1,0:T(8,128)(2,1)S(1)}, u32[]{:S(2)}, u32[]{:S(2)}) %collective-permute-start.3) | collective-permute-done | bytes 131104 | tf_op jit(solution)/shard_map/ppermute | solution.py:34
  23.2 6.8 %collective-permute-done.2.mine23 = bf16[512,256]{1,0:T(8,128)(2,1)S(1)} collective-permute-done((bf16[512,256]{1,0:T(8,128)(2,1)S(1)}, bf16[512,256]{1,0:T(8,128)(2,1)S(1)}, u32[]{:S(2)}, u32[]{:S(2)}) %collective-permute-start.2) | collective-permute-done | bytes 262176 | tf_op jit(solution)/shard_map/ppermute | solution.py:30
  30.0 1.5 collective-permute-start.5
  31.7 6.4 %collective-permute-done.5.other23 = bf16[512,256]{1,0:T(8,128)(2,1)S(1)} collective-permute-done((bf16[512,256]{1,0:T(8,128)(2,1)S(1)}, bf16[512,256]{1,0:T(8,128)(2,1)S(1)}, u32[]{:S(2)}, u32[]{:S(2)}) %collective-permute-start.5) | collective-permute-done | bytes 262176 | tf_op jit(solution)/shard_map/ppermute | solution.py:34
  41.4 12.2 %attention.1 = (bf16[256,1024]{1,0:T(8,128)(2,1)}, bf16[4,256,512]{2,1,0:T(8,128)(2,1)S(1)}, bf16[5,256,512]{2,1,0:T(8,128)(2,1)S(1)}) custom-call(s32[2]{0:T(128)S(1)} %pad_add_fusion.side_ref, s32[1,1024]{1,0:T(1,128)S(1)} %bitcast.49, bf16[256,1024]{1,0:T(8,128)(2,1)S(1)} %copy-done.1, bf16[256,1024]{1,0:T(8,128)(2,1)S(1)} %copy-done.2, ...), custom_call_target="tpu_custom_call" | custom-call | flops 6039797760 | bytes 8388608 | tf_op jit(solution)/shard_map/attention/pallas_call | solution.py:171
  53.7 2.7 %constant_dynamic-slice_fusion = (bf16[256,1024]{1,0:T(8,128)(2,1)}, bf16[256,1024]{1,0:T(8,128)(2,1)S(1)}, bf16[256,1024]{1,0:T(8,128)(2,1)}, bf16[256,1024]{1,0:T(8,128)(2,1)}) fusion(bf16[256,4096]{1,0:T(8,128)(2,1)} %param.9, s32[]{:T(128)S(6)} %select_n.207, s32[]{:T(128)S(6)} %select_n.203, s32[]{:T(128)S(6)} %select_n.201, s32[]{:T(128)S(6)} %select_n.205), kind=kLoop, calls=%fused_computation.61 | loop fusion | bytes 4194320 | tf_op jit(solution)/shard_map/dynamic_slice | solution.py:43
  56.4 5.4 %collective-permute-start.10 = (bf16[256,1024]{1,0:T(8,128)(2,1)}, bf16[256,1024]{1,0:T(8,128)(2,1)}, u32[]{:S(2)}, u32[]{:S(2)}) collective-permute-start(bf16[256,1024]{1,0:T(8,128)(2,1)} %get-tuple-element.30), channel_id=1, source_target_pairs={{0,128},{64,192},{128,0},{192,64},{1,129},{65,193},{129,1},{193,65... | collective-permute-start | bytes 1572872 | tf_op jit(solution)/shard_map/ppermute | solution.py:39
  64.0 11.0 %collective-permute-done.10 = bf16[256,1024]{1,0:T(8,128)(2,1)} collective-permute-done((bf16[256,1024]{1,0:T(8,128)(2,1)}, bf16[256,1024]{1,0:T(8,128)(2,1)}, u32[]{:S(2)}, u32[]{:S(2)}) %collective-permute-start.10) | collective-permute-done | bytes 524320 | tf_op jit(solution)/shard_map/ppermute | solution.py:39
  75.0 11.2 %collective-permute-done.11 = bf16[256,1024]{1,0:T(8,128)(2,1)} collective-permute-done((bf16[256,1024]{1,0:T(8,128)(2,1)}, bf16[256,1024]{1,0:T(8,128)(2,1)}, u32[]{:S(2)}, u32[]{:S(2)}) %collective-permute-start.11) | collective-permute-done | bytes 524320 | tf_op jit(solution)/shard_map/ppermute | solution.py:39
  87.9 1.8 %collective-permute-start.13 = (bf16[512,256]{1,0:T(8,128)(2,1)S(1)}, bf16[512,256]{1,0:T(8,128)(2,1)S(1)}, u32[]{:S(2)}, u32[]{:S(2)}) collective-permute-start(bf16[512,256]{1,0:T(8,128)(2,1)S(1)} %pad_maximum_fusion.2), channel_id=1, source_target_pairs={{0,1},{1,0},{2,3},{3,2},{4,5},{5,4},{6,7},{7,6},{8,9},{9,8},{10,11... | collective-permute-start | bytes 786440 | tf_op jit(solution)/shard_map/ppermute | solution.py:34
  89.7 6.2 %collective-permute-done.13.refs_1_ = bf16[512,256]{1,0:T(8,128)(2,1)S(1)} collective-permute-done((bf16[512,256]{1,0:T(8,128)(2,1)S(1)}, bf16[512,256]{1,0:T(8,128)(2,1)S(1)}, u32[]{:S(2)}, u32[]{:S(2)}) %collective-permute-start.13) | collective-permute-done | bytes 262176 | tf_op jit(solution)/shard_map/ppermute | solution.py:34
  97.3 2.0 %collective-permute-start.17 = (bf16[256,256]{1,0:T(8,128)(2,1)S(1)}, bf16[256,256]{1,0:T(8,128)(2,1)S(1)}, u32[]{:S(2)}, u32[]{:S(2)}) collective-permute-start(bf16[256,256]{1,0:T(8,128)(2,1)S(1)} %get-tuple-element.56), channel_id=1, source_target_pairs={{0,1},{1,0},{2,3},{3,2},{4,5},{5,4},{6,7},{7,6},{8,9},{9,8},{10,11... | collective-permute-start | bytes 393224 | tf_op jit(solution)/shard_map/ppermute | solution.py:34
  99.6 1.7 %collective-permute-start.12 = (bf16[256,256]{1,0:T(8,128)(2,1)S(1)}, bf16[256,256]{1,0:T(8,128)(2,1)S(1)}, u32[]{:S(2)}, u32[]{:S(2)}) collective-permute-start(bf16[256,256]{1,0:T(8,128)(2,1)S(1)} %get-tuple-element.50), channel_id=1, source_target_pairs={{0,1},{1,0},{2,3},{3,2},{4,5},{5,4},{6,7},{7,6},{8,9},{9,8},{10,11... | collective-permute-start | bytes 393224 | tf_op jit(solution)/shard_map/ppermute | solution.py:34
  101.3 2.6 %collective-permute-done.17.refs_1_ = bf16[256,256]{1,0:T(8,128)(2,1)S(1)} collective-permute-done((bf16[256,256]{1,0:T(8,128)(2,1)S(1)}, bf16[256,256]{1,0:T(8,128)(2,1)S(1)}, u32[]{:S(2)}, u32[]{:S(2)}) %collective-permute-start.17) | collective-permute-done | bytes 131104 | tf_op jit(solution)/shard_map/ppermute | solution.py:34
  105.3 3.0 %collective-permute-done.14 = bf16[512,256]{1,0:T(8,128)(2,1)S(1)} collective-permute-done((bf16[512,256]{1,0:T(8,128)(2,1)S(1)}, bf16[512,256]{1,0:T(8,128)(2,1)S(1)}, u32[]{:S(2)}, u32[]{:S(2)}) %collective-permute-start.14) | collective-permute-done | bytes 262176 | tf_op jit(solution)/shard_map/ppermute | solution.py:30
  108.4 8.1 %collective-permute-start.16 = (bf16[256,256]{1,0:T(8,128)(2,1)S(1)}, bf16[256,256]{1,0:T(8,128)(2,1)S(1)}, u32[]{:S(2)}, u32[]{:S(2)}) collective-permute-start(bf16[256,256]{1,0:T(8,128)(2,1)S(1)} %merge.4), channel_id=1, source_target_pairs={{4,0},{5,1},{6,2},{7,3},{8,4},{9,5},{10,6},{11,7},{12,8},{13,9},{1... | collective-permute-start | bytes 393224 | tf_op jit(solution)/shard_map/ppermute | solution.py:30
  116.5 2.5 %collective-permute-done.16 = bf16[256,256]{1,0:T(8,128)(2,1)S(1)} collective-permute-done((bf16[256,256]{1,0:T(8,128)(2,1)S(1)}, bf16[256,256]{1,0:T(8,128)(2,1)S(1)}, u32[]{:S(2)}, u32[]{:S(2)}) %collective-permute-start.16) | collective-permute-done | bytes 131104 | tf_op jit(solution)/shard_map/ppermute | solution.py:30
  119.1 1.5 collective-permute-start.19
  120.6 2.4 %collective-permute-start.20 = (bf16[256,256]{1,0:T(8,128)(2,1)S(1)}, bf16[256,256]{1,0:T(8,128)(2,1)S(1)}, u32[]{:S(2)}, u32[]{:S(2)}) collective-permute-start(bf16[256,256]{1,0:T(8,128)(2,1)S(1)} %fusion.35), channel_id=1, source_target_pairs={{0,64},{64,128},{128,192},{192,0},{1,65},{65,129},{129,193},{193,1... | collective-permute-start | bytes 393224 | tf_op jit(solution)/shard_map/ppermute | solution.py:39
  123.0 3.6 %collective-permute-start.21 = (bf16[256,256]{1,0:T(8,128)(2,1)S(1)}, bf16[256,256]{1,0:T(8,128)(2,1)S(1)}, u32[]{:S(2)}, u32[]{:S(2)}) collective-permute-start(bf16[256,256]{1,0:T(8,128)(2,1)S(1)} %fusion.35), channel_id=1, source_target_pairs={{0,128},{64,192},{128,0},{192,64},{1,129},{65,193},{129,1},{193,65... | collective-permute-start | bytes 393224 | tf_op jit(solution)/shard_map/ppermute | solution.py:39
  126.6 1.9 %collective-permute-start.22 = (bf16[256,256]{1,0:T(8,128)(2,1)S(1)}, bf16[256,256]{1,0:T(8,128)(2,1)S(1)}, u32[]{:S(2)}, u32[]{:S(2)}) collective-permute-start(bf16[256,256]{1,0:T(8,128)(2,1)S(1)} %fusion.35), channel_id=1, source_target_pairs={{0,192},{64,0},{128,64},{192,128},{1,193},{65,1},{129,65},{193,129... | collective-permute-start | bytes 393224 | tf_op jit(solution)/shard_map/ppermute | solution.py:39
  128.5 2.4 %collective-permute-done.21 = bf16[256,256]{1,0:T(8,128)(2,1)S(1)} collective-permute-done((bf16[256,256]{1,0:T(8,128)(2,1)S(1)}, bf16[256,256]{1,0:T(8,128)(2,1)S(1)}, u32[]{:S(2)}, u32[]{:S(2)}) %collective-permute-start.21) | collective-permute-done | bytes 131104 | tf_op jit(solution)/shard_map/ppermute | solution.py:39
  131.6 2.1 %fusion.11 = f32[1024,256]{1,0:T(8,128)S(1)} fusion(bf16[256,1024]{1,0:T(8,128)(2,1)} %collective-permute-done.11, bf16[256,1024]{1,0:T(8,128)(2,1)} %collective-permute-done.10, bf16[256,1024]{1,0:T(8,128)(2,1)} %collective-permute-done.9, bf16[256,1024]{1,0:T(8,128)(2,1)S(1)} %copy-done.4, bf16[256,256]{1,0:T(8,128)(2,1)S(1)} %collective-permute-done.22, ...), kind=kOutput, calls=%fused_computation.13 | convolution fusion | flops 547618816 | bytes 3670016 | tf_op jit(solution)/shard_map/dot_general | solution.py:335
  133.8 1.7 %collective-permute-done.23 = bf16[16,32,256]{2,1,0:T(8,128)(2,1)} collective-permute-done((bf16[16,32,256]{2,1,0:T(8,128)(2,1)S(1)}, bf16[16,32,256]{2,1,0:T(8,128)(2,1)}, u32[]{:S(2)}, u32[]{:S(2)}) %collective-permute-start.23) | collective-permute-done | bytes 262176 | tf_op jit(solution)/shard_map/ppermute | solution.py:34
  135.5 1.7 %fusion.21 = bf16[16,32,256]{2,1,0:T(8,128)(2,1)} fusion(bf16[16,32,256]{2,1,0:T(8,128)(2,1)} %collective-permute-done.23, f32[16,2,32,256]{3,2,1,0:T(8,128)S(1)} %bitcast.52, s32[]{:T(128)S(6)} %select_n.229), kind=kLoop, calls=%fused_computation.27 | loop fusion | flops 393216 | bytes 1048580 | tf_op jit(solution)/shard_map/convert_element_type | solution.py:341
  137.2 10.0 %all-to-all-start = ((bf16[16,32,256]{2,1,0:T(8,128)(2,1)}), bf16[16,32,256]{2,1,0:T(8,128)(2,1)S(1)}, u32[]{:S(2)}, u32[]{:S(2)}) async-start(bf16[16,32,256]{2,1,0:T(8,128)(2,1)} %fusion.21), calls=%async_computation | async-start | bytes 524288 | tf_op jit(solution)/shard_map/all_to_all | solution.py:342
  148.1 1.7 %convolution_convert_fusion = bf16[256,2048]{1,0:T(8,128)(2,1)} fusion(bf16[2048,256]{1,0:T(8,128)(2,1)S(1)} %get-tuple-element.32, bf16[2048,256]{1,0:T(8,128)(2,1)S(1)} %get-tuple-element.31, bf16[256,256]{1,0:T(8,128)(2,1)S(1)} %copy-done.6, bf16[256,256]{1,0:T(8,128)(2,1)S(1)} %fusion.35), kind=kOutput, calls=%fused_computation | convolution fusion | flops 542113792 | bytes 3407872 | tf_op jit(solution)/shard_map/dot_general | solution.py:326
  149.8 9.2 %all-to-all-done = bf16[16,32,256]{2,1,0:T(8,128)(2,1)S(1)} async-done(((bf16[16,32,256]{2,1,0:T(8,128)(2,1)}), bf16[16,32,256]{2,1,0:T(8,128)(2,1)S(1)}, u32[]{:S(2)}, u32[]{:S(2)}) %all-to-all-start) | async-done | bytes 262176 | tf_op jit(solution)/shard_map/all_to_all | solution.py:342
  (65 shorter events, 17.4 us)
Async XLA Ops:
  1.8 36.5 %copy-start = (bf16[256,512]{1,0:T(8,128)(2,1)S(1)}, bf16[256,512]{1,0:T(8,128)(2,1)}, u32[]{:S(2)}) copy-start(bf16[256,512]{1,0:T(8,128)(2,1)} %own_ref.1) | copy-start | bytes 786436
  1.8 11.3 %collective-permute-start = (bf16[256,256]{1,0:T(8,128)(2,1)S(1)}, bf16[256,256]{1,0:T(8,128)(2,1)S(1)}, u32[]{:S(2)}, u32[]{:S(2)}) collective-permute-start(bf16[256,256]{1,0:T(8,128)(2,1)S(1)} %get-tuple-element.65), channel_id=1, source_target_pairs={{0,4},{1,5},{2,6},{3,7},{4,8},{5,9},{6,10},{7,11},{8,12},{9,13},{1... | collective-permute-start | bytes 393224 | tf_op jit(solution)/shard_map/ppermute | solution.py:30
  5.8 12.8 %collective-permute-start.1 = (bf16[256,256]{1,0:T(8,128)(2,1)S(1)}, bf16[256,256]{1,0:T(8,128)(2,1)S(1)}, u32[]{:S(2)}, u32[]{:S(2)}) collective-permute-start(bf16[256,256]{1,0:T(8,128)(2,1)S(1)} %get-tuple-element.64), channel_id=1, source_target_pairs={{0,16},{1,17},{2,18},{3,19},{4,20},{5,21},{6,22},{7,23},{8,24},{9,... | collective-permute-start | bytes 393224 | tf_op jit(solution)/shard_map/ppermute | solution.py:30
  13.1 16.9 %collective-permute-start.2 = (bf16[512,256]{1,0:T(8,128)(2,1)S(1)}, bf16[512,256]{1,0:T(8,128)(2,1)S(1)}, u32[]{:S(2)}, u32[]{:S(2)}) collective-permute-start(bf16[512,256]{1,0:T(8,128)(2,1)S(1)} %pad_maximum_fusion.1), channel_id=1, source_target_pairs={{0,8},{1,9},{2,10},{3,11},{4,12},{5,13},{6,14},{7,15},{8,16},{9,17... | collective-permute-start | bytes 786440 | tf_op jit(solution)/shard_map/ppermute | solution.py:30
  17.0 6.1 %collective-permute-start.3 = (bf16[256,256]{1,0:T(8,128)(2,1)S(1)}, bf16[256,256]{1,0:T(8,128)(2,1)S(1)}, u32[]{:S(2)}, u32[]{:S(2)}) collective-permute-start(bf16[256,256]{1,0:T(8,128)(2,1)S(1)} %collective-permute-done.mine1), channel_id=1, source_target_pairs={{0,1},{1,0},{2,3},{3,2},{4,5},{5,4},{6,7},{7,6},{8,9},{9,8},{10,11... | collective-permute-start | bytes 393224 | tf_op jit(solution)/shard_map/ppermute | solution.py:34
  18.6 12.9 %collective-permute-start.4 = (bf16[256,256]{1,0:T(8,128)(2,1)S(1)}, bf16[256,256]{1,0:T(8,128)(2,1)S(1)}, u32[]{:S(2)}, u32[]{:S(2)}) collective-permute-start(bf16[256,256]{1,0:T(8,128)(2,1)S(1)} %collective-permute-done.1.mine4), channel_id=1, source_target_pairs={{0,1},{1,0},{2,3},{3,2},{4,5},{5,4},{6,7},{7,6},{8,9},{9,8},{10,11... | collective-permute-start | bytes 393224 | tf_op jit(solution)/shard_map/ppermute | solution.py:34
  30.0 8.1 %collective-permute-start.5 = (bf16[512,256]{1,0:T(8,128)(2,1)S(1)}, bf16[512,256]{1,0:T(8,128)(2,1)S(1)}, u32[]{:S(2)}, u32[]{:S(2)}) collective-permute-start(bf16[512,256]{1,0:T(8,128)(2,1)S(1)} %collective-permute-done.2.mine23), channel_id=1, source_target_pairs={{0,1},{1,0},{2,3},{3,2},{4,5},{5,4},{6,7},{7,6},{8,9},{9,8},{10,11... | collective-permute-start | bytes 786440 | tf_op jit(solution)/shard_map/ppermute | solution.py:34
  31.7 9.8 %copy-start.1 = (bf16[256,1024]{1,0:T(8,128)(2,1)S(1)}, bf16[256,1024]{1,0:T(8,128)(2,1)}, u32[]{:S(2)}) copy-start(bf16[256,1024]{1,0:T(8,128)(2,1)} %query_ref.1) | copy-start | bytes 1572868
  31.7 9.7 %copy-start.2 = (bf16[256,1024]{1,0:T(8,128)(2,1)S(1)}, bf16[256,1024]{1,0:T(8,128)(2,1)}, u32[]{:S(2)}) copy-start(bf16[256,1024]{1,0:T(8,128)(2,1)} %out_ref.1) | copy-start | bytes 1572868
  38.7 2.0 %collective-permute-start.6 = (bf16[512,512]{1,0:T(8,128)(2,1)S(1)}, bf16[512,512]{1,0:T(8,128)(2,1)S(1)}, u32[]{:S(2)}, u32[]{:S(2)}) collective-permute-start(bf16[512,512]{1,0:T(8,128)(2,1)S(1)} %get-tuple-element.58), channel_id=1, source_target_pairs={{0,2},{2,0},{1,3},{3,1},{4,6},{6,4},{5,7},{7,5},{8,10},{10,8},{9,1... | collective-permute-start | bytes 1572872 | tf_op jit(solution)/shard_map/ppermute | solution.py:34
  38.8 2.6 %collective-permute-start.7 = (bf16[512,512]{1,0:T(8,128)(2,1)S(1)}, bf16[512,512]{1,0:T(8,128)(2,1)S(1)}, u32[]{:S(2)}, u32[]{:S(2)}) collective-permute-start(bf16[512,512]{1,0:T(8,128)(2,1)S(1)} %get-tuple-element.57), channel_id=1, source_target_pairs={{0,2},{2,0},{1,3},{3,1},{4,6},{6,4},{5,7},{7,5},{8,10},{10,8},{9,1... | collective-permute-start | bytes 1572872 | tf_op jit(solution)/shard_map/ppermute | solution.py:34
  53.6 32.6 %collective-permute-start.8 = (bf16[1024,512]{1,0:T(8,128)(2,1)S(1)}, bf16[1024,512]{1,0:T(8,128)(2,1)}, u32[]{:S(2)}, u32[]{:S(2)}) collective-permute-start(bf16[1024,512]{1,0:T(8,128)(2,1)S(1)} %bitcast.50), channel_id=1, source_target_pairs={{0,2},{2,0},{1,3},{3,1},{4,6},{6,4},{5,7},{7,5},{8,10},{10,8},{9,1... | collective-permute-start | bytes 3145736 | tf_op jit(solution)/shard_map/ppermute | solution.py:34
  56.4 18.5 %collective-permute-start.10 = (bf16[256,1024]{1,0:T(8,128)(2,1)}, bf16[256,1024]{1,0:T(8,128)(2,1)}, u32[]{:S(2)}, u32[]{:S(2)}) collective-permute-start(bf16[256,1024]{1,0:T(8,128)(2,1)} %get-tuple-element.30), channel_id=1, source_target_pairs={{0,128},{64,192},{128,0},{192,64},{1,129},{65,193},{129,1},{193,65... | collective-permute-start | bytes 1572872 | tf_op jit(solution)/shard_map/ppermute | solution.py:39
  61.8 24.3 %collective-permute-start.11 = (bf16[256,1024]{1,0:T(8,128)(2,1)}, bf16[256,1024]{1,0:T(8,128)(2,1)}, u32[]{:S(2)}, u32[]{:S(2)}) collective-permute-start(bf16[256,1024]{1,0:T(8,128)(2,1)} %get-tuple-element.27), channel_id=1, source_target_pairs={{0,192},{64,0},{128,64},{192,128},{1,193},{65,1},{129,65},{193,129... | collective-permute-start | bytes 1572872 | tf_op jit(solution)/shard_map/ppermute | solution.py:39
  62.9 23.3 %collective-permute-start.9 = (bf16[256,1024]{1,0:T(8,128)(2,1)S(1)}, bf16[256,1024]{1,0:T(8,128)(2,1)}, u32[]{:S(2)}, u32[]{:S(2)}) collective-permute-start(bf16[256,1024]{1,0:T(8,128)(2,1)S(1)} %get-tuple-element.28), channel_id=1, source_target_pairs={{0,64},{64,128},{128,192},{192,0},{1,65},{65,129},{129,193},{193,1... | collective-permute-start | bytes 1572872 | tf_op jit(solution)/shard_map/ppermute | solution.py:39
  87.9 8.0 %collective-permute-start.13 = (bf16[512,256]{1,0:T(8,128)(2,1)S(1)}, bf16[512,256]{1,0:T(8,128)(2,1)S(1)}, u32[]{:S(2)}, u32[]{:S(2)}) collective-permute-start(bf16[512,256]{1,0:T(8,128)(2,1)S(1)} %pad_maximum_fusion.2), channel_id=1, source_target_pairs={{0,1},{1,0},{2,3},{3,2},{4,5},{5,4},{6,7},{7,6},{8,9},{9,8},{10,11... | collective-permute-start | bytes 786440 | tf_op jit(solution)/shard_map/ppermute | solution.py:34
  89.7 41.9 %copy-start.4 = (bf16[256,1024]{1,0:T(8,128)(2,1)S(1)}, bf16[256,1024]{1,0:T(8,128)(2,1)}, u32[]{:S(2)}) copy-start(bf16[256,1024]{1,0:T(8,128)(2,1)} %get-tuple-element.20) | copy-start | bytes 1572868
  96.0 12.3 %collective-permute-start.14 = (bf16[512,256]{1,0:T(8,128)(2,1)S(1)}, bf16[512,256]{1,0:T(8,128)(2,1)S(1)}, u32[]{:S(2)}, u32[]{:S(2)}) collective-permute-start(bf16[512,256]{1,0:T(8,128)(2,1)S(1)} %merge.3), channel_id=1, source_target_pairs={{8,0},{9,1},{10,2},{11,3},{12,4},{13,5},{14,6},{15,7},{16,8},{17,9... | collective-permute-start | bytes 786440 | tf_op jit(solution)/shard_map/ppermute | solution.py:30
  97.3 6.6 %collective-permute-start.17 = (bf16[256,256]{1,0:T(8,128)(2,1)S(1)}, bf16[256,256]{1,0:T(8,128)(2,1)S(1)}, u32[]{:S(2)}, u32[]{:S(2)}) collective-permute-start(bf16[256,256]{1,0:T(8,128)(2,1)S(1)} %get-tuple-element.56), channel_id=1, source_target_pairs={{0,1},{1,0},{2,3},{3,2},{4,5},{5,4},{6,7},{7,6},{8,9},{9,8},{10,11... | collective-permute-start | bytes 393224 | tf_op jit(solution)/shard_map/ppermute | solution.py:34
  99.3 9.0 %collective-permute-start.15 = (bf16[256,256]{1,0:T(8,128)(2,1)S(1)}, bf16[256,256]{1,0:T(8,128)(2,1)S(1)}, u32[]{:S(2)}, u32[]{:S(2)}) collective-permute-start(bf16[256,256]{1,0:T(8,128)(2,1)S(1)} %get-tuple-element.46), channel_id=1, source_target_pairs={{0,1},{1,0},{2,3},{3,2},{4,5},{5,4},{6,7},{7,6},{8,9},{9,8},{10,11... | collective-permute-start | bytes 393224 | tf_op jit(solution)/shard_map/ppermute | solution.py:34
  99.6 16.9 %collective-permute-start.12 = (bf16[256,256]{1,0:T(8,128)(2,1)S(1)}, bf16[256,256]{1,0:T(8,128)(2,1)S(1)}, u32[]{:S(2)}, u32[]{:S(2)}) collective-permute-start(bf16[256,256]{1,0:T(8,128)(2,1)S(1)} %get-tuple-element.50), channel_id=1, source_target_pairs={{0,1},{1,0},{2,3},{3,2},{4,5},{5,4},{6,7},{7,6},{8,9},{9,8},{10,11... | collective-permute-start | bytes 393224 | tf_op jit(solution)/shard_map/ppermute | solution.py:34
  104.0 12.5 %collective-permute-start.18 = (bf16[256,256]{1,0:T(8,128)(2,1)S(1)}, bf16[256,256]{1,0:T(8,128)(2,1)S(1)}, u32[]{:S(2)}, u32[]{:S(2)}) collective-permute-start(bf16[256,256]{1,0:T(8,128)(2,1)S(1)} %merge.5), channel_id=1, source_target_pairs={{16,0},{17,1},{18,2},{19,3},{20,4},{21,5},{22,6},{23,7},{24,8},{25... | collective-permute-start | bytes 393224 | tf_op jit(solution)/shard_map/ppermute | solution.py:30
  108.4 10.6 %collective-permute-start.16 = (bf16[256,256]{1,0:T(8,128)(2,1)S(1)}, bf16[256,256]{1,0:T(8,128)(2,1)S(1)}, u32[]{:S(2)}, u32[]{:S(2)}) collective-permute-start(bf16[256,256]{1,0:T(8,128)(2,1)S(1)} %merge.4), channel_id=1, source_target_pairs={{4,0},{5,1},{6,2},{7,3},{8,4},{9,5},{10,6},{11,7},{12,8},{13,9},{1... | collective-permute-start | bytes 393224 | tf_op jit(solution)/shard_map/ppermute | solution.py:30
  119.1 9.4 %collective-permute-start.19 = (bf16[256,256]{1,0:T(8,128)(2,1)S(1)}, bf16[256,256]{1,0:T(8,128)(2,1)S(1)}, u32[]{:S(2)}, u32[]{:S(2)}) collective-permute-start(bf16[256,256]{1,0:T(8,128)(2,1)S(1)} %fusion.35), channel_id=1, source_target_pairs={{0,1},{1,0},{2,3},{3,2},{4,5},{5,4},{6,7},{7,6},{8,9},{9,8},{10,11... | collective-permute-start | bytes 393224 | tf_op jit(solution)/shard_map/ppermute | solution.py:34
  120.6 8.0 %collective-permute-start.20 = (bf16[256,256]{1,0:T(8,128)(2,1)S(1)}, bf16[256,256]{1,0:T(8,128)(2,1)S(1)}, u32[]{:S(2)}, u32[]{:S(2)}) collective-permute-start(bf16[256,256]{1,0:T(8,128)(2,1)S(1)} %fusion.35), channel_id=1, source_target_pairs={{0,64},{64,128},{128,192},{192,0},{1,65},{65,129},{129,193},{193,1... | collective-permute-start | bytes 393224 | tf_op jit(solution)/shard_map/ppermute | solution.py:39
  123.0 8.0 %collective-permute-start.21 = (bf16[256,256]{1,0:T(8,128)(2,1)S(1)}, bf16[256,256]{1,0:T(8,128)(2,1)S(1)}, u32[]{:S(2)}, u32[]{:S(2)}) collective-permute-start(bf16[256,256]{1,0:T(8,128)(2,1)S(1)} %fusion.35), channel_id=1, source_target_pairs={{0,128},{64,192},{128,0},{192,64},{1,129},{65,193},{129,1},{193,65... | collective-permute-start | bytes 393224 | tf_op jit(solution)/shard_map/ppermute | solution.py:39
  126.6 5.0 %collective-permute-start.22 = (bf16[256,256]{1,0:T(8,128)(2,1)S(1)}, bf16[256,256]{1,0:T(8,128)(2,1)S(1)}, u32[]{:S(2)}, u32[]{:S(2)}) collective-permute-start(bf16[256,256]{1,0:T(8,128)(2,1)S(1)} %fusion.35), channel_id=1, source_target_pairs={{0,192},{64,0},{128,64},{192,128},{1,193},{65,1},{129,65},{193,129... | collective-permute-start | bytes 393224 | tf_op jit(solution)/shard_map/ppermute | solution.py:39
  128.4 3.1 %copy-start.5 = (bf16[256,256]{1,0:T(8,128)(2,1)}, bf16[256,256]{1,0:T(8,128)(2,1)S(1)}, u32[]{:S(2)}) copy-start(bf16[256,256]{1,0:T(8,128)(2,1)S(1)} %collective-permute-done.19) | copy-start | bytes 393220
  133.7 13.6 %copy-start.3 = (bf16[2,2048,256]{2,1,0:T(8,128)(2,1)S(1)}, bf16[2,2048,256]{2,1,0:T(8,128)(2,1)}, u32[]{:S(2)}) copy-start(bf16[2,2048,256]{2,1,0:T(8,128)(2,1)} %param.10) | copy-start | bytes 6291460
  133.7 1.8 %collective-permute-start.23 = (bf16[16,32,256]{2,1,0:T(8,128)(2,1)S(1)}, bf16[16,32,256]{2,1,0:T(8,128)(2,1)}, u32[]{:S(2)}, u32[]{:S(2)}) collective-permute-start(bf16[16,32,256]{2,1,0:T(8,128)(2,1)S(1)} %fusion.22), channel_id=1, source_target_pairs={{0,2},{2,0},{1,3},{3,1},{4,6},{6,4},{5,7},{7,5},{8,10},{10,8},{9,1... | collective-permute-start | bytes 786440 | tf_op jit(solution)/shard_map/ppermute | solution.py:34
  137.2 21.9 %all-to-all-start = ((bf16[16,32,256]{2,1,0:T(8,128)(2,1)}), bf16[16,32,256]{2,1,0:T(8,128)(2,1)S(1)}, u32[]{:S(2)}, u32[]{:S(2)}) async-start(bf16[16,32,256]{2,1,0:T(8,128)(2,1)} %fusion.21), calls=%async_computation | async-start | bytes 524288 | tf_op jit(solution)/shard_map/all_to_all | solution.py:342
  147.2 0.9 copy-start.6

commit v3 on v0

--- a/solution.py
+++ b/solution.py
@@ -108,7 +108,7 @@
     def first(block, carry, diagonal):
         top, mass, delta = carry
         row = lax.broadcasted_iota(jnp.int32, (tok, wide), 0)
-        ok = row + block * tok >= low
+        ok = row >= low - block * tok
         if diagonal:
             column = lax.broadcasted_iota(jnp.int32, (tok, wide), 1)
             ok = ok & (row <= (column & (tok - 1)))
@@ -213,6 +213,25 @@
     )(one, two)
 
 
+def core_merge_kernel(core_ref, own_ref, arrived_ref, sum_ref):
+    total = own_ref[:, core_ref[0]] + arrived_ref[...].astype(F32)
+    sum_ref[...] = total.astype(BF)
+
+
+def core_merged(core, own, arrived):
+    vmem = pl.BlockSpec(memory_space=pltpu.VMEM)
+    size = arrived.size
+    return pl.pallas_call(
+        core_merge_kernel,
+        out_shape=jax.ShapeDtypeStruct(arrived.shape, BF),
+        in_specs=[pl.BlockSpec(memory_space=pltpu.SMEM), vmem, vmem],
+        out_specs=vmem,
+        compiler_params=pltpu.CompilerParams(vmem_limit_bytes=8 * 1024 * 1024),
+        cost_estimate=pl.CostEstimate(flops=size, transcendentals=0, bytes_accessed=size * 8),
+        name="core_merge",
+    )(core.reshape(1).astype(jnp.int32), own, arrived)
+
+
 def local(query, key_value, out_grad, inputs_normed, kv_weight, segment_ids):
     tok = query.shape[0]
     hd = key_value.shape[1] // 2
@@ -225,7 +244,7 @@
         return columns(key_value, l ^ turn, hd)
 
     mine, other = {}, {}
-    for d in (4, 1, 2, 3):
+    for d in (3, 4, 2, 1):
         mine[d] = moved(taken(d), d, True)
     for d in (1, 2, 3, 4):
         other[d] = swapped(mine[d], "l")
@@ -270,7 +289,6 @@
         far,
     )
     arrived = swapped(given.reshape(4 * tok, 2 * hd), "c")
-    arrived, x_parts = lax.optimization_barrier((arrived, x_parts))
     x_rows = jnp.concatenate(x_parts, axis=0)
 
     def core_sum(d, which):
@@ -314,9 +332,8 @@
         x_rows, rows, (((0,), (0,)), ((), ())), preferred_element_type=F32
     )
     weight_part = (weight_part * norm).reshape(16, 2, width // 32, hd)
-    kept = lax.dynamic_index_in_dim(weight_part, c, 1, keepdims=False)
     given = lax.dynamic_index_in_dim(weight_part, 1 - c, 1, keepdims=False)
-    total = (kept + swapped(given.astype(BF), "c").astype(F32)).astype(BF)
+    total = core_merged(c, weight_part, swapped(given.astype(BF), "c"))
     spread = lax.all_to_all(total, ("xh", "z"), split_axis=0, concat_axis=0, tiled=True)
     weight_grad = spread.astype(F32).sum(axis=0)
     return (query_grad, input_grad, weight_grad[None])

time: 161 us -> 143 us (0.89)
  waiting for transfers between devices: 69.4 us -> 41.9 us
  starting transfers between devices: 61 us -> 73.5 us
  local copies, waits for them, and re-layouts: 7.85 us -> 4.84 us
    ppermute x8, waiting for transfers between devices: 19.4 us -> 2.59 us  [moved(): return lax.ppermute(value, ALL, routes)]
    ppermute x6, waiting for transfers between devices: 27.2 us -> 12 us  [turned(): lax.ppermute(value, axis, [(i, (i + steps) % count) for i in range(count)])]
    ppermute x6, starting transfers between devices: 15.5 us -> 30.4 us  [turned(): lax.ppermute(value, axis, [(i, (i + steps) % count) for i in range(count)])]
    ppermute x14, waiting for transfers between devices: 13.5 us -> 17.4 us  [swapped(): return lax.ppermute(value, axis, [(0, 1), (1, 0)])]
    dynamic_slice x2, local copies, waits for them, and re-layouts: 3.97 us -> 1.71 us  [columns(): return lax.dynamic_slice_in_dim(value, which * width, width, 1)]
    all_to_all x1, starting transfers between devices: 8.5 us -> 6.43 us  [local(): lax.all_to_all(total, ('xh', 'z'), split_axis=0, concat_axis=0, tiled=True)]
    convert_element_type x1 -> x0, other arithmetic: 1.72 us -> none  [local(): total = (kept + swapped(given.astype(BF), 'c').astype(F32)).astype(BF)]
  transfers between devices with their start and end apart: 29 -> 29, of which waited for: 21 -> 18; matrix products, arithmetic and copies ran while one was open for 5% -> 4% of each run, Pallas kernels for 0% -> 0%
where the time goes in v3:
time: 143 us; the launch traced here: 142 us
  starting transfers between devices  73.5 us (51%)
  waiting for transfers between devices  41.9 us (29%)
  Pallas kernels  12.7 us (9%)
  local copies, waits for them, and re-layouts  4.84 us (3%)
  other arithmetic  4.16 us (3%)
  matrix products  3.82 us (3%)
    ppermute x6, starting transfers between devices, turned(): lax.ppermute(value, axis, [(i, (i + steps) % count) for i in range(count)])  30.4 us
    ppermute x8, starting transfers between devices, moved(): return lax.ppermute(value, ALL, routes)  25.5 us
    ppermute x14, waiting for transfers between devices, swapped(): return lax.ppermute(value, axis, [(0, 1), (1, 0)])  17.4 us
    ppermute x6, waiting for transfers between devices, turned(): lax.ppermute(value, axis, [(i, (i + steps) % count) for i in range(count)])  12 us
    pallas_call x1, Pallas kernels, attention(): pl.pallas_call(attention_kernel, out_shape=(jax.ShapeDtypeStruct((tok, wi...  11.9 us
    ppermute x14, starting transfers between devices, swapped(): return lax.ppermute(value, axis, [(0, 1), (1, 0)])  11.2 us
    all_to_all x1, waiting for transfers between devices, local(): lax.all_to_all(total, ('xh', 'z'), split_axis=0, concat_axis=0, tiled=True)  9.99 us
    all_to_all x1, starting transfers between devices, local(): lax.all_to_all(total, ('xh', 'z'), split_axis=0, concat_axis=0, tiled=True)  6.43 us
  transfers between devices with their start and end apart: 29, of which 18 were waited for; matrix products, arithmetic and copies ran while one was open for 4% of the time, Pallas kernels for 0%

profile of v3, /device:TPU:32, one launch (start us, length us, event | category | flops | bytes accessed | tf_op | source)
XLA Modules:
  0.0 141.9 jit_solution(13359582880183145605)
XLA Ops:
  0.7 1.5 %constant_dynamic-slice_fusion.4 = (bf16[256,256]{1,0:T(8,128)(2,1)S(1)}, bf16[256,256]{1,0:T(8,128)(2,1)S(1)}, bf16[256,256]{1,0:T(8,128)(2,1)S(1)}, bf16[256,256]{1,0:T(8,128)(2,1)S(1)}) fusion(bf16[256,512]{1,0:T(8,128)(2,1)} %own_ref.1, s32[]{:T(128)S(6)} %select_n.183, s32[]{:T(128)S(6)} %select_n.182, s32[]{:T(128)S(6)} %select_n.181, s32[]{:T(128)S(6)} %select_n.180), kind=kLoop, calls=%fused_computation.61 | loop fusion | bytes 1048592 | tf_op jit(solution)/shard_map/dynamic_slice | solution.py:43
  2.2 3.8 %collective-permute-start = (bf16[256,256]{1,0:T(8,128)(2,1)S(1)}, bf16[256,256]{1,0:T(8,128)(2,1)S(1)}, u32[]{:S(2)}, u32[]{:S(2)}) collective-permute-start(bf16[256,256]{1,0:T(8,128)(2,1)S(1)} %get-tuple-element.52), channel_id=1, source_target_pairs={{0,4},{1,5},{2,6},{3,7},{4,8},{5,9},{6,10},{7,11},{8,12},{9,13},{1... | collective-permute-start | bytes 393224 | tf_op jit(solution)/shard_map/ppermute | solution.py:30
  6.0 6.2 %collective-permute-start.1 = (bf16[256,256]{1,0:T(8,128)(2,1)S(1)}, bf16[256,256]{1,0:T(8,128)(2,1)S(1)}, u32[]{:S(2)}, u32[]{:S(2)}) collective-permute-start(bf16[256,256]{1,0:T(8,128)(2,1)S(1)} %get-tuple-element.51), channel_id=1, source_target_pairs={{0,8},{1,9},{2,10},{3,11},{4,12},{5,13},{6,14},{7,15},{8,16},{9,17... | collective-permute-start | bytes 393224 | tf_op jit(solution)/shard_map/ppermute | solution.py:30
  12.2 3.9 %collective-permute-start.2 = (bf16[256,256]{1,0:T(8,128)(2,1)S(1)}, bf16[256,256]{1,0:T(8,128)(2,1)S(1)}, u32[]{:S(2)}, u32[]{:S(2)}) collective-permute-start(bf16[256,256]{1,0:T(8,128)(2,1)S(1)} %get-tuple-element.50), channel_id=1, source_target_pairs={{0,12},{1,13},{2,14},{3,15},{4,16},{5,17},{6,18},{7,19},{8,20},{9,... | collective-permute-start | bytes 393224 | tf_op jit(solution)/shard_map/ppermute | solution.py:30
  16.1 5.5 %collective-permute-start.3 = (bf16[256,256]{1,0:T(8,128)(2,1)S(1)}, bf16[256,256]{1,0:T(8,128)(2,1)S(1)}, u32[]{:S(2)}, u32[]{:S(2)}) collective-permute-start(bf16[256,256]{1,0:T(8,128)(2,1)S(1)} %get-tuple-element.49), channel_id=1, source_target_pairs={{0,16},{1,17},{2,18},{3,19},{4,20},{5,21},{6,22},{7,23},{8,24},{9,... | collective-permute-start | bytes 393224 | tf_op jit(solution)/shard_map/ppermute | solution.py:30
  22.1 1.6 %collective-permute-start.5 = (bf16[256,256]{1,0:T(8,128)(2,1)S(1)}, bf16[256,256]{1,0:T(8,128)(2,1)S(1)}, u32[]{:S(2)}, u32[]{:S(2)}) collective-permute-start(bf16[256,256]{1,0:T(8,128)(2,1)S(1)} %collective-permute-done.1.m2), channel_id=1, source_target_pairs={{0,1},{1,0},{2,3},{3,2},{4,5},{5,4},{6,7},{7,6},{8,9},{9,8},{10,11... | collective-permute-start | bytes 393224 | tf_op jit(solution)/shard_map/ppermute | solution.py:34
  25.7 1.6 %collective-permute-start.7 = (bf16[256,256]{1,0:T(8,128)(2,1)S(1)}, bf16[256,256]{1,0:T(8,128)(2,1)S(1)}, u32[]{:S(2)}, u32[]{:S(2)}) collective-permute-start(bf16[256,256]{1,0:T(8,128)(2,1)S(1)} %collective-permute-done.3.m4), channel_id=1, source_target_pairs={{0,1},{1,0},{2,3},{3,2},{4,5},{5,4},{6,7},{7,6},{8,9},{9,8},{10,11... | collective-permute-start | bytes 393224 | tf_op jit(solution)/shard_map/ppermute | solution.py:34
  28.2 2.7 %collective-permute-done.5.o2 = bf16[256,256]{1,0:T(8,128)(2,1)S(1)} collective-permute-done((bf16[256,256]{1,0:T(8,128)(2,1)S(1)}, bf16[256,256]{1,0:T(8,128)(2,1)S(1)}, u32[]{:S(2)}, u32[]{:S(2)}) %collective-permute-start.5) | collective-permute-done | bytes 131104 | tf_op jit(solution)/shard_map/ppermute | solution.py:34
  31.0 1.8 %collective-permute-done.6.o3 = bf16[256,256]{1,0:T(8,128)(2,1)S(1)} collective-permute-done((bf16[256,256]{1,0:T(8,128)(2,1)S(1)}, bf16[256,256]{1,0:T(8,128)(2,1)S(1)}, u32[]{:S(2)}, u32[]{:S(2)}) %collective-permute-start.6) | collective-permute-done | bytes 131104 | tf_op jit(solution)/shard_map/ppermute | solution.py:34
  37.5 11.9 %attention.1 = (bf16[256,1024]{1,0:T(8,128)(2,1)}, bf16[4,256,512]{2,1,0:T(8,128)(2,1)S(1)}, bf16[5,256,512]{2,1,0:T(8,128)(2,1)S(1)}) custom-call(s32[1]{0:T(128)} %bitcast.side_ref, s32[1,1024]{1,0:T(1,128)S(1)} %bitcast.51, bf16[256,1024]{1,0:T(8,128)(2,1)S(1)} %copy-done.1, bf16[256,1024]{1,0:T(8,128)(2,1)S(1)} %copy-done.2, ...), custom_call_target="tpu_custom_call" | custom-call | flops 6039797760 | bytes 8388608 | tf_op jit(solution)/shard_map/attention/pallas_call | solution.py:172
  49.7 2.5 %collective-permute-done.10 = bf16[1024,512]{1,0:T(8,128)(2,1)} collective-permute-done((bf16[1024,512]{1,0:T(8,128)(2,1)S(1)}, bf16[1024,512]{1,0:T(8,128)(2,1)}, u32[]{:S(2)}, u32[]{:S(2)}) %collective-permute-start.10) | collective-permute-done | bytes 1048608 | tf_op jit(solution)/shard_map/ppermute | solution.py:34
  54.4 1.6 %collective-permute-start.14 = (bf16[256,256]{1,0:T(8,128)(2,1)S(1)}, bf16[256,256]{1,0:T(8,128)(2,1)S(1)}, u32[]{:S(2)}, u32[]{:S(2)}) collective-permute-start(bf16[256,256]{1,0:T(8,128)(2,1)S(1)} %get-tuple-element.42), channel_id=1, source_target_pairs={{0,1},{1,0},{2,3},{3,2},{4,5},{5,4},{6,7},{7,6},{8,9},{9,8},{10,11... | collective-permute-start | bytes 393224 | tf_op jit(solution)/shard_map/ppermute | solution.py:34
  56.5 1.6 %collective-permute-start.18 = (bf16[256,256]{1,0:T(8,128)(2,1)S(1)}, bf16[256,256]{1,0:T(8,128)(2,1)S(1)}, u32[]{:S(2)}, u32[]{:S(2)}) collective-permute-start(bf16[256,256]{1,0:T(8,128)(2,1)S(1)} %get-tuple-element.46), channel_id=1, source_target_pairs={{0,1},{1,0},{2,3},{3,2},{4,5},{5,4},{6,7},{7,6},{8,9},{9,8},{10,11... | collective-permute-start | bytes 393224 | tf_op jit(solution)/shard_map/ppermute | solution.py:34
  58.5 1.9 %collective-permute-done.12.two_ref = bf16[256,256]{1,0:T(8,128)(2,1)S(1)} collective-permute-done((bf16[256,256]{1,0:T(8,128)(2,1)S(1)}, bf16[256,256]{1,0:T(8,128)(2,1)S(1)}, u32[]{:S(2)}, u32[]{:S(2)}) %collective-permute-start.12) | collective-permute-done | bytes 131104 | tf_op jit(solution)/shard_map/ppermute | solution.py:34
  60.4 2.3 %collective-permute-start.13 = (bf16[256,256]{1,0:T(8,128)(2,1)S(1)}, bf16[256,256]{1,0:T(8,128)(2,1)S(1)}, u32[]{:S(2)}, u32[]{:S(2)}) collective-permute-start(bf16[256,256]{1,0:T(8,128)(2,1)S(1)} %merge.4), channel_id=1, source_target_pairs={{4,0},{5,1},{6,2},{7,3},{8,4},{9,5},{10,6},{11,7},{12,8},{13,9},{1... | collective-permute-start | bytes 393224 | tf_op jit(solution)/shard_map/ppermute | solution.py:30
  64.5 1.5 %collective-permute-done.16.two_ref = bf16[256,256]{1,0:T(8,128)(2,1)S(1)} collective-permute-done((bf16[256,256]{1,0:T(8,128)(2,1)S(1)}, bf16[256,256]{1,0:T(8,128)(2,1)S(1)}, u32[]{:S(2)}, u32[]{:S(2)}) %collective-permute-start.16) | collective-permute-done | bytes 131104 | tf_op jit(solution)/shard_map/ppermute | solution.py:34
  67.3 1.5 %collective-permute-done.18.two_ref = bf16[256,256]{1,0:T(8,128)(2,1)S(1)} collective-permute-done((bf16[256,256]{1,0:T(8,128)(2,1)S(1)}, bf16[256,256]{1,0:T(8,128)(2,1)S(1)}, u32[]{:S(2)}, u32[]{:S(2)}) %collective-permute-start.18) | collective-permute-done | bytes 131104 | tf_op jit(solution)/shard_map/ppermute | solution.py:34
  68.8 1.3 collective-permute-start.19
  70.8 15.2 %collective-permute-start.24 = (bf16[256,1024]{1,0:T(8,128)(2,1)S(1)}, bf16[256,1024]{1,0:T(8,128)(2,1)}, u32[]{:S(2)}, u32[]{:S(2)}) collective-permute-start(bf16[256,1024]{1,0:T(8,128)(2,1)S(1)} %get-tuple-element.18), channel_id=1, source_target_pairs={{0,64},{64,128},{128,192},{192,0},{1,65},{65,129},{129,193},{193,1... | collective-permute-start | bytes 1572872 | tf_op jit(solution)/shard_map/ppermute | solution.py:39
  86.0 3.2 %collective-permute-start.25 = (bf16[256,1024]{1,0:T(8,128)(2,1)S(1)}, bf16[256,1024]{1,0:T(8,128)(2,1)}, u32[]{:S(2)}, u32[]{:S(2)}) collective-permute-start(bf16[256,1024]{1,0:T(8,128)(2,1)S(1)} %get-tuple-element.20), channel_id=1, source_target_pairs={{0,128},{64,192},{128,0},{192,64},{1,129},{65,193},{129,1},{193,65... | collective-permute-start | bytes 1572872 | tf_op jit(solution)/shard_map/ppermute | solution.py:39
  90.2 2.6 %collective-permute-done.19 = bf16[256,256]{1,0:T(8,128)(2,1)} collective-permute-done((bf16[256,256]{1,0:T(8,128)(2,1)S(1)}, bf16[256,256]{1,0:T(8,128)(2,1)}, u32[]{:S(2)}, u32[]{:S(2)}) %collective-permute-start.19) | collective-permute-done | bytes 131104 | tf_op jit(solution)/shard_map/ppermute | solution.py:30
  93.9 1.6 %collective-permute-start.20 = (bf16[256,256]{1,0:T(8,128)(2,1)S(1)}, bf16[256,256]{1,0:T(8,128)(2,1)S(1)}, u32[]{:S(2)}, u32[]{:S(2)}) collective-permute-start(bf16[256,256]{1,0:T(8,128)(2,1)S(1)} %fusion.35), channel_id=1, source_target_pairs={{0,1},{1,0},{2,3},{3,2},{4,5},{5,4},{6,7},{7,6},{8,9},{9,8},{10,11... | collective-permute-start | bytes 393224 | tf_op jit(solution)/shard_map/ppermute | solution.py:34
  95.5 3.5 %collective-permute-start.21 = (bf16[256,256]{1,0:T(8,128)(2,1)S(1)}, bf16[256,256]{1,0:T(8,128)(2,1)S(1)}, u32[]{:S(2)}, u32[]{:S(2)}) collective-permute-start(bf16[256,256]{1,0:T(8,128)(2,1)S(1)} %fusion.35), channel_id=1, source_target_pairs={{0,64},{64,128},{128,192},{192,0},{1,65},{65,129},{129,193},{193,1... | collective-permute-start | bytes 393224 | tf_op jit(solution)/shard_map/ppermute | solution.py:39
  99.0 6.0 %collective-permute-start.22 = (bf16[256,256]{1,0:T(8,128)(2,1)S(1)}, bf16[256,256]{1,0:T(8,128)(2,1)S(1)}, u32[]{:S(2)}, u32[]{:S(2)}) collective-permute-start(bf16[256,256]{1,0:T(8,128)(2,1)S(1)} %fusion.35), channel_id=1, source_target_pairs={{0,128},{64,192},{128,0},{192,64},{1,129},{65,193},{129,1},{193,65... | collective-permute-start | bytes 393224 | tf_op jit(solution)/shard_map/ppermute | solution.py:39
  105.0 8.4 %collective-permute-done.21 = bf16[256,256]{1,0:T(8,128)(2,1)S(1)} collective-permute-done((bf16[256,256]{1,0:T(8,128)(2,1)S(1)}, bf16[256,256]{1,0:T(8,128)(2,1)S(1)}, u32[]{:S(2)}, u32[]{:S(2)}) %collective-permute-start.21) | collective-permute-done | bytes 131104 | tf_op jit(solution)/shard_map/ppermute | solution.py:39
  113.5 1.4 %collective-permute-start.23 = (bf16[256,256]{1,0:T(8,128)(2,1)S(1)}, bf16[256,256]{1,0:T(8,128)(2,1)S(1)}, u32[]{:S(2)}, u32[]{:S(2)}) collective-permute-start(bf16[256,256]{1,0:T(8,128)(2,1)S(1)} %fusion.35), channel_id=1, source_target_pairs={{0,192},{64,0},{128,64},{192,128},{1,193},{65,1},{129,65},{193,129... | collective-permute-start | bytes 393224 | tf_op jit(solution)/shard_map/ppermute | solution.py:39
  115.7 2.7 %collective-permute-done.23 = bf16[256,256]{1,0:T(8,128)(2,1)S(1)} collective-permute-done((bf16[256,256]{1,0:T(8,128)(2,1)S(1)}, bf16[256,256]{1,0:T(8,128)(2,1)S(1)}, u32[]{:S(2)}, u32[]{:S(2)}) %collective-permute-start.23) | collective-permute-done | bytes 131104 | tf_op jit(solution)/shard_map/ppermute | solution.py:39
  118.4 2.1 %fusion.11 = f32[1024,256]{1,0:T(8,128)S(1)} fusion(bf16[256,1024]{1,0:T(8,128)(2,1)} %collective-permute-done.26, bf16[256,1024]{1,0:T(8,128)(2,1)} %collective-permute-done.25, bf16[256,1024]{1,0:T(8,128)(2,1)} %collective-permute-done.24, bf16[256,1024]{1,0:T(8,128)(2,1)S(1)} %get-tuple-element.17, bf16[256,256]{1,0:T(8,128)(2,1)S(1)} %collective-permute-done.23, ...), kind=kOutput, calls=%fused_computation.13 | convolution fusion | flops 547618816 | bytes 3670016 | tf_op jit(solution)/shard_map/dot_general | solution.py:331
  120.7 1.5 %collective-permute-done.27.arrived_ref = bf16[16,32,256]{2,1,0:T(8,128)(2,1)S(1)} collective-permute-done((bf16[16,32,256]{2,1,0:T(8,128)(2,1)S(1)}, bf16[16,32,256]{2,1,0:T(8,128)(2,1)S(1)}, u32[]{:S(2)}, u32[]{:S(2)}) %collective-permute-start.27) | collective-permute-done | bytes 262176 | tf_op jit(solution)/shard_map/ppermute | solution.py:34
  123.0 6.4 %all-to-all-start = ((bf16[16,32,256]{2,1,0:T(8,128)(2,1)}), bf16[16,32,256]{2,1,0:T(8,128)(2,1)S(1)}, u32[]{:S(2)}, u32[]{:S(2)}) async-start(bf16[16,32,256]{2,1,0:T(8,128)(2,1)} %core_merge.1), calls=%async_computation | async-start | bytes 524288 | tf_op jit(solution)/shard_map/all_to_all | solution.py:337
  129.6 1.7 %convolution_convert_fusion = bf16[256,2048]{1,0:T(8,128)(2,1)} fusion(bf16[2048,256]{1,0:T(8,128)(2,1)S(1)} %get-tuple-element.22, bf16[2048,256]{1,0:T(8,128)(2,1)S(1)} %get-tuple-element.21, bf16[256,256]{1,0:T(8,128)(2,1)S(1)} %collective-permute-done.20, bf16[256,256]{1,0:T(8,128)(2,1)S(1)} %fusion.35), kind=kOutput, calls=%fused_computation | convolution fusion | flops 542113792 | bytes 3407872 | tf_op jit(solution)/shard_map/dot_general | solution.py:322
  131.3 10.0 %all-to-all-done = bf16[16,32,256]{2,1,0:T(8,128)(2,1)S(1)} async-done(((bf16[16,32,256]{2,1,0:T(8,128)(2,1)}), bf16[16,32,256]{2,1,0:T(8,128)(2,1)S(1)}, u32[]{:S(2)}, u32[]{:S(2)}) %all-to-all-start) | async-done | bytes 262176 | tf_op jit(solution)/shard_map/all_to_all | solution.py:337
  (64 shorter events, 20.0 us)
Async XLA Ops:
  0.6 33.7 %copy-start = (bf16[256,512]{1,0:T(8,128)(2,1)S(1)}, bf16[256,512]{1,0:T(8,128)(2,1)}, u32[]{:S(2)}) copy-start(bf16[256,512]{1,0:T(8,128)(2,1)} %own_ref.1) | copy-start | bytes 786436
  2.2 19.4 %collective-permute-start = (bf16[256,256]{1,0:T(8,128)(2,1)S(1)}, bf16[256,256]{1,0:T(8,128)(2,1)S(1)}, u32[]{:S(2)}, u32[]{:S(2)}) collective-permute-start(bf16[256,256]{1,0:T(8,128)(2,1)S(1)} %get-tuple-element.52), channel_id=1, source_target_pairs={{0,4},{1,5},{2,6},{3,7},{4,8},{5,9},{6,10},{7,11},{8,12},{9,13},{1... | collective-permute-start | bytes 393224 | tf_op jit(solution)/shard_map/ppermute | solution.py:30
  6.0 16.1 %collective-permute-start.1 = (bf16[256,256]{1,0:T(8,128)(2,1)S(1)}, bf16[256,256]{1,0:T(8,128)(2,1)S(1)}, u32[]{:S(2)}, u32[]{:S(2)}) collective-permute-start(bf16[256,256]{1,0:T(8,128)(2,1)S(1)} %get-tuple-element.51), channel_id=1, source_target_pairs={{0,8},{1,9},{2,10},{3,11},{4,12},{5,13},{6,14},{7,15},{8,16},{9,17... | collective-permute-start | bytes 393224 | tf_op jit(solution)/shard_map/ppermute | solution.py:30
  12.2 13.1 %collective-permute-start.2 = (bf16[256,256]{1,0:T(8,128)(2,1)S(1)}, bf16[256,256]{1,0:T(8,128)(2,1)S(1)}, u32[]{:S(2)}, u32[]{:S(2)}) collective-permute-start(bf16[256,256]{1,0:T(8,128)(2,1)S(1)} %get-tuple-element.50), channel_id=1, source_target_pairs={{0,12},{1,13},{2,14},{3,15},{4,16},{5,17},{6,18},{7,19},{8,20},{9,... | collective-permute-start | bytes 393224 | tf_op jit(solution)/shard_map/ppermute | solution.py:30
  16.1 9.7 %collective-permute-start.3 = (bf16[256,256]{1,0:T(8,128)(2,1)S(1)}, bf16[256,256]{1,0:T(8,128)(2,1)S(1)}, u32[]{:S(2)}, u32[]{:S(2)}) collective-permute-start(bf16[256,256]{1,0:T(8,128)(2,1)S(1)} %get-tuple-element.49), channel_id=1, source_target_pairs={{0,16},{1,17},{2,18},{3,19},{4,20},{5,21},{6,22},{7,23},{8,24},{9,... | collective-permute-start | bytes 393224 | tf_op jit(solution)/shard_map/ppermute | solution.py:30
  21.6 6.5 %collective-permute-start.4 = (bf16[256,256]{1,0:T(8,128)(2,1)S(1)}, bf16[256,256]{1,0:T(8,128)(2,1)S(1)}, u32[]{:S(2)}, u32[]{:S(2)}) collective-permute-start(bf16[256,256]{1,0:T(8,128)(2,1)S(1)} %collective-permute-done.m1), channel_id=1, source_target_pairs={{0,1},{1,0},{2,3},{3,2},{4,5},{5,4},{6,7},{7,6},{8,9},{9,8},{10,11... | collective-permute-start | bytes 393224 | tf_op jit(solution)/shard_map/ppermute | solution.py:34
  22.1 8.8 %collective-permute-start.5 = (bf16[256,256]{1,0:T(8,128)(2,1)S(1)}, bf16[256,256]{1,0:T(8,128)(2,1)S(1)}, u32[]{:S(2)}, u32[]{:S(2)}) collective-permute-start(bf16[256,256]{1,0:T(8,128)(2,1)S(1)} %collective-permute-done.1.m2), channel_id=1, source_target_pairs={{0,1},{1,0},{2,3},{3,2},{4,5},{5,4},{6,7},{7,6},{8,9},{9,8},{10,11... | collective-permute-start | bytes 393224 | tf_op jit(solution)/shard_map/ppermute | solution.py:34
  25.3 7.6 %collective-permute-start.6 = (bf16[256,256]{1,0:T(8,128)(2,1)S(1)}, bf16[256,256]{1,0:T(8,128)(2,1)S(1)}, u32[]{:S(2)}, u32[]{:S(2)}) collective-permute-start(bf16[256,256]{1,0:T(8,128)(2,1)S(1)} %collective-permute-done.2.m3), channel_id=1, source_target_pairs={{0,1},{1,0},{2,3},{3,2},{4,5},{5,4},{6,7},{7,6},{8,9},{9,8},{10,11... | collective-permute-start | bytes 393224 | tf_op jit(solution)/shard_map/ppermute | solution.py:34
  25.7 8.5 %collective-permute-start.7 = (bf16[256,256]{1,0:T(8,128)(2,1)S(1)}, bf16[256,256]{1,0:T(8,128)(2,1)S(1)}, u32[]{:S(2)}, u32[]{:S(2)}) collective-permute-start(bf16[256,256]{1,0:T(8,128)(2,1)S(1)} %collective-permute-done.3.m4), channel_id=1, source_target_pairs={{0,1},{1,0},{2,3},{3,2},{4,5},{5,4},{6,7},{7,6},{8,9},{9,8},{10,11... | collective-permute-start | bytes 393224 | tf_op jit(solution)/shard_map/ppermute | solution.py:34
  28.2 9.3 %copy-start.1 = (bf16[256,1024]{1,0:T(8,128)(2,1)S(1)}, bf16[256,1024]{1,0:T(8,128)(2,1)}, u32[]{:S(2)}) copy-start(bf16[256,1024]{1,0:T(8,128)(2,1)} %query_ref.1) | copy-start | bytes 1572868
  34.8 2.0 %collective-permute-start.8 = (bf16[512,512]{1,0:T(8,128)(2,1)S(1)}, bf16[512,512]{1,0:T(8,128)(2,1)S(1)}, u32[]{:S(2)}, u32[]{:S(2)}) collective-permute-start(bf16[512,512]{1,0:T(8,128)(2,1)S(1)} %get-tuple-element.48), channel_id=1, source_target_pairs={{0,2},{2,0},{1,3},{3,1},{4,6},{6,4},{5,7},{7,5},{8,10},{10,8},{9,1... | collective-permute-start | bytes 1572872 | tf_op jit(solution)/shard_map/ppermute | solution.py:34
  34.9 2.6 %collective-permute-start.9 = (bf16[512,512]{1,0:T(8,128)(2,1)S(1)}, bf16[512,512]{1,0:T(8,128)(2,1)S(1)}, u32[]{:S(2)}, u32[]{:S(2)}) collective-permute-start(bf16[512,512]{1,0:T(8,128)(2,1)S(1)} %get-tuple-element.47), channel_id=1, source_target_pairs={{0,2},{2,0},{1,3},{3,1},{4,6},{6,4},{5,7},{7,5},{8,10},{10,8},{9,1... | collective-permute-start | bytes 1572872 | tf_op jit(solution)/shard_map/ppermute | solution.py:34
  49.4 2.8 %collective-permute-start.10 = (bf16[1024,512]{1,0:T(8,128)(2,1)S(1)}, bf16[1024,512]{1,0:T(8,128)(2,1)}, u32[]{:S(2)}, u32[]{:S(2)}) collective-permute-start(bf16[1024,512]{1,0:T(8,128)(2,1)S(1)} %bitcast.52), channel_id=1, source_target_pairs={{0,2},{2,0},{1,3},{3,1},{4,6},{6,4},{5,7},{7,5},{8,10},{10,8},{9,1... | collective-permute-start | bytes 3145736 | tf_op jit(solution)/shard_map/ppermute | solution.py:34
  53.9 6.5 %collective-permute-start.12 = (bf16[256,256]{1,0:T(8,128)(2,1)S(1)}, bf16[256,256]{1,0:T(8,128)(2,1)S(1)}, u32[]{:S(2)}, u32[]{:S(2)}) collective-permute-start(bf16[256,256]{1,0:T(8,128)(2,1)S(1)} %get-tuple-element.32), channel_id=1, source_target_pairs={{0,1},{1,0},{2,3},{3,2},{4,5},{5,4},{6,7},{7,6},{8,9},{9,8},{10,11... | collective-permute-start | bytes 393224 | tf_op jit(solution)/shard_map/ppermute | solution.py:34
  54.4 8.7 %collective-permute-start.14 = (bf16[256,256]{1,0:T(8,128)(2,1)S(1)}, bf16[256,256]{1,0:T(8,128)(2,1)S(1)}, u32[]{:S(2)}, u32[]{:S(2)}) collective-permute-start(bf16[256,256]{1,0:T(8,128)(2,1)S(1)} %get-tuple-element.42), channel_id=1, source_target_pairs={{0,1},{1,0},{2,3},{3,2},{4,5},{5,4},{6,7},{7,6},{8,9},{9,8},{10,11... | collective-permute-start | bytes 393224 | tf_op jit(solution)/shard_map/ppermute | solution.py:34
  56.0 10.0 %collective-permute-start.16 = (bf16[256,256]{1,0:T(8,128)(2,1)S(1)}, bf16[256,256]{1,0:T(8,128)(2,1)S(1)}, u32[]{:S(2)}, u32[]{:S(2)}) collective-permute-start(bf16[256,256]{1,0:T(8,128)(2,1)S(1)} %get-tuple-element.44), channel_id=1, source_target_pairs={{0,1},{1,0},{2,3},{3,2},{4,5},{5,4},{6,7},{7,6},{8,9},{9,8},{10,11... | collective-permute-start | bytes 393224 | tf_op jit(solution)/shard_map/ppermute | solution.py:34
  56.5 12.3 %collective-permute-start.18 = (bf16[256,256]{1,0:T(8,128)(2,1)S(1)}, bf16[256,256]{1,0:T(8,128)(2,1)S(1)}, u32[]{:S(2)}, u32[]{:S(2)}) collective-permute-start(bf16[256,256]{1,0:T(8,128)(2,1)S(1)} %get-tuple-element.46), channel_id=1, source_target_pairs={{0,1},{1,0},{2,3},{3,2},{4,5},{5,4},{6,7},{7,6},{8,9},{9,8},{10,11... | collective-permute-start | bytes 393224 | tf_op jit(solution)/shard_map/ppermute | solution.py:34
  58.1 12.1 %copy-start.4 = (bf16[256,4096]{1,0:T(8,128)(2,1)S(1)}, bf16[256,4096]{1,0:T(8,128)(2,1)}, u32[]{:S(2)}) copy-start(bf16[256,4096]{1,0:T(8,128)(2,1)} %param.9) | copy-start | bytes 6291460
  58.1 12.7 %collective-permute-start.11 = (bf16[256,256]{1,0:T(8,128)(2,1)S(1)}, bf16[256,256]{1,0:T(8,128)(2,1)S(1)}, u32[]{:S(2)}, u32[]{:S(2)}) collective-permute-start(bf16[256,256]{1,0:T(8,128)(2,1)S(1)} %get-tuple-element.40), channel_id=1, source_target_pairs={{0,1},{1,0},{2,3},{3,2},{4,5},{5,4},{6,7},{7,6},{8,9},{9,8},{10,11... | collective-permute-start | bytes 393224 | tf_op jit(solution)/shard_map/ppermute | solution.py:34
  60.4 25.6 %collective-permute-start.13 = (bf16[256,256]{1,0:T(8,128)(2,1)S(1)}, bf16[256,256]{1,0:T(8,128)(2,1)S(1)}, u32[]{:S(2)}, u32[]{:S(2)}) collective-permute-start(bf16[256,256]{1,0:T(8,128)(2,1)S(1)} %merge.4), channel_id=1, source_target_pairs={{4,0},{5,1},{6,2},{7,3},{8,4},{9,5},{10,6},{11,7},{12,8},{13,9},{1... | collective-permute-start | bytes 393224 | tf_op jit(solution)/shard_map/ppermute | solution.py:30
  63.2 25.9 %collective-permute-start.15 = (bf16[256,256]{1,0:T(8,128)(2,1)S(1)}, bf16[256,256]{1,0:T(8,128)(2,1)S(1)}, u32[]{:S(2)}, u32[]{:S(2)}) collective-permute-start(bf16[256,256]{1,0:T(8,128)(2,1)S(1)} %merge.5), channel_id=1, source_target_pairs={{8,0},{9,1},{10,2},{11,3},{12,4},{13,5},{14,6},{15,7},{16,8},{17,9... | collective-permute-start | bytes 393224 | tf_op jit(solution)/shard_map/ppermute | solution.py:30
  66.0 24.2 %collective-permute-start.17 = (bf16[256,256]{1,0:T(8,128)(2,1)S(1)}, bf16[256,256]{1,0:T(8,128)(2,1)}, u32[]{:S(2)}, u32[]{:S(2)}) collective-permute-start(bf16[256,256]{1,0:T(8,128)(2,1)S(1)} %merge.6), channel_id=1, source_target_pairs={{12,0},{13,1},{14,2},{15,3},{16,4},{17,5},{18,6},{19,7},{20,8},{21... | collective-permute-start | bytes 393224 | tf_op jit(solution)/shard_map/ppermute | solution.py:30
  68.8 24.0 %collective-permute-start.19 = (bf16[256,256]{1,0:T(8,128)(2,1)S(1)}, bf16[256,256]{1,0:T(8,128)(2,1)}, u32[]{:S(2)}, u32[]{:S(2)}) collective-permute-start(bf16[256,256]{1,0:T(8,128)(2,1)S(1)} %merge.7), channel_id=1, source_target_pairs={{16,0},{17,1},{18,2},{19,3},{20,4},{21,5},{22,6},{23,7},{24,8},{25... | collective-permute-start | bytes 393224 | tf_op jit(solution)/shard_map/ppermute | solution.py:30
  70.8 47.6 %collective-permute-start.24 = (bf16[256,1024]{1,0:T(8,128)(2,1)S(1)}, bf16[256,1024]{1,0:T(8,128)(2,1)}, u32[]{:S(2)}, u32[]{:S(2)}) collective-permute-start(bf16[256,1024]{1,0:T(8,128)(2,1)S(1)} %get-tuple-element.18), channel_id=1, source_target_pairs={{0,64},{64,128},{128,192},{192,0},{1,65},{65,129},{129,193},{193,1... | collective-permute-start | bytes 1572872 | tf_op jit(solution)/shard_map/ppermute | solution.py:39
  86.0 32.5 %collective-permute-start.25 = (bf16[256,1024]{1,0:T(8,128)(2,1)S(1)}, bf16[256,1024]{1,0:T(8,128)(2,1)}, u32[]{:S(2)}, u32[]{:S(2)}) collective-permute-start(bf16[256,1024]{1,0:T(8,128)(2,1)S(1)} %get-tuple-element.20), channel_id=1, source_target_pairs={{0,128},{64,192},{128,0},{192,64},{1,129},{65,193},{129,1},{193,65... | collective-permute-start | bytes 1572872 | tf_op jit(solution)/shard_map/ppermute | solution.py:39
  89.2 29.3 %collective-permute-start.26 = (bf16[256,1024]{1,0:T(8,128)(2,1)S(1)}, bf16[256,1024]{1,0:T(8,128)(2,1)}, u32[]{:S(2)}, u32[]{:S(2)}) collective-permute-start(bf16[256,1024]{1,0:T(8,128)(2,1)S(1)} %get-tuple-element.19), channel_id=1, source_target_pairs={{0,192},{64,0},{128,64},{192,128},{1,193},{65,1},{129,65},{193,129... | collective-permute-start | bytes 1572872 | tf_op jit(solution)/shard_map/ppermute | solution.py:39
  93.9 5.1 %collective-permute-start.20 = (bf16[256,256]{1,0:T(8,128)(2,1)S(1)}, bf16[256,256]{1,0:T(8,128)(2,1)S(1)}, u32[]{:S(2)}, u32[]{:S(2)}) collective-permute-start(bf16[256,256]{1,0:T(8,128)(2,1)S(1)} %fusion.35), channel_id=1, source_target_pairs={{0,1},{1,0},{2,3},{3,2},{4,5},{5,4},{6,7},{7,6},{8,9},{9,8},{10,11... | collective-permute-start | bytes 393224 | tf_op jit(solution)/shard_map/ppermute | solution.py:34
  95.5 17.9 %collective-permute-start.21 = (bf16[256,256]{1,0:T(8,128)(2,1)S(1)}, bf16[256,256]{1,0:T(8,128)(2,1)S(1)}, u32[]{:S(2)}, u32[]{:S(2)}) collective-permute-start(bf16[256,256]{1,0:T(8,128)(2,1)S(1)} %fusion.35), channel_id=1, source_target_pairs={{0,64},{64,128},{128,192},{192,0},{1,65},{65,129},{129,193},{193,1... | collective-permute-start | bytes 393224 | tf_op jit(solution)/shard_map/ppermute | solution.py:39
  99.0 16.7 %collective-permute-start.22 = (bf16[256,256]{1,0:T(8,128)(2,1)S(1)}, bf16[256,256]{1,0:T(8,128)(2,1)S(1)}, u32[]{:S(2)}, u32[]{:S(2)}) collective-permute-start(bf16[256,256]{1,0:T(8,128)(2,1)S(1)} %fusion.35), channel_id=1, source_target_pairs={{0,128},{64,192},{128,0},{192,64},{1,129},{65,193},{129,1},{193,65... | collective-permute-start | bytes 393224 | tf_op jit(solution)/shard_map/ppermute | solution.py:39
  113.5 5.0 %collective-permute-start.23 = (bf16[256,256]{1,0:T(8,128)(2,1)S(1)}, bf16[256,256]{1,0:T(8,128)(2,1)S(1)}, u32[]{:S(2)}, u32[]{:S(2)}) collective-permute-start(bf16[256,256]{1,0:T(8,128)(2,1)S(1)} %fusion.35), channel_id=1, source_target_pairs={{0,192},{64,0},{128,64},{192,128},{1,193},{65,1},{129,65},{193,129... | collective-permute-start | bytes 393224 | tf_op jit(solution)/shard_map/ppermute | solution.py:39
  120.6 1.6 %collective-permute-start.27 = (bf16[16,32,256]{2,1,0:T(8,128)(2,1)S(1)}, bf16[16,32,256]{2,1,0:T(8,128)(2,1)S(1)}, u32[]{:S(2)}, u32[]{:S(2)}) collective-permute-start(bf16[16,32,256]{2,1,0:T(8,128)(2,1)S(1)} %fusion.21), channel_id=1, source_target_pairs={{0,2},{2,0},{1,3},{3,1},{4,6},{6,4},{5,7},{7,5},{8,10},{10,8},{9,1... | collective-permute-start | bytes 786440 | tf_op jit(solution)/shard_map/ppermute | solution.py:34
  123.0 18.3 %all-to-all-start = ((bf16[16,32,256]{2,1,0:T(8,128)(2,1)}), bf16[16,32,256]{2,1,0:T(8,128)(2,1)S(1)}, u32[]{:S(2)}, u32[]{:S(2)}) async-start(bf16[16,32,256]{2,1,0:T(8,128)(2,1)} %core_merge.1), calls=%async_computation | async-start | bytes 524288 | tf_op jit(solution)/shard_map/all_to_all | solution.py:337
  (2 other events, 18.2 us)

commit v4 on v3

--- a/solution.py
+++ b/solution.py
@@ -49,14 +49,12 @@
     query_ref,
     out_ref,
     own_ref,
-    m1,
-    m2,
-    m3,
-    m4,
-    o1,
-    o2,
-    o3,
-    o4,
+    mine1,
+    mine4,
+    mine23,
+    other1,
+    other4,
+    other23,
     near_ref,
     far_ref,
     query_grad_ref,
@@ -76,8 +74,8 @@
     inv_root = 1.0 / math.sqrt(hd)
     to_two = inv_root * math.log2(math.e)
     last = blocks - 1
-    mine = {1: m1, 2: m2, 3: m3, 4: m4}
-    other = {1: o1, 2: o2, 3: o3, 4: o4}
+    mine = {1: mine1, 4: mine4, 2: mine23.at[:tok], 3: mine23.at[tok:]}
+    other = {1: other1, 4: other4, 2: other23.at[:tok], 3: other23.at[tok:]}
     for h in range(heads):
         queries[h * tok : (h + 1) * tok, :] = query_ref[:, h * hd : (h + 1) * hd]
         outs[h * tok : (h + 1) * tok, :] = out_ref[:, h * hd : (h + 1) * hd]
@@ -176,7 +174,7 @@
             jax.ShapeDtypeStruct((4, tok, 2 * hd), BF),
             jax.ShapeDtypeStruct((5, tok, 2 * hd), BF),
         ),
-        in_specs=[pl.BlockSpec(memory_space=pltpu.SMEM)] + [vmem] * 14,
+        in_specs=[pl.BlockSpec(memory_space=pltpu.SMEM)] + [vmem] * 12,
         out_specs=(vmem, vmem, vmem),
         scratch_shapes=[
             pltpu.VMEM((9, tok, hd), BF),
@@ -243,11 +241,14 @@
         turn = (z + distance >= LINE).astype(jnp.int32)
         return columns(key_value, l ^ turn, hd)
 
-    mine, other = {}, {}
-    for d in (3, 4, 2, 1):
-        mine[d] = moved(taken(d), d, True)
-    for d in (1, 2, 3, 4):
-        other[d] = swapped(mine[d], "l")
+    mine1 = moved(taken(1), 1, True)
+    mine4 = moved(taken(4), 4, True)
+    mine23 = moved(jnp.concatenate([columns(key_value, l, hd), mine1], axis=0), 2, False)
+    other1 = swapped(mine1, "l")
+    other4 = swapped(mine4, "l")
+    other23 = swapped(mine23, "l")
+    mine = {1: mine1, 4: mine4, 2: mine23[:tok], 3: mine23[tok:]}
+    other = {1: other1, 4: other4, 2: other23[:tok], 3: other23[tok:]}
     blocks = {0: key_value}
     for d in (1, 2, 3, 4):
         blocks[d] = jnp.where(
@@ -283,8 +284,8 @@
         query,
         out_grad,
         key_value,
-        [mine[d] for d in (1, 2, 3, 4)],
-        [other[d] for d in (1, 2, 3, 4)],
+        (mine1, mine4, mine23),
+        (other1, other4, other23),
         near,
         far,
     )

time: 143 us -> 144 us (level)
  waiting for transfers between devices: 41.9 us -> 55.6 us
  starting transfers between devices: 73.5 us -> 61.4 us
    ppermute x8 -> x7, waiting for transfers between devices: 2.59 us -> 13.4 us  [moved(): return lax.ppermute(value, ALL, routes)]
    ppermute x6, starting transfers between devices: 30.4 us -> 23.2 us  [turned(): lax.ppermute(value, axis, [(i, (i + steps) % count) for i in range(count)])]
    ppermute x8 -> x7, starting transfers between devices: 25.5 us -> 19.2 us  [moved(): return lax.ppermute(value, ALL, routes)]
    ppermute x14 -> x13, waiting for transfers between devices: 17.4 us -> 20.8 us  [swapped(): return lax.ppermute(value, axis, [(0, 1), (1, 0)])]
    ppermute x14 -> x13, starting transfers between devices: 11.2 us -> 11.4 us  [swapped(): return lax.ppermute(value, axis, [(0, 1), (1, 0)])]
  transfers between devices with their start and end apart: 29 -> 27, of which waited for: 18 -> 19; matrix products, arithmetic and copies ran while one was open for 4% -> 4% of each run, Pallas kernels for 0% -> 0%
where the time goes in v4:
time: 144 us; the launch traced here: 143 us
  starting transfers between devices  61.4 us (43%)
  waiting for transfers between devices  55.6 us (39%)
  Pallas kernels  12.7 us (9%)
  local copies, waits for them, and re-layouts  4.65 us (3%)
  other arithmetic  4.06 us (3%)
  matrix products  3.81 us (3%)
    ppermute x6, starting transfers between devices, turned(): lax.ppermute(value, axis, [(i, (i + steps) % count) for i in range(count)])  23.2 us
    ppermute x13, waiting for transfers between devices, swapped(): return lax.ppermute(value, axis, [(0, 1), (1, 0)])  20.8 us
    ppermute x7, starting transfers between devices, moved(): return lax.ppermute(value, ALL, routes)  19.2 us
    ppermute x7, waiting for transfers between devices, moved(): return lax.ppermute(value, ALL, routes)  13.4 us
    pallas_call x1, Pallas kernels, attention(): pl.pallas_call(attention_kernel, out_shape=(jax.ShapeDtypeStruct((tok, wi...  11.9 us
    ppermute x13, starting transfers between devices, swapped(): return lax.ppermute(value, axis, [(0, 1), (1, 0)])  11.4 us
    ppermute x6, waiting for transfers between devices, turned(): lax.ppermute(value, axis, [(i, (i + steps) % count) for i in range(count)])  11.4 us
    all_to_all x1, waiting for transfers between devices, local(): lax.all_to_all(total, ('xh', 'z'), split_axis=0, concat_axis=0, tiled=True)  10 us
  transfers between devices with their start and end apart: 27, of which 19 were waited for; matrix products, arithmetic and copies ran while one was open for 4% of the time, Pallas kernels for 0%

profile of v4, /device:TPU:32, one launch (start us, length us, event | category | flops | bytes accessed | tf_op | source)
XLA Modules:
  0.0 143.2 jit_solution(9495048317948397810)
XLA Ops:
  1.9 4.0 %collective-permute-start = (bf16[256,256]{1,0:T(8,128)(2,1)S(1)}, bf16[256,256]{1,0:T(8,128)(2,1)S(1)}, u32[]{:S(2)}, u32[]{:S(2)}) collective-permute-start(bf16[256,256]{1,0:T(8,128)(2,1)S(1)} %get-tuple-element.55), channel_id=1, source_target_pairs={{0,4},{1,5},{2,6},{3,7},{4,8},{5,9},{6,10},{7,11},{8,12},{9,13},{1... | collective-permute-start | bytes 393224 | tf_op jit(solution)/shard_map/ppermute | solution.py:30
  5.9 7.1 %collective-permute-start.1 = (bf16[256,256]{1,0:T(8,128)(2,1)S(1)}, bf16[256,256]{1,0:T(8,128)(2,1)S(1)}, u32[]{:S(2)}, u32[]{:S(2)}) collective-permute-start(bf16[256,256]{1,0:T(8,128)(2,1)S(1)} %get-tuple-element.54), channel_id=1, source_target_pairs={{0,16},{1,17},{2,18},{3,19},{4,20},{5,21},{6,22},{7,23},{8,24},{9,... | collective-permute-start | bytes 393224 | tf_op jit(solution)/shard_map/ppermute | solution.py:30
  13.0 2.4 %collective-permute-start.2 = (bf16[512,256]{1,0:T(8,128)(2,1)S(1)}, bf16[512,256]{1,0:T(8,128)(2,1)S(1)}, u32[]{:S(2)}, u32[]{:S(2)}) collective-permute-start(bf16[512,256]{1,0:T(8,128)(2,1)S(1)} %pad_maximum_fusion), channel_id=1, source_target_pairs={{0,8},{1,9},{2,10},{3,11},{4,12},{5,13},{6,14},{7,15},{8,16},{9,17... | collective-permute-start | bytes 786440 | tf_op jit(solution)/shard_map/ppermute | solution.py:30
  15.4 1.6 %collective-permute-start.3 = (bf16[256,256]{1,0:T(8,128)(2,1)S(1)}, bf16[256,256]{1,0:T(8,128)(2,1)S(1)}, u32[]{:S(2)}, u32[]{:S(2)}) collective-permute-start(bf16[256,256]{1,0:T(8,128)(2,1)S(1)} %collective-permute-done.mine1), channel_id=1, source_target_pairs={{0,1},{1,0},{2,3},{3,2},{4,5},{5,4},{6,7},{7,6},{8,9},{9,8},{10,11... | collective-permute-start | bytes 393224 | tf_op jit(solution)/shard_map/ppermute | solution.py:34
  19.5 1.5 %collective-permute-done.3.other1 = bf16[256,256]{1,0:T(8,128)(2,1)S(1)} collective-permute-done((bf16[256,256]{1,0:T(8,128)(2,1)S(1)}, bf16[256,256]{1,0:T(8,128)(2,1)S(1)}, u32[]{:S(2)}, u32[]{:S(2)}) %collective-permute-start.3) | collective-permute-done | bytes 131104 | tf_op jit(solution)/shard_map/ppermute | solution.py:34
  21.1 8.9 %collective-permute-done.2.mine23 = bf16[512,256]{1,0:T(8,128)(2,1)S(1)} collective-permute-done((bf16[512,256]{1,0:T(8,128)(2,1)S(1)}, bf16[512,256]{1,0:T(8,128)(2,1)S(1)}, u32[]{:S(2)}, u32[]{:S(2)}) %collective-permute-start.2) | collective-permute-done | bytes 262176 | tf_op jit(solution)/shard_map/ppermute | solution.py:30
  30.0 1.5 %collective-permute-start.5 = (bf16[512,256]{1,0:T(8,128)(2,1)S(1)}, bf16[512,256]{1,0:T(8,128)(2,1)S(1)}, u32[]{:S(2)}, u32[]{:S(2)}) collective-permute-start(bf16[512,256]{1,0:T(8,128)(2,1)S(1)} %collective-permute-done.2.mine23), channel_id=1, source_target_pairs={{0,1},{1,0},{2,3},{3,2},{4,5},{5,4},{6,7},{7,6},{8,9},{9,8},{10,11... | collective-permute-start | bytes 786440 | tf_op jit(solution)/shard_map/ppermute | solution.py:34
  31.7 6.6 %collective-permute-done.5.other23 = bf16[512,256]{1,0:T(8,128)(2,1)S(1)} collective-permute-done((bf16[512,256]{1,0:T(8,128)(2,1)S(1)}, bf16[512,256]{1,0:T(8,128)(2,1)S(1)}, u32[]{:S(2)}, u32[]{:S(2)}) %collective-permute-start.5) | collective-permute-done | bytes 262176 | tf_op jit(solution)/shard_map/ppermute | solution.py:34
  41.6 11.9 %attention.1 = (bf16[256,1024]{1,0:T(8,128)(2,1)}, bf16[4,256,512]{2,1,0:T(8,128)(2,1)S(1)}, bf16[5,256,512]{2,1,0:T(8,128)(2,1)S(1)}) custom-call(s32[1]{0:T(128)} %bitcast.side_ref, s32[1,1024]{1,0:T(1,128)S(1)} %bitcast.51, bf16[256,1024]{1,0:T(8,128)(2,1)S(1)} %copy-done.1, bf16[256,1024]{1,0:T(8,128)(2,1)S(1)} %copy-done.2, ...), custom_call_target="tpu_custom_call" | custom-call | flops 6039797760 | bytes 8388608 | tf_op jit(solution)/shard_map/attention/pallas_call | solution.py:170
  53.7 2.5 %collective-permute-done.8 = bf16[1024,512]{1,0:T(8,128)(2,1)} collective-permute-done((bf16[1024,512]{1,0:T(8,128)(2,1)S(1)}, bf16[1024,512]{1,0:T(8,128)(2,1)}, u32[]{:S(2)}, u32[]{:S(2)}) %collective-permute-start.8) | collective-permute-done | bytes 1048608 | tf_op jit(solution)/shard_map/ppermute | solution.py:34
  58.0 1.5 %collective-permute-start.10 = (bf16[256,256]{1,0:T(8,128)(2,1)S(1)}, bf16[256,256]{1,0:T(8,128)(2,1)S(1)}, u32[]{:S(2)}, u32[]{:S(2)}) collective-permute-start(bf16[256,256]{1,0:T(8,128)(2,1)S(1)} %get-tuple-element.32), channel_id=1, source_target_pairs={{0,1},{1,0},{2,3},{3,2},{4,5},{5,4},{6,7},{7,6},{8,9},{9,8},{10,11... | collective-permute-start | bytes 393224 | tf_op jit(solution)/shard_map/ppermute | solution.py:34
  60.1 1.4 %collective-permute-start.14 = (bf16[256,256]{1,0:T(8,128)(2,1)S(1)}, bf16[256,256]{1,0:T(8,128)(2,1)S(1)}, u32[]{:S(2)}, u32[]{:S(2)}) collective-permute-start(bf16[256,256]{1,0:T(8,128)(2,1)S(1)} %get-tuple-element.44), channel_id=1, source_target_pairs={{0,1},{1,0},{2,3},{3,2},{4,5},{5,4},{6,7},{7,6},{8,9},{9,8},{10,11... | collective-permute-start | bytes 393224 | tf_op jit(solution)/shard_map/ppermute | solution.py:34
  62.1 1.4 %collective-permute-start.9 = (bf16[256,256]{1,0:T(8,128)(2,1)S(1)}, bf16[256,256]{1,0:T(8,128)(2,1)S(1)}, u32[]{:S(2)}, u32[]{:S(2)}) collective-permute-start(bf16[256,256]{1,0:T(8,128)(2,1)S(1)} %get-tuple-element.40), channel_id=1, source_target_pairs={{0,1},{1,0},{2,3},{3,2},{4,5},{5,4},{6,7},{7,6},{8,9},{9,8},{10,11... | collective-permute-start | bytes 393224 | tf_op jit(solution)/shard_map/ppermute | solution.py:34
  64.5 1.9 %collective-permute-start.11 = (bf16[256,256]{1,0:T(8,128)(2,1)S(1)}, bf16[256,256]{1,0:T(8,128)(2,1)S(1)}, u32[]{:S(2)}, u32[]{:S(2)}) collective-permute-start(bf16[256,256]{1,0:T(8,128)(2,1)S(1)} %merge.4), channel_id=1, source_target_pairs={{4,0},{5,1},{6,2},{7,3},{8,4},{9,5},{10,6},{11,7},{12,8},{13,9},{1... | collective-permute-start | bytes 393224 | tf_op jit(solution)/shard_map/ppermute | solution.py:30
  67.3 1.3 collective-permute-start.13
  68.6 1.5 %collective-permute-done.14.two_ref = bf16[256,256]{1,0:T(8,128)(2,1)S(1)} collective-permute-done((bf16[256,256]{1,0:T(8,128)(2,1)S(1)}, bf16[256,256]{1,0:T(8,128)(2,1)S(1)}, u32[]{:S(2)}, u32[]{:S(2)}) %collective-permute-start.14) | collective-permute-done | bytes 131104 | tf_op jit(solution)/shard_map/ppermute | solution.py:34
  71.4 1.5 %collective-permute-done.16.two_ref = bf16[256,256]{1,0:T(8,128)(2,1)S(1)} collective-permute-done((bf16[256,256]{1,0:T(8,128)(2,1)S(1)}, bf16[256,256]{1,0:T(8,128)(2,1)S(1)}, u32[]{:S(2)}, u32[]{:S(2)}) %collective-permute-start.16) | collective-permute-done | bytes 131104 | tf_op jit(solution)/shard_map/ppermute | solution.py:34
  72.9 1.3 collective-permute-start.17
  74.8 12.0 %collective-permute-start.22 = (bf16[256,1024]{1,0:T(8,128)(2,1)S(1)}, bf16[256,1024]{1,0:T(8,128)(2,1)}, u32[]{:S(2)}, u32[]{:S(2)}) collective-permute-start(bf16[256,1024]{1,0:T(8,128)(2,1)S(1)} %get-tuple-element.18), channel_id=1, source_target_pairs={{0,64},{64,128},{128,192},{192,0},{1,65},{65,129},{129,193},{193,1... | collective-permute-start | bytes 1572872 | tf_op jit(solution)/shard_map/ppermute | solution.py:39
  86.9 3.1 %collective-permute-start.23 = (bf16[256,1024]{1,0:T(8,128)(2,1)S(1)}, bf16[256,1024]{1,0:T(8,128)(2,1)}, u32[]{:S(2)}, u32[]{:S(2)}) collective-permute-start(bf16[256,1024]{1,0:T(8,128)(2,1)S(1)} %get-tuple-element.20), channel_id=1, source_target_pairs={{0,128},{64,192},{128,0},{192,64},{1,129},{65,193},{129,1},{193,65... | collective-permute-start | bytes 1572872 | tf_op jit(solution)/shard_map/ppermute | solution.py:39
  91.1 3.9 %collective-permute-done.17 = bf16[256,256]{1,0:T(8,128)(2,1)} collective-permute-done((bf16[256,256]{1,0:T(8,128)(2,1)S(1)}, bf16[256,256]{1,0:T(8,128)(2,1)}, u32[]{:S(2)}, u32[]{:S(2)}) %collective-permute-start.17) | collective-permute-done | bytes 131104 | tf_op jit(solution)/shard_map/ppermute | solution.py:30
  96.1 1.6 %collective-permute-start.18 = (bf16[256,256]{1,0:T(8,128)(2,1)S(1)}, bf16[256,256]{1,0:T(8,128)(2,1)S(1)}, u32[]{:S(2)}, u32[]{:S(2)}) collective-permute-start(bf16[256,256]{1,0:T(8,128)(2,1)S(1)} %fusion.35), channel_id=1, source_target_pairs={{0,1},{1,0},{2,3},{3,2},{4,5},{5,4},{6,7},{7,6},{8,9},{9,8},{10,11... | collective-permute-start | bytes 393224 | tf_op jit(solution)/shard_map/ppermute | solution.py:34
  98.7 2.5 %collective-permute-done.18 = bf16[256,256]{1,0:T(8,128)(2,1)S(1)} collective-permute-done((bf16[256,256]{1,0:T(8,128)(2,1)S(1)}, bf16[256,256]{1,0:T(8,128)(2,1)S(1)}, u32[]{:S(2)}, u32[]{:S(2)}) %collective-permute-start.18) | collective-permute-done | bytes 131104 | tf_op jit(solution)/shard_map/ppermute | solution.py:34
  101.1 4.5 %collective-permute-start.20 = (bf16[256,256]{1,0:T(8,128)(2,1)S(1)}, bf16[256,256]{1,0:T(8,128)(2,1)S(1)}, u32[]{:S(2)}, u32[]{:S(2)}) collective-permute-start(bf16[256,256]{1,0:T(8,128)(2,1)S(1)} %fusion.35), channel_id=1, source_target_pairs={{0,128},{64,192},{128,0},{192,64},{1,129},{65,193},{129,1},{193,65... | collective-permute-start | bytes 393224 | tf_op jit(solution)/shard_map/ppermute | solution.py:39
  105.6 8.0 %collective-permute-done.19 = bf16[256,256]{1,0:T(8,128)(2,1)S(1)} collective-permute-done((bf16[256,256]{1,0:T(8,128)(2,1)S(1)}, bf16[256,256]{1,0:T(8,128)(2,1)S(1)}, u32[]{:S(2)}, u32[]{:S(2)}) %collective-permute-start.19) | collective-permute-done | bytes 131104 | tf_op jit(solution)/shard_map/ppermute | solution.py:39
  113.6 1.6 %collective-permute-start.21 = (bf16[256,256]{1,0:T(8,128)(2,1)S(1)}, bf16[256,256]{1,0:T(8,128)(2,1)S(1)}, u32[]{:S(2)}, u32[]{:S(2)}) collective-permute-start(bf16[256,256]{1,0:T(8,128)(2,1)S(1)} %fusion.35), channel_id=1, source_target_pairs={{0,192},{64,0},{128,64},{192,128},{1,193},{65,1},{129,65},{193,129... | collective-permute-start | bytes 393224 | tf_op jit(solution)/shard_map/ppermute | solution.py:39
  116.0 2.5 %collective-permute-done.21 = bf16[256,256]{1,0:T(8,128)(2,1)S(1)} collective-permute-done((bf16[256,256]{1,0:T(8,128)(2,1)S(1)}, bf16[256,256]{1,0:T(8,128)(2,1)S(1)}, u32[]{:S(2)}, u32[]{:S(2)}) %collective-permute-start.21) | collective-permute-done | bytes 131104 | tf_op jit(solution)/shard_map/ppermute | solution.py:39
  118.6 2.1 %fusion.11 = f32[1024,256]{1,0:T(8,128)S(1)} fusion(bf16[256,1024]{1,0:T(8,128)(2,1)} %collective-permute-done.24, bf16[256,1024]{1,0:T(8,128)(2,1)} %collective-permute-done.23, bf16[256,1024]{1,0:T(8,128)(2,1)} %collective-permute-done.22, bf16[256,1024]{1,0:T(8,128)(2,1)S(1)} %get-tuple-element.17, bf16[256,256]{1,0:T(8,128)(2,1)S(1)} %collective-permute-done.21, ...), kind=kOutput, calls=%fused_computation.13 | convolution fusion | flops 547618816 | bytes 3670016 | tf_op jit(solution)/shard_map/dot_general | solution.py:332
  120.9 1.5 %collective-permute-done.25.arrived_ref = bf16[16,32,256]{2,1,0:T(8,128)(2,1)S(1)} collective-permute-done((bf16[16,32,256]{2,1,0:T(8,128)(2,1)S(1)}, bf16[16,32,256]{2,1,0:T(8,128)(2,1)S(1)}, u32[]{:S(2)}, u32[]{:S(2)}) %collective-permute-start.25) | collective-permute-done | bytes 262176 | tf_op jit(solution)/shard_map/ppermute | solution.py:34
  123.1 7.5 %all-to-all-start = ((bf16[16,32,256]{2,1,0:T(8,128)(2,1)}), bf16[16,32,256]{2,1,0:T(8,128)(2,1)S(1)}, u32[]{:S(2)}, u32[]{:S(2)}) async-start(bf16[16,32,256]{2,1,0:T(8,128)(2,1)} %core_merge.1), calls=%async_computation | async-start | bytes 524288 | tf_op jit(solution)/shard_map/all_to_all | solution.py:338
  130.8 1.7 %convolution_convert_fusion = bf16[256,2048]{1,0:T(8,128)(2,1)} fusion(bf16[2048,256]{1,0:T(8,128)(2,1)S(1)} %get-tuple-element.22, bf16[2048,256]{1,0:T(8,128)(2,1)S(1)} %get-tuple-element.21, bf16[256,256]{1,0:T(8,128)(2,1)S(1)} %collective-permute-done.18, bf16[256,256]{1,0:T(8,128)(2,1)S(1)} %fusion.35), kind=kOutput, calls=%fused_computation | convolution fusion | flops 542113792 | bytes 3407872 | tf_op jit(solution)/shard_map/dot_general | solution.py:323
  132.5 10.0 %all-to-all-done = bf16[16,32,256]{2,1,0:T(8,128)(2,1)S(1)} async-done(((bf16[16,32,256]{2,1,0:T(8,128)(2,1)}), bf16[16,32,256]{2,1,0:T(8,128)(2,1)S(1)}, u32[]{:S(2)}, u32[]{:S(2)}) %all-to-all-start) | async-done | bytes 262176 | tf_op jit(solution)/shard_map/all_to_all | solution.py:338
  (62 shorter events, 19.9 us)
Async XLA Ops:
  1.9 36.5 %copy-start = (bf16[256,512]{1,0:T(8,128)(2,1)S(1)}, bf16[256,512]{1,0:T(8,128)(2,1)}, u32[]{:S(2)}) copy-start(bf16[256,512]{1,0:T(8,128)(2,1)} %own_ref.1) | copy-start | bytes 786436
  1.9 11.1 %collective-permute-start = (bf16[256,256]{1,0:T(8,128)(2,1)S(1)}, bf16[256,256]{1,0:T(8,128)(2,1)S(1)}, u32[]{:S(2)}, u32[]{:S(2)}) collective-permute-start(bf16[256,256]{1,0:T(8,128)(2,1)S(1)} %get-tuple-element.55), channel_id=1, source_target_pairs={{0,4},{1,5},{2,6},{3,7},{4,8},{5,9},{6,10},{7,11},{8,12},{9,13},{1... | collective-permute-start | bytes 393224 | tf_op jit(solution)/shard_map/ppermute | solution.py:30
  5.9 11.7 %collective-permute-start.1 = (bf16[256,256]{1,0:T(8,128)(2,1)S(1)}, bf16[256,256]{1,0:T(8,128)(2,1)S(1)}, u32[]{:S(2)}, u32[]{:S(2)}) collective-permute-start(bf16[256,256]{1,0:T(8,128)(2,1)S(1)} %get-tuple-element.54), channel_id=1, source_target_pairs={{0,16},{1,17},{2,18},{3,19},{4,20},{5,21},{6,22},{7,23},{8,24},{9,... | collective-permute-start | bytes 393224 | tf_op jit(solution)/shard_map/ppermute | solution.py:30
  13.0 16.9 %collective-permute-start.2 = (bf16[512,256]{1,0:T(8,128)(2,1)S(1)}, bf16[512,256]{1,0:T(8,128)(2,1)S(1)}, u32[]{:S(2)}, u32[]{:S(2)}) collective-permute-start(bf16[512,256]{1,0:T(8,128)(2,1)S(1)} %pad_maximum_fusion), channel_id=1, source_target_pairs={{0,8},{1,9},{2,10},{3,11},{4,12},{5,13},{6,14},{7,15},{8,16},{9,17... | collective-permute-start | bytes 786440 | tf_op jit(solution)/shard_map/ppermute | solution.py:30
  15.4 5.5 %collective-permute-start.3 = (bf16[256,256]{1,0:T(8,128)(2,1)S(1)}, bf16[256,256]{1,0:T(8,128)(2,1)S(1)}, u32[]{:S(2)}, u32[]{:S(2)}) collective-permute-start(bf16[256,256]{1,0:T(8,128)(2,1)S(1)} %collective-permute-done.mine1), channel_id=1, source_target_pairs={{0,1},{1,0},{2,3},{3,2},{4,5},{5,4},{6,7},{7,6},{8,9},{9,8},{10,11... | collective-permute-start | bytes 393224 | tf_op jit(solution)/shard_map/ppermute | solution.py:34
  17.6 13.9 %collective-permute-start.4 = (bf16[256,256]{1,0:T(8,128)(2,1)S(1)}, bf16[256,256]{1,0:T(8,128)(2,1)S(1)}, u32[]{:S(2)}, u32[]{:S(2)}) collective-permute-start(bf16[256,256]{1,0:T(8,128)(2,1)S(1)} %collective-permute-done.1.mine4), channel_id=1, source_target_pairs={{0,1},{1,0},{2,3},{3,2},{4,5},{5,4},{6,7},{7,6},{8,9},{9,8},{10,11... | collective-permute-start | bytes 393224 | tf_op jit(solution)/shard_map/ppermute | solution.py:34
  30.0 8.3 %collective-permute-start.5 = (bf16[512,256]{1,0:T(8,128)(2,1)S(1)}, bf16[512,256]{1,0:T(8,128)(2,1)S(1)}, u32[]{:S(2)}, u32[]{:S(2)}) collective-permute-start(bf16[512,256]{1,0:T(8,128)(2,1)S(1)} %collective-permute-done.2.mine23), channel_id=1, source_target_pairs={{0,1},{1,0},{2,3},{3,2},{4,5},{5,4},{6,7},{7,6},{8,9},{9,8},{10,11... | collective-permute-start | bytes 786440 | tf_op jit(solution)/shard_map/ppermute | solution.py:34
  31.6 9.9 %copy-start.1 = (bf16[256,1024]{1,0:T(8,128)(2,1)S(1)}, bf16[256,1024]{1,0:T(8,128)(2,1)}, u32[]{:S(2)}) copy-start(bf16[256,1024]{1,0:T(8,128)(2,1)} %query_ref.1) | copy-start | bytes 1572868
  31.6 9.9 %copy-start.2 = (bf16[256,1024]{1,0:T(8,128)(2,1)S(1)}, bf16[256,1024]{1,0:T(8,128)(2,1)}, u32[]{:S(2)}) copy-start(bf16[256,1024]{1,0:T(8,128)(2,1)} %out_ref.1) | copy-start | bytes 1572868
  38.8 2.0 %collective-permute-start.6 = (bf16[512,512]{1,0:T(8,128)(2,1)S(1)}, bf16[512,512]{1,0:T(8,128)(2,1)S(1)}, u32[]{:S(2)}, u32[]{:S(2)}) collective-permute-start(bf16[512,512]{1,0:T(8,128)(2,1)S(1)} %get-tuple-element.48), channel_id=1, source_target_pairs={{0,2},{2,0},{1,3},{3,1},{4,6},{6,4},{5,7},{7,5},{8,10},{10,8},{9,1... | collective-permute-start | bytes 1572872 | tf_op jit(solution)/shard_map/ppermute | solution.py:34
  38.9 2.6 %collective-permute-start.7 = (bf16[512,512]{1,0:T(8,128)(2,1)S(1)}, bf16[512,512]{1,0:T(8,128)(2,1)S(1)}, u32[]{:S(2)}, u32[]{:S(2)}) collective-permute-start(bf16[512,512]{1,0:T(8,128)(2,1)S(1)} %get-tuple-element.47), channel_id=1, source_target_pairs={{0,2},{2,0},{1,3},{3,1},{4,6},{6,4},{5,7},{7,5},{8,10},{10,8},{9,1... | collective-permute-start | bytes 1572872 | tf_op jit(solution)/shard_map/ppermute | solution.py:34
  53.4 2.8 %collective-permute-start.8 = (bf16[1024,512]{1,0:T(8,128)(2,1)S(1)}, bf16[1024,512]{1,0:T(8,128)(2,1)}, u32[]{:S(2)}, u32[]{:S(2)}) collective-permute-start(bf16[1024,512]{1,0:T(8,128)(2,1)S(1)} %bitcast.52), channel_id=1, source_target_pairs={{0,2},{2,0},{1,3},{3,1},{4,6},{6,4},{5,7},{7,5},{8,10},{10,8},{9,1... | collective-permute-start | bytes 3145736 | tf_op jit(solution)/shard_map/ppermute | solution.py:34
  58.0 6.5 %collective-permute-start.10 = (bf16[256,256]{1,0:T(8,128)(2,1)S(1)}, bf16[256,256]{1,0:T(8,128)(2,1)S(1)}, u32[]{:S(2)}, u32[]{:S(2)}) collective-permute-start(bf16[256,256]{1,0:T(8,128)(2,1)S(1)} %get-tuple-element.32), channel_id=1, source_target_pairs={{0,1},{1,0},{2,3},{3,2},{4,5},{5,4},{6,7},{7,6},{8,9},{9,8},{10,11... | collective-permute-start | bytes 393224 | tf_op jit(solution)/shard_map/ppermute | solution.py:34
  59.5 7.7 %collective-permute-start.12 = (bf16[256,256]{1,0:T(8,128)(2,1)S(1)}, bf16[256,256]{1,0:T(8,128)(2,1)S(1)}, u32[]{:S(2)}, u32[]{:S(2)}) collective-permute-start(bf16[256,256]{1,0:T(8,128)(2,1)S(1)} %get-tuple-element.42), channel_id=1, source_target_pairs={{0,1},{1,0},{2,3},{3,2},{4,5},{5,4},{6,7},{7,6},{8,9},{9,8},{10,11... | collective-permute-start | bytes 393224 | tf_op jit(solution)/shard_map/ppermute | solution.py:34
  60.1 10.0 %collective-permute-start.14 = (bf16[256,256]{1,0:T(8,128)(2,1)S(1)}, bf16[256,256]{1,0:T(8,128)(2,1)S(1)}, u32[]{:S(2)}, u32[]{:S(2)}) collective-permute-start(bf16[256,256]{1,0:T(8,128)(2,1)S(1)} %get-tuple-element.44), channel_id=1, source_target_pairs={{0,1},{1,0},{2,3},{3,2},{4,5},{5,4},{6,7},{7,6},{8,9},{9,8},{10,11... | collective-permute-start | bytes 393224 | tf_op jit(solution)/shard_map/ppermute | solution.py:34
  61.5 11.3 %collective-permute-start.16 = (bf16[256,256]{1,0:T(8,128)(2,1)S(1)}, bf16[256,256]{1,0:T(8,128)(2,1)S(1)}, u32[]{:S(2)}, u32[]{:S(2)}) collective-permute-start(bf16[256,256]{1,0:T(8,128)(2,1)S(1)} %get-tuple-element.46), channel_id=1, source_target_pairs={{0,1},{1,0},{2,3},{3,2},{4,5},{5,4},{6,7},{7,6},{8,9},{9,8},{10,11... | collective-permute-start | bytes 393224 | tf_op jit(solution)/shard_map/ppermute | solution.py:34
  62.1 12.1 %copy-start.4 = (bf16[256,4096]{1,0:T(8,128)(2,1)S(1)}, bf16[256,4096]{1,0:T(8,128)(2,1)}, u32[]{:S(2)}) copy-start(bf16[256,4096]{1,0:T(8,128)(2,1)} %param.9) | copy-start | bytes 6291460
  62.1 12.7 %collective-permute-start.9 = (bf16[256,256]{1,0:T(8,128)(2,1)S(1)}, bf16[256,256]{1,0:T(8,128)(2,1)S(1)}, u32[]{:S(2)}, u32[]{:S(2)}) collective-permute-start(bf16[256,256]{1,0:T(8,128)(2,1)S(1)} %get-tuple-element.40), channel_id=1, source_target_pairs={{0,1},{1,0},{2,3},{3,2},{4,5},{5,4},{6,7},{7,6},{8,9},{9,8},{10,11... | collective-permute-start | bytes 393224 | tf_op jit(solution)/shard_map/ppermute | solution.py:34
  64.5 22.4 %collective-permute-start.11 = (bf16[256,256]{1,0:T(8,128)(2,1)S(1)}, bf16[256,256]{1,0:T(8,128)(2,1)S(1)}, u32[]{:S(2)}, u32[]{:S(2)}) collective-permute-start(bf16[256,256]{1,0:T(8,128)(2,1)S(1)} %merge.4), channel_id=1, source_target_pairs={{4,0},{5,1},{6,2},{7,3},{8,4},{9,5},{10,6},{11,7},{12,8},{13,9},{1... | collective-permute-start | bytes 393224 | tf_op jit(solution)/shard_map/ppermute | solution.py:30
  67.3 22.7 %collective-permute-start.13 = (bf16[256,256]{1,0:T(8,128)(2,1)S(1)}, bf16[256,256]{1,0:T(8,128)(2,1)S(1)}, u32[]{:S(2)}, u32[]{:S(2)}) collective-permute-start(bf16[256,256]{1,0:T(8,128)(2,1)S(1)} %merge.5), channel_id=1, source_target_pairs={{8,0},{9,1},{10,2},{11,3},{12,4},{13,5},{14,6},{15,7},{16,8},{17,9... | collective-permute-start | bytes 393224 | tf_op jit(solution)/shard_map/ppermute | solution.py:30
  70.1 21.0 %collective-permute-start.15 = (bf16[256,256]{1,0:T(8,128)(2,1)S(1)}, bf16[256,256]{1,0:T(8,128)(2,1)}, u32[]{:S(2)}, u32[]{:S(2)}) collective-permute-start(bf16[256,256]{1,0:T(8,128)(2,1)S(1)} %merge.6), channel_id=1, source_target_pairs={{12,0},{13,1},{14,2},{15,3},{16,4},{17,5},{18,6},{19,7},{20,8},{21... | collective-permute-start | bytes 393224 | tf_op jit(solution)/shard_map/ppermute | solution.py:30
  72.9 22.1 %collective-permute-start.17 = (bf16[256,256]{1,0:T(8,128)(2,1)S(1)}, bf16[256,256]{1,0:T(8,128)(2,1)}, u32[]{:S(2)}, u32[]{:S(2)}) collective-permute-start(bf16[256,256]{1,0:T(8,128)(2,1)S(1)} %merge.7), channel_id=1, source_target_pairs={{16,0},{17,1},{18,2},{19,3},{20,4},{21,5},{22,6},{23,7},{24,8},{25... | collective-permute-start | bytes 393224 | tf_op jit(solution)/shard_map/ppermute | solution.py:30
  74.8 43.7 %collective-permute-start.22 = (bf16[256,1024]{1,0:T(8,128)(2,1)S(1)}, bf16[256,1024]{1,0:T(8,128)(2,1)}, u32[]{:S(2)}, u32[]{:S(2)}) collective-permute-start(bf16[256,1024]{1,0:T(8,128)(2,1)S(1)} %get-tuple-element.18), channel_id=1, source_target_pairs={{0,64},{64,128},{128,192},{192,0},{1,65},{65,129},{129,193},{193,1... | collective-permute-start | bytes 1572872 | tf_op jit(solution)/shard_map/ppermute | solution.py:39
  86.9 31.7 %collective-permute-start.23 = (bf16[256,1024]{1,0:T(8,128)(2,1)S(1)}, bf16[256,1024]{1,0:T(8,128)(2,1)}, u32[]{:S(2)}, u32[]{:S(2)}) collective-permute-start(bf16[256,1024]{1,0:T(8,128)(2,1)S(1)} %get-tuple-element.20), channel_id=1, source_target_pairs={{0,128},{64,192},{128,0},{192,64},{1,129},{65,193},{129,1},{193,65... | collective-permute-start | bytes 1572872 | tf_op jit(solution)/shard_map/ppermute | solution.py:39
  90.0 28.6 %collective-permute-start.24 = (bf16[256,1024]{1,0:T(8,128)(2,1)S(1)}, bf16[256,1024]{1,0:T(8,128)(2,1)}, u32[]{:S(2)}, u32[]{:S(2)}) collective-permute-start(bf16[256,1024]{1,0:T(8,128)(2,1)S(1)} %get-tuple-element.19), channel_id=1, source_target_pairs={{0,192},{64,0},{128,64},{192,128},{1,193},{65,1},{129,65},{193,129... | collective-permute-start | bytes 1572872 | tf_op jit(solution)/shard_map/ppermute | solution.py:39
  96.1 5.1 %collective-permute-start.18 = (bf16[256,256]{1,0:T(8,128)(2,1)S(1)}, bf16[256,256]{1,0:T(8,128)(2,1)S(1)}, u32[]{:S(2)}, u32[]{:S(2)}) collective-permute-start(bf16[256,256]{1,0:T(8,128)(2,1)S(1)} %fusion.35), channel_id=1, source_target_pairs={{0,1},{1,0},{2,3},{3,2},{4,5},{5,4},{6,7},{7,6},{8,9},{9,8},{10,11... | collective-permute-start | bytes 393224 | tf_op jit(solution)/shard_map/ppermute | solution.py:34
  97.7 15.9 %collective-permute-start.19 = (bf16[256,256]{1,0:T(8,128)(2,1)S(1)}, bf16[256,256]{1,0:T(8,128)(2,1)S(1)}, u32[]{:S(2)}, u32[]{:S(2)}) collective-permute-start(bf16[256,256]{1,0:T(8,128)(2,1)S(1)} %fusion.35), channel_id=1, source_target_pairs={{0,64},{64,128},{128,192},{192,0},{1,65},{65,129},{129,193},{193,1... | collective-permute-start | bytes 393224 | tf_op jit(solution)/shard_map/ppermute | solution.py:39
  101.1 14.9 %collective-permute-start.20 = (bf16[256,256]{1,0:T(8,128)(2,1)S(1)}, bf16[256,256]{1,0:T(8,128)(2,1)S(1)}, u32[]{:S(2)}, u32[]{:S(2)}) collective-permute-start(bf16[256,256]{1,0:T(8,128)(2,1)S(1)} %fusion.35), channel_id=1, source_target_pairs={{0,128},{64,192},{128,0},{192,64},{1,129},{65,193},{129,1},{193,65... | collective-permute-start | bytes 393224 | tf_op jit(solution)/shard_map/ppermute | solution.py:39
  113.6 5.0 %collective-permute-start.21 = (bf16[256,256]{1,0:T(8,128)(2,1)S(1)}, bf16[256,256]{1,0:T(8,128)(2,1)S(1)}, u32[]{:S(2)}, u32[]{:S(2)}) collective-permute-start(bf16[256,256]{1,0:T(8,128)(2,1)S(1)} %fusion.35), channel_id=1, source_target_pairs={{0,192},{64,0},{128,64},{192,128},{1,193},{65,1},{129,65},{193,129... | collective-permute-start | bytes 393224 | tf_op jit(solution)/shard_map/ppermute | solution.py:39
  120.7 10.0 %copy-start.3 = (bf16[2,2048,256]{2,1,0:T(8,128)(2,1)S(1)}, bf16[2,2048,256]{2,1,0:T(8,128)(2,1)}, u32[]{:S(2)}) copy-start(bf16[2,2048,256]{2,1,0:T(8,128)(2,1)} %param.10) | copy-start | bytes 6291460
  120.8 1.6 %collective-permute-start.25 = (bf16[16,32,256]{2,1,0:T(8,128)(2,1)S(1)}, bf16[16,32,256]{2,1,0:T(8,128)(2,1)S(1)}, u32[]{:S(2)}, u32[]{:S(2)}) collective-permute-start(bf16[16,32,256]{2,1,0:T(8,128)(2,1)S(1)} %fusion.21), channel_id=1, source_target_pairs={{0,2},{2,0},{1,3},{3,1},{4,6},{6,4},{5,7},{7,5},{8,10},{10,8},{9,1... | collective-permute-start | bytes 786440 | tf_op jit(solution)/shard_map/ppermute | solution.py:34
  123.1 19.4 %all-to-all-start = ((bf16[16,32,256]{2,1,0:T(8,128)(2,1)}), bf16[16,32,256]{2,1,0:T(8,128)(2,1)S(1)}, u32[]{:S(2)}, u32[]{:S(2)}) async-start(bf16[16,32,256]{2,1,0:T(8,128)(2,1)} %core_merge.1), calls=%async_computation | async-start | bytes 524288 | tf_op jit(solution)/shard_map/all_to_all | solution.py:338

commit v5 on v4

--- a/solution.py
+++ b/solution.py
@@ -80,17 +80,19 @@
         queries[h * tok : (h + 1) * tok, :] = query_ref[:, h * hd : (h + 1) * hd]
         outs[h * tok : (h + 1) * tok, :] = out_ref[:, h * hd : (h + 1) * hd]
 
-    @pl.when(side_ref[0] == 0)
-    def _():
-        for d in mine:
-            keys[last - 2 * d] = mine[d][...]
-            values[last - 2 * d] = other[d][...]
-
-    @pl.when(side_ref[0] != 0)
-    def _():
-        for d in mine:
-            keys[last - 2 * d] = other[d][...]
-            values[last - 2 * d] = mine[d][...]
+    for at, distances in ((0, (2, 3, 4)), (1, (1,))):
+
+        @pl.when(side_ref[at] == 0)
+        def _():
+            for d in distances:
+                keys[last - 2 * d] = mine[d][...]
+                values[last - 2 * d] = other[d][...]
+
+        @pl.when(side_ref[at] != 0)
+        def _():
+            for d in distances:
+                keys[last - 2 * d] = other[d][...]
+                values[last - 2 * d] = mine[d][...]
 
     keys[last] = own_ref[:, :hd]
     values[last] = own_ref[:, hd:]
@@ -241,9 +243,13 @@
         turn = (z + distance >= LINE).astype(jnp.int32)
         return columns(key_value, l ^ turn, hd)
 
-    mine1 = moved(taken(1), 1, True)
+    ahead = (z >= LINE - 2).astype(jnp.int32)
+    ahead_next = ((z + 1) % LINE >= LINE - 2).astype(jnp.int32)
+    turn = (z + 1 >= LINE).astype(jnp.int32)
+    mine1 = moved(columns(key_value, l ^ turn ^ ahead_next, hd), 1, True)
     mine4 = moved(taken(4), 4, True)
-    mine23 = moved(jnp.concatenate([columns(key_value, l, hd), mine1], axis=0), 2, False)
+    couple = jnp.concatenate([taken(2), mine1], axis=0)
+    mine23 = moved(couple, 2, True)
     other1 = swapped(mine1, "l")
     other4 = swapped(mine4, "l")
     other23 = swapped(mine23, "l")
@@ -252,7 +258,7 @@
     blocks = {0: key_value}
     for d in (1, 2, 3, 4):
         blocks[d] = jnp.where(
-            l == 0,
+            (l ^ ahead if d == 1 else l) == 0,
             jnp.concatenate([mine[d], other[d]], axis=1),
             jnp.concatenate([other[d], mine[d]], axis=1),
         )
@@ -267,9 +273,10 @@
     near = swapped(crossing(0, 1), "c")
     far = swapped(crossing(2, 3), "c")
     width = inputs_normed.shape[1] // 4
-    x_parts = [columns(inputs_normed, y, width)]
+    inputs, _ = lax.optimization_barrier((inputs_normed, couple))
+    x_parts = [columns(inputs, y, width)]
     for k in (1, 2, 3):
-        x_parts.append(turned(columns(inputs_normed, (y + k) % 4, width), "y", k))
+        x_parts.append(turned(columns(inputs, (y + k) % 4, width), "y", k))
 
     begin = seq_index * tok
     padded = jnp.concatenate([jnp.full((WIN,), -1, jnp.int32), segment_ids], axis=0)
@@ -279,7 +286,7 @@
     low = jnp.maximum(before, 1 + jnp.arange(tok, dtype=jnp.int32))
     low = jnp.tile(low, heads)[None, :]
     query_grad, given, kept = attention(
-        l.reshape(1).astype(jnp.int32),
+        jnp.stack([l, l ^ ahead]).astype(jnp.int32),
         low,
         query,
         out_grad,

time: 144 us -> 148 us (1.028)
  waiting for transfers between devices: 55.6 us -> 62.7 us
  starting transfers between devices: 61.4 us -> 56.2 us
    ppermute x6, waiting for transfers between devices: 11.4 us -> 20.2 us  [turned(): lax.ppermute(value, axis, [(i, (i + steps) % count) for i in range(count)])]
    ppermute x6, starting transfers between devices: 23.2 us -> 19.5 us  [turned(): lax.ppermute(value, axis, [(i, (i + steps) % count) for i in range(count)])]
    ppermute x13, starting transfers between devices: 11.4 us -> 9.85 us  [swapped(): return lax.ppermute(value, axis, [(0, 1), (1, 0)])]
  transfers between devices with their start and end apart: 27 -> 27, of which waited for: 19 -> 17; matrix products, arithmetic and copies ran while one was open for 4% -> 4% of each run, Pallas kernels for 0% -> 0%
where the time goes in v5:
time: 148 us; the launch traced here: 146 us
  waiting for transfers between devices  62.7 us (42%)
  starting transfers between devices  56.2 us (38%)
  Pallas kernels  13.3 us (9%)
  local copies, waits for them, and re-layouts  4.66 us (3%)
  other arithmetic  4.13 us (3%)
  matrix products  3.82 us (3%)
    ppermute x13, waiting for transfers between devices, swapped(): return lax.ppermute(value, axis, [(0, 1), (1, 0)])  20.6 us
    ppermute x6, waiting for transfers between devices, turned(): lax.ppermute(value, axis, [(i, (i + steps) % count) for i in range(count)])  20.2 us
    ppermute x6, starting transfers between devices, turned(): lax.ppermute(value, axis, [(i, (i + steps) % count) for i in range(count)])  19.5 us
    ppermute x7, starting transfers between devices, moved(): return lax.ppermute(value, ALL, routes)  19.3 us
    pallas_call x1, Pallas kernels, attention(): pl.pallas_call(attention_kernel, out_shape=(jax.ShapeDtypeStruct((tok, wi...  12.4 us
    ppermute x7, waiting for transfers between devices, moved(): return lax.ppermute(value, ALL, routes)  11.9 us
    all_to_all x1, waiting for transfers between devices, local(): lax.all_to_all(total, ('xh', 'z'), split_axis=0, concat_axis=0, tiled=True)  9.99 us
    ppermute x13, starting transfers between devices, swapped(): return lax.ppermute(value, axis, [(0, 1), (1, 0)])  9.85 us
  transfers between devices with their start and end apart: 27, of which 17 were waited for; matrix products, arithmetic and copies ran while one was open for 4% of the time, Pallas kernels for 0%

profile of v5, /device:TPU:32, one launch (start us, length us, event | category | flops | bytes accessed | tf_op | source)
XLA Modules:
  0.0 145.8 jit_solution(6659595436179352331)
XLA Ops:
  0.7 1.3 constant_dynamic-slice_fusion.4
  1.9 4.0 %collective-permute-start = (bf16[256,256]{1,0:T(8,128)(2,1)S(1)}, bf16[256,256]{1,0:T(8,128)(2,1)S(1)}, u32[]{:S(2)}, u32[]{:S(2)}) collective-permute-start(bf16[256,256]{1,0:T(8,128)(2,1)S(1)} %get-tuple-element.57), channel_id=1, source_target_pairs={{0,4},{1,5},{2,6},{3,7},{4,8},{5,9},{6,10},{7,11},{8,12},{9,13},{1... | collective-permute-start | bytes 393224 | tf_op jit(solution)/shard_map/ppermute | solution.py:30
  5.9 7.2 %collective-permute-start.1 = (bf16[256,256]{1,0:T(8,128)(2,1)S(1)}, bf16[256,256]{1,0:T(8,128)(2,1)S(1)}, u32[]{:S(2)}, u32[]{:S(2)}) collective-permute-start(bf16[256,256]{1,0:T(8,128)(2,1)S(1)} %get-tuple-element.56), channel_id=1, source_target_pairs={{0,16},{1,17},{2,18},{3,19},{4,20},{5,21},{6,22},{7,23},{8,24},{9,... | collective-permute-start | bytes 393224 | tf_op jit(solution)/shard_map/ppermute | solution.py:30
  13.1 2.4 %collective-permute-start.2 = (bf16[512,256]{1,0:T(8,128)(2,1)S(1)}, bf16[512,256]{1,0:T(8,128)(2,1)S(1)}, u32[]{:S(2)}, u32[]{:S(2)}) collective-permute-start(bf16[512,256]{1,0:T(8,128)(2,1)S(1)} %pad_maximum_fusion), channel_id=1, source_target_pairs={{0,8},{1,9},{2,10},{3,11},{4,12},{5,13},{6,14},{7,15},{8,16},{9,17... | collective-permute-start | bytes 786440 | tf_op jit(solution)/shard_map/ppermute | solution.py:30
  17.1 1.6 %collective-permute-start.3 = (bf16[256,256]{1,0:T(8,128)(2,1)S(1)}, bf16[256,256]{1,0:T(8,128)(2,1)S(1)}, u32[]{:S(2)}, u32[]{:S(2)}) collective-permute-start(bf16[256,256]{1,0:T(8,128)(2,1)S(1)} %collective-permute-done.mine1), channel_id=1, source_target_pairs={{0,1},{1,0},{2,3},{3,2},{4,5},{5,4},{6,7},{7,6},{8,9},{9,8},{10,11... | collective-permute-start | bytes 393224 | tf_op jit(solution)/shard_map/ppermute | solution.py:34
  20.2 3.0 %collective-permute-done.3.other1 = bf16[256,256]{1,0:T(8,128)(2,1)S(1)} collective-permute-done((bf16[256,256]{1,0:T(8,128)(2,1)S(1)}, bf16[256,256]{1,0:T(8,128)(2,1)S(1)}, u32[]{:S(2)}, u32[]{:S(2)}) %collective-permute-start.3) | collective-permute-done | bytes 131104 | tf_op jit(solution)/shard_map/ppermute | solution.py:34
  23.3 6.7 %collective-permute-done.2.mine23 = bf16[512,256]{1,0:T(8,128)(2,1)S(1)} collective-permute-done((bf16[512,256]{1,0:T(8,128)(2,1)S(1)}, bf16[512,256]{1,0:T(8,128)(2,1)S(1)}, u32[]{:S(2)}, u32[]{:S(2)}) %collective-permute-start.2) | collective-permute-done | bytes 262176 | tf_op jit(solution)/shard_map/ppermute | solution.py:30
  30.0 1.5 %collective-permute-start.5 = (bf16[512,256]{1,0:T(8,128)(2,1)S(1)}, bf16[512,256]{1,0:T(8,128)(2,1)S(1)}, u32[]{:S(2)}, u32[]{:S(2)}) collective-permute-start(bf16[512,256]{1,0:T(8,128)(2,1)S(1)} %collective-permute-done.2.mine23), channel_id=1, source_target_pairs={{0,1},{1,0},{2,3},{3,2},{4,5},{5,4},{6,7},{7,6},{8,9},{9,8},{10,11... | collective-permute-start | bytes 786440 | tf_op jit(solution)/shard_map/ppermute | solution.py:34
  31.7 6.4 %collective-permute-done.5.other23 = bf16[512,256]{1,0:T(8,128)(2,1)S(1)} collective-permute-done((bf16[512,256]{1,0:T(8,128)(2,1)S(1)}, bf16[512,256]{1,0:T(8,128)(2,1)S(1)}, u32[]{:S(2)}, u32[]{:S(2)}) %collective-permute-start.5) | collective-permute-done | bytes 262176 | tf_op jit(solution)/shard_map/ppermute | solution.py:34
  39.3 1.3 collective-permute-done.7.far_ref
  41.4 12.4 %attention.1 = (bf16[256,1024]{1,0:T(8,128)(2,1)}, bf16[4,256,512]{2,1,0:T(8,128)(2,1)S(1)}, bf16[5,256,512]{2,1,0:T(8,128)(2,1)S(1)}) custom-call(s32[2]{0:T(128)S(1)} %pad_add_fusion.side_ref, s32[1,1024]{1,0:T(1,128)S(1)} %bitcast.52, bf16[256,1024]{1,0:T(8,128)(2,1)S(1)} %copy-done.1, bf16[256,1024]{1,0:T(8,128)(2,1)S(1)} %copy-done.2, ...), custom_call_target="tpu_custom_call" | custom-call | flops 6039797760 | bytes 8388608 | tf_op jit(solution)/shard_map/attention/pallas_call | solution.py:172
  54.1 2.5 %collective-permute-done.8 = bf16[1024,512]{1,0:T(8,128)(2,1)} collective-permute-done((bf16[1024,512]{1,0:T(8,128)(2,1)S(1)}, bf16[1024,512]{1,0:T(8,128)(2,1)}, u32[]{:S(2)}, u32[]{:S(2)}) %collective-permute-start.8) | collective-permute-done | bytes 1048608 | tf_op jit(solution)/shard_map/ppermute | solution.py:34
  56.6 1.3 fusion.39
  58.3 1.4 collective-permute-start.10
  60.4 1.4 collective-permute-start.14
  62.5 1.4 collective-permute-start.9
  64.8 1.9 %collective-permute-start.11 = (bf16[256,256]{1,0:T(8,128)(2,1)S(1)}, bf16[256,256]{1,0:T(8,128)(2,1)S(1)}, u32[]{:S(2)}, u32[]{:S(2)}) collective-permute-start(bf16[256,256]{1,0:T(8,128)(2,1)S(1)} %merge.4), channel_id=1, source_target_pairs={{4,0},{5,1},{6,2},{7,3},{8,4},{9,5},{10,6},{11,7},{12,8},{13,9},{1... | collective-permute-start | bytes 393224 | tf_op jit(solution)/shard_map/ppermute | solution.py:30
  67.6 1.3 collective-permute-start.13
  68.9 1.5 %collective-permute-done.14.two_ref = bf16[256,256]{1,0:T(8,128)(2,1)S(1)} collective-permute-done((bf16[256,256]{1,0:T(8,128)(2,1)S(1)}, bf16[256,256]{1,0:T(8,128)(2,1)S(1)}, u32[]{:S(2)}, u32[]{:S(2)}) %collective-permute-start.14) | collective-permute-done | bytes 131104 | tf_op jit(solution)/shard_map/ppermute | solution.py:34
  70.4 1.3 collective-permute-start.15
  71.7 1.5 %collective-permute-done.16.two_ref = bf16[256,256]{1,0:T(8,128)(2,1)S(1)} collective-permute-done((bf16[256,256]{1,0:T(8,128)(2,1)S(1)}, bf16[256,256]{1,0:T(8,128)(2,1)S(1)}, u32[]{:S(2)}, u32[]{:S(2)}) %collective-permute-start.16) | collective-permute-done | bytes 131104 | tf_op jit(solution)/shard_map/ppermute | solution.py:34
  73.2 1.3 collective-permute-start.17
  75.2 13.8 %collective-permute-start.24 = (bf16[256,1024]{1,0:T(8,128)(2,1)S(1)}, bf16[256,1024]{1,0:T(8,128)(2,1)}, u32[]{:S(2)}, u32[]{:S(2)}) collective-permute-start(bf16[256,1024]{1,0:T(8,128)(2,1)S(1)} %get-tuple-element.20), channel_id=1, source_target_pairs={{0,192},{64,0},{128,64},{192,128},{1,193},{65,1},{129,65},{193,129... | collective-permute-start | bytes 1572872 | tf_op jit(solution)/shard_map/ppermute | solution.py:39
  90.3 5.2 %collective-permute-done.17 = bf16[256,256]{1,0:T(8,128)(2,1)} collective-permute-done((bf16[256,256]{1,0:T(8,128)(2,1)S(1)}, bf16[256,256]{1,0:T(8,128)(2,1)}, u32[]{:S(2)}, u32[]{:S(2)}) %collective-permute-start.17) | collective-permute-done | bytes 131104 | tf_op jit(solution)/shard_map/ppermute | solution.py:30
  96.6 3.8 %collective-permute-start.21 = (bf16[256,256]{1,0:T(8,128)(2,1)S(1)}, bf16[256,256]{1,0:T(8,128)(2,1)S(1)}, u32[]{:S(2)}, u32[]{:S(2)}) collective-permute-start(bf16[256,256]{1,0:T(8,128)(2,1)S(1)} %fusion.35), channel_id=1, source_target_pairs={{0,192},{64,0},{128,64},{192,128},{1,193},{65,1},{129,65},{193,129... | collective-permute-start | bytes 393224 | tf_op jit(solution)/shard_map/ppermute | solution.py:39
  101.0 13.5 %collective-permute-done.21 = bf16[256,256]{1,0:T(8,128)(2,1)S(1)} collective-permute-done((bf16[256,256]{1,0:T(8,128)(2,1)S(1)}, bf16[256,256]{1,0:T(8,128)(2,1)S(1)}, u32[]{:S(2)}, u32[]{:S(2)}) %collective-permute-start.21) | collective-permute-done | bytes 131104 | tf_op jit(solution)/shard_map/ppermute | solution.py:39
  115.5 5.7 %collective-permute-done.19 = bf16[256,256]{1,0:T(8,128)(2,1)S(1)} collective-permute-done((bf16[256,256]{1,0:T(8,128)(2,1)S(1)}, bf16[256,256]{1,0:T(8,128)(2,1)S(1)}, u32[]{:S(2)}, u32[]{:S(2)}) %collective-permute-start.19) | collective-permute-done | bytes 131104 | tf_op jit(solution)/shard_map/ppermute | solution.py:39
  121.2 2.1 %fusion.11 = f32[1024,256]{1,0:T(8,128)S(1)} fusion(bf16[256,1024]{1,0:T(8,128)(2,1)} %collective-permute-done.24, bf16[256,1024]{1,0:T(8,128)(2,1)} %collective-permute-done.23, bf16[256,1024]{1,0:T(8,128)(2,1)} %collective-permute-done.22, bf16[256,1024]{1,0:T(8,128)(2,1)S(1)} %get-tuple-element.19, bf16[256,256]{1,0:T(8,128)(2,1)S(1)} %collective-permute-done.21, ...), kind=kOutput, calls=%fused_computation.13 | convolution fusion | flops 547618816 | bytes 3670016 | tf_op jit(solution)/shard_map/dot_general | solution.py:339
  123.4 1.5 %collective-permute-done.25.arrived_ref = bf16[16,32,256]{2,1,0:T(8,128)(2,1)S(1)} collective-permute-done((bf16[16,32,256]{2,1,0:T(8,128)(2,1)S(1)}, bf16[16,32,256]{2,1,0:T(8,128)(2,1)S(1)}, u32[]{:S(2)}, u32[]{:S(2)}) %collective-permute-start.25) | collective-permute-done | bytes 262176 | tf_op jit(solution)/shard_map/ppermute | solution.py:34
  125.7 7.6 %all-to-all-start = ((bf16[16,32,256]{2,1,0:T(8,128)(2,1)}), bf16[16,32,256]{2,1,0:T(8,128)(2,1)S(1)}, u32[]{:S(2)}, u32[]{:S(2)}) async-start(bf16[16,32,256]{2,1,0:T(8,128)(2,1)} %core_merge.1), calls=%async_computation | async-start | bytes 524288 | tf_op jit(solution)/shard_map/all_to_all | solution.py:345
  133.4 1.7 %convolution_convert_fusion = bf16[256,2048]{1,0:T(8,128)(2,1)} fusion(bf16[2048,256]{1,0:T(8,128)(2,1)S(1)} %get-tuple-element.24, bf16[2048,256]{1,0:T(8,128)(2,1)S(1)} %get-tuple-element.23, bf16[256,256]{1,0:T(8,128)(2,1)S(1)} %collective-permute-done.18, bf16[256,256]{1,0:T(8,128)(2,1)S(1)} %fusion.35), kind=kOutput, calls=%fused_computation | convolution fusion | flops 542113792 | bytes 3407872 | tf_op jit(solution)/shard_map/dot_general | solution.py:330
  135.2 10.0 %all-to-all-done = bf16[16,32,256]{2,1,0:T(8,128)(2,1)S(1)} async-done(((bf16[16,32,256]{2,1,0:T(8,128)(2,1)}), bf16[16,32,256]{2,1,0:T(8,128)(2,1)S(1)}, u32[]{:S(2)}, u32[]{:S(2)}) %all-to-all-start) | async-done | bytes 262176 | tf_op jit(solution)/shard_map/all_to_all | solution.py:345
  (63 shorter events, 15.6 us)
Async XLA Ops:
  1.9 36.3 %copy-start = (bf16[256,512]{1,0:T(8,128)(2,1)S(1)}, bf16[256,512]{1,0:T(8,128)(2,1)}, u32[]{:S(2)}) copy-start(bf16[256,512]{1,0:T(8,128)(2,1)} %own_ref.1) | copy-start | bytes 786436
  1.9 11.1 %collective-permute-start = (bf16[256,256]{1,0:T(8,128)(2,1)S(1)}, bf16[256,256]{1,0:T(8,128)(2,1)S(1)}, u32[]{:S(2)}, u32[]{:S(2)}) collective-permute-start(bf16[256,256]{1,0:T(8,128)(2,1)S(1)} %get-tuple-element.57), channel_id=1, source_target_pairs={{0,4},{1,5},{2,6},{3,7},{4,8},{5,9},{6,10},{7,11},{8,12},{9,13},{1... | collective-permute-start | bytes 393224 | tf_op jit(solution)/shard_map/ppermute | solution.py:30
  5.9 12.8 %collective-permute-start.1 = (bf16[256,256]{1,0:T(8,128)(2,1)S(1)}, bf16[256,256]{1,0:T(8,128)(2,1)S(1)}, u32[]{:S(2)}, u32[]{:S(2)}) collective-permute-start(bf16[256,256]{1,0:T(8,128)(2,1)S(1)} %get-tuple-element.56), channel_id=1, source_target_pairs={{0,16},{1,17},{2,18},{3,19},{4,20},{5,21},{6,22},{7,23},{8,24},{9,... | collective-permute-start | bytes 393224 | tf_op jit(solution)/shard_map/ppermute | solution.py:30
  13.1 16.9 %collective-permute-start.2 = (bf16[512,256]{1,0:T(8,128)(2,1)S(1)}, bf16[512,256]{1,0:T(8,128)(2,1)S(1)}, u32[]{:S(2)}, u32[]{:S(2)}) collective-permute-start(bf16[512,256]{1,0:T(8,128)(2,1)S(1)} %pad_maximum_fusion), channel_id=1, source_target_pairs={{0,8},{1,9},{2,10},{3,11},{4,12},{5,13},{6,14},{7,15},{8,16},{9,17... | collective-permute-start | bytes 786440 | tf_op jit(solution)/shard_map/ppermute | solution.py:30
  17.1 6.1 %collective-permute-start.3 = (bf16[256,256]{1,0:T(8,128)(2,1)S(1)}, bf16[256,256]{1,0:T(8,128)(2,1)S(1)}, u32[]{:S(2)}, u32[]{:S(2)}) collective-permute-start(bf16[256,256]{1,0:T(8,128)(2,1)S(1)} %collective-permute-done.mine1), channel_id=1, source_target_pairs={{0,1},{1,0},{2,3},{3,2},{4,5},{5,4},{6,7},{7,6},{8,9},{9,8},{10,11... | collective-permute-start | bytes 393224 | tf_op jit(solution)/shard_map/ppermute | solution.py:34
  18.7 12.8 %collective-permute-start.4 = (bf16[256,256]{1,0:T(8,128)(2,1)S(1)}, bf16[256,256]{1,0:T(8,128)(2,1)S(1)}, u32[]{:S(2)}, u32[]{:S(2)}) collective-permute-start(bf16[256,256]{1,0:T(8,128)(2,1)S(1)} %collective-permute-done.1.mine4), channel_id=1, source_target_pairs={{0,1},{1,0},{2,3},{3,2},{4,5},{5,4},{6,7},{7,6},{8,9},{9,8},{10,11... | collective-permute-start | bytes 393224 | tf_op jit(solution)/shard_map/ppermute | solution.py:34
  30.0 8.1 %collective-permute-start.5 = (bf16[512,256]{1,0:T(8,128)(2,1)S(1)}, bf16[512,256]{1,0:T(8,128)(2,1)S(1)}, u32[]{:S(2)}, u32[]{:S(2)}) collective-permute-start(bf16[512,256]{1,0:T(8,128)(2,1)S(1)} %collective-permute-done.2.mine23), channel_id=1, source_target_pairs={{0,1},{1,0},{2,3},{3,2},{4,5},{5,4},{6,7},{7,6},{8,9},{9,8},{10,11... | collective-permute-start | bytes 786440 | tf_op jit(solution)/shard_map/ppermute | solution.py:34
  31.7 9.7 %copy-start.1 = (bf16[256,1024]{1,0:T(8,128)(2,1)S(1)}, bf16[256,1024]{1,0:T(8,128)(2,1)}, u32[]{:S(2)}) copy-start(bf16[256,1024]{1,0:T(8,128)(2,1)} %query_ref.1) | copy-start | bytes 1572868
  31.7 9.7 %copy-start.2 = (bf16[256,1024]{1,0:T(8,128)(2,1)S(1)}, bf16[256,1024]{1,0:T(8,128)(2,1)}, u32[]{:S(2)}) copy-start(bf16[256,1024]{1,0:T(8,128)(2,1)} %out_ref.1) | copy-start | bytes 1572868
  38.6 2.0 %collective-permute-start.7 = (bf16[512,512]{1,0:T(8,128)(2,1)S(1)}, bf16[512,512]{1,0:T(8,128)(2,1)S(1)}, u32[]{:S(2)}, u32[]{:S(2)}) collective-permute-start(bf16[512,512]{1,0:T(8,128)(2,1)S(1)} %get-tuple-element.49), channel_id=1, source_target_pairs={{0,2},{2,0},{1,3},{3,1},{4,6},{6,4},{5,7},{7,5},{8,10},{10,8},{9,1... | collective-permute-start | bytes 1572872 | tf_op jit(solution)/shard_map/ppermute | solution.py:34
  38.7 2.6 %collective-permute-start.6 = (bf16[512,512]{1,0:T(8,128)(2,1)S(1)}, bf16[512,512]{1,0:T(8,128)(2,1)S(1)}, u32[]{:S(2)}, u32[]{:S(2)}) collective-permute-start(bf16[512,512]{1,0:T(8,128)(2,1)S(1)} %get-tuple-element.50), channel_id=1, source_target_pairs={{0,2},{2,0},{1,3},{3,1},{4,6},{6,4},{5,7},{7,5},{8,10},{10,8},{9,1... | collective-permute-start | bytes 1572872 | tf_op jit(solution)/shard_map/ppermute | solution.py:34
  53.8 2.8 %collective-permute-start.8 = (bf16[1024,512]{1,0:T(8,128)(2,1)S(1)}, bf16[1024,512]{1,0:T(8,128)(2,1)}, u32[]{:S(2)}, u32[]{:S(2)}) collective-permute-start(bf16[1024,512]{1,0:T(8,128)(2,1)S(1)} %bitcast.53), channel_id=1, source_target_pairs={{0,2},{2,0},{1,3},{3,1},{4,6},{6,4},{5,7},{7,5},{8,10},{10,8},{9,1... | collective-permute-start | bytes 3145736 | tf_op jit(solution)/shard_map/ppermute | solution.py:34
  58.3 6.5 %collective-permute-start.10 = (bf16[256,256]{1,0:T(8,128)(2,1)S(1)}, bf16[256,256]{1,0:T(8,128)(2,1)S(1)}, u32[]{:S(2)}, u32[]{:S(2)}) collective-permute-start(bf16[256,256]{1,0:T(8,128)(2,1)S(1)} %get-tuple-element.34), channel_id=1, source_target_pairs={{0,1},{1,0},{2,3},{3,2},{4,5},{5,4},{6,7},{7,6},{8,9},{9,8},{10,11... | collective-permute-start | bytes 393224 | tf_op jit(solution)/shard_map/ppermute | solution.py:34
  59.8 7.8 %collective-permute-start.12 = (bf16[256,256]{1,0:T(8,128)(2,1)S(1)}, bf16[256,256]{1,0:T(8,128)(2,1)S(1)}, u32[]{:S(2)}, u32[]{:S(2)}) collective-permute-start(bf16[256,256]{1,0:T(8,128)(2,1)S(1)} %get-tuple-element.44), channel_id=1, source_target_pairs={{0,1},{1,0},{2,3},{3,2},{4,5},{5,4},{6,7},{7,6},{8,9},{9,8},{10,11... | collective-permute-start | bytes 393224 | tf_op jit(solution)/shard_map/ppermute | solution.py:34
  60.4 10.0 %collective-permute-start.14 = (bf16[256,256]{1,0:T(8,128)(2,1)S(1)}, bf16[256,256]{1,0:T(8,128)(2,1)S(1)}, u32[]{:S(2)}, u32[]{:S(2)}) collective-permute-start(bf16[256,256]{1,0:T(8,128)(2,1)S(1)} %get-tuple-element.46), channel_id=1, source_target_pairs={{0,1},{1,0},{2,3},{3,2},{4,5},{5,4},{6,7},{7,6},{8,9},{9,8},{10,11... | collective-permute-start | bytes 393224 | tf_op jit(solution)/shard_map/ppermute | solution.py:34
  61.8 11.4 %collective-permute-start.16 = (bf16[256,256]{1,0:T(8,128)(2,1)S(1)}, bf16[256,256]{1,0:T(8,128)(2,1)S(1)}, u32[]{:S(2)}, u32[]{:S(2)}) collective-permute-start(bf16[256,256]{1,0:T(8,128)(2,1)S(1)} %get-tuple-element.48), channel_id=1, source_target_pairs={{0,1},{1,0},{2,3},{3,2},{4,5},{5,4},{6,7},{7,6},{8,9},{9,8},{10,11... | collective-permute-start | bytes 393224 | tf_op jit(solution)/shard_map/ppermute | solution.py:34
  62.5 12.1 %copy-start.4 = (bf16[256,4096]{1,0:T(8,128)(2,1)S(1)}, bf16[256,4096]{1,0:T(8,128)(2,1)}, u32[]{:S(2)}) copy-start(bf16[256,4096]{1,0:T(8,128)(2,1)} %param.9) | copy-start | bytes 6291460
  62.5 12.7 %collective-permute-start.9 = (bf16[256,256]{1,0:T(8,128)(2,1)S(1)}, bf16[256,256]{1,0:T(8,128)(2,1)S(1)}, u32[]{:S(2)}, u32[]{:S(2)}) collective-permute-start(bf16[256,256]{1,0:T(8,128)(2,1)S(1)} %get-tuple-element.42), channel_id=1, source_target_pairs={{0,1},{1,0},{2,3},{3,2},{4,5},{5,4},{6,7},{7,6},{8,9},{9,8},{10,11... | collective-permute-start | bytes 393224 | tf_op jit(solution)/shard_map/ppermute | solution.py:34
  64.8 24.2 %collective-permute-start.11 = (bf16[256,256]{1,0:T(8,128)(2,1)S(1)}, bf16[256,256]{1,0:T(8,128)(2,1)S(1)}, u32[]{:S(2)}, u32[]{:S(2)}) collective-permute-start(bf16[256,256]{1,0:T(8,128)(2,1)S(1)} %merge.4), channel_id=1, source_target_pairs={{4,0},{5,1},{6,2},{7,3},{8,4},{9,5},{10,6},{11,7},{12,8},{13,9},{1... | collective-permute-start | bytes 393224 | tf_op jit(solution)/shard_map/ppermute | solution.py:30
  67.6 21.9 %collective-permute-start.13 = (bf16[256,256]{1,0:T(8,128)(2,1)S(1)}, bf16[256,256]{1,0:T(8,128)(2,1)S(1)}, u32[]{:S(2)}, u32[]{:S(2)}) collective-permute-start(bf16[256,256]{1,0:T(8,128)(2,1)S(1)} %merge.5), channel_id=1, source_target_pairs={{8,0},{9,1},{10,2},{11,3},{12,4},{13,5},{14,6},{15,7},{16,8},{17,9... | collective-permute-start | bytes 393224 | tf_op jit(solution)/shard_map/ppermute | solution.py:30
  70.4 19.9 %collective-permute-start.15 = (bf16[256,256]{1,0:T(8,128)(2,1)S(1)}, bf16[256,256]{1,0:T(8,128)(2,1)}, u32[]{:S(2)}, u32[]{:S(2)}) collective-permute-start(bf16[256,256]{1,0:T(8,128)(2,1)S(1)} %merge.6), channel_id=1, source_target_pairs={{12,0},{13,1},{14,2},{15,3},{16,4},{17,5},{18,6},{19,7},{20,8},{21... | collective-permute-start | bytes 393224 | tf_op jit(solution)/shard_map/ppermute | solution.py:30
  73.2 22.2 %collective-permute-start.17 = (bf16[256,256]{1,0:T(8,128)(2,1)S(1)}, bf16[256,256]{1,0:T(8,128)(2,1)}, u32[]{:S(2)}, u32[]{:S(2)}) collective-permute-start(bf16[256,256]{1,0:T(8,128)(2,1)S(1)} %merge.7), channel_id=1, source_target_pairs={{16,0},{17,1},{18,2},{19,3},{20,4},{21,5},{22,6},{23,7},{24,8},{25... | collective-permute-start | bytes 393224 | tf_op jit(solution)/shard_map/ppermute | solution.py:30
  75.2 46.0 %collective-permute-start.24 = (bf16[256,1024]{1,0:T(8,128)(2,1)S(1)}, bf16[256,1024]{1,0:T(8,128)(2,1)}, u32[]{:S(2)}, u32[]{:S(2)}) collective-permute-start(bf16[256,1024]{1,0:T(8,128)(2,1)S(1)} %get-tuple-element.20), channel_id=1, source_target_pairs={{0,192},{64,0},{128,64},{192,128},{1,193},{65,1},{129,65},{193,129... | collective-permute-start | bytes 1572872 | tf_op jit(solution)/shard_map/ppermute | solution.py:39
  89.0 32.2 %collective-permute-start.23 = (bf16[256,1024]{1,0:T(8,128)(2,1)S(1)}, bf16[256,1024]{1,0:T(8,128)(2,1)}, u32[]{:S(2)}, u32[]{:S(2)}) collective-permute-start(bf16[256,1024]{1,0:T(8,128)(2,1)S(1)} %get-tuple-element.21), channel_id=1, source_target_pairs={{0,128},{64,192},{128,0},{192,64},{1,129},{65,193},{129,1},{193,65... | collective-permute-start | bytes 1572872 | tf_op jit(solution)/shard_map/ppermute | solution.py:39
  89.5 31.6 %collective-permute-start.22 = (bf16[256,1024]{1,0:T(8,128)(2,1)S(1)}, bf16[256,1024]{1,0:T(8,128)(2,1)}, u32[]{:S(2)}, u32[]{:S(2)}) collective-permute-start(bf16[256,1024]{1,0:T(8,128)(2,1)S(1)} %get-tuple-element.22), channel_id=1, source_target_pairs={{0,64},{64,128},{128,192},{192,0},{1,65},{65,129},{129,193},{193,1... | collective-permute-start | bytes 1572872 | tf_op jit(solution)/shard_map/ppermute | solution.py:39
  96.6 17.9 %collective-permute-start.21 = (bf16[256,256]{1,0:T(8,128)(2,1)S(1)}, bf16[256,256]{1,0:T(8,128)(2,1)S(1)}, u32[]{:S(2)}, u32[]{:S(2)}) collective-permute-start(bf16[256,256]{1,0:T(8,128)(2,1)S(1)} %fusion.35), channel_id=1, source_target_pairs={{0,192},{64,0},{128,64},{192,128},{1,193},{65,1},{129,65},{193,129... | collective-permute-start | bytes 393224 | tf_op jit(solution)/shard_map/ppermute | solution.py:39
  100.3 15.1 %collective-permute-start.20 = (bf16[256,256]{1,0:T(8,128)(2,1)S(1)}, bf16[256,256]{1,0:T(8,128)(2,1)S(1)}, u32[]{:S(2)}, u32[]{:S(2)}) collective-permute-start(bf16[256,256]{1,0:T(8,128)(2,1)S(1)} %fusion.35), channel_id=1, source_target_pairs={{0,128},{64,192},{128,0},{192,64},{1,129},{65,193},{129,1},{193,65... | collective-permute-start | bytes 393224 | tf_op jit(solution)/shard_map/ppermute | solution.py:39
  114.5 6.6 %collective-permute-start.19 = (bf16[256,256]{1,0:T(8,128)(2,1)S(1)}, bf16[256,256]{1,0:T(8,128)(2,1)S(1)}, u32[]{:S(2)}, u32[]{:S(2)}) collective-permute-start(bf16[256,256]{1,0:T(8,128)(2,1)S(1)} %fusion.35), channel_id=1, source_target_pairs={{0,64},{64,128},{128,192},{192,0},{1,65},{65,129},{129,193},{193,1... | collective-permute-start | bytes 393224 | tf_op jit(solution)/shard_map/ppermute | solution.py:39
  115.5 5.7 %collective-permute-start.18 = (bf16[256,256]{1,0:T(8,128)(2,1)S(1)}, bf16[256,256]{1,0:T(8,128)(2,1)S(1)}, u32[]{:S(2)}, u32[]{:S(2)}) collective-permute-start(bf16[256,256]{1,0:T(8,128)(2,1)S(1)} %fusion.35), channel_id=1, source_target_pairs={{0,1},{1,0},{2,3},{3,2},{4,5},{5,4},{6,7},{7,6},{8,9},{9,8},{10,11... | collective-permute-start | bytes 393224 | tf_op jit(solution)/shard_map/ppermute | solution.py:34
  123.3 10.0 %copy-start.3 = (bf16[2,2048,256]{2,1,0:T(8,128)(2,1)S(1)}, bf16[2,2048,256]{2,1,0:T(8,128)(2,1)}, u32[]{:S(2)}) copy-start(bf16[2,2048,256]{2,1,0:T(8,128)(2,1)} %param.10) | copy-start | bytes 6291460
  123.3 1.6 %collective-permute-start.25 = (bf16[16,32,256]{2,1,0:T(8,128)(2,1)S(1)}, bf16[16,32,256]{2,1,0:T(8,128)(2,1)S(1)}, u32[]{:S(2)}, u32[]{:S(2)}) collective-permute-start(bf16[16,32,256]{2,1,0:T(8,128)(2,1)S(1)} %fusion.21), channel_id=1, source_target_pairs={{0,2},{2,0},{1,3},{3,1},{4,6},{6,4},{5,7},{7,5},{8,10},{10,8},{9,1... | collective-permute-start | bytes 786440 | tf_op jit(solution)/shard_map/ppermute | solution.py:34
  125.7 19.4 %all-to-all-start = ((bf16[16,32,256]{2,1,0:T(8,128)(2,1)}), bf16[16,32,256]{2,1,0:T(8,128)(2,1)S(1)}, u32[]{:S(2)}, u32[]{:S(2)}) async-start(bf16[16,32,256]{2,1,0:T(8,128)(2,1)} %core_merge.1), calls=%async_computation | async-start | bytes 524288 | tf_op jit(solution)/shard_map/all_to_all | solution.py:345
